TPU v7x, 8 devices: a whole 2x2x1 slice. The times are simulated.
8 devices in a mesh: dp: 2 (over z, y), tp: 4 (over x, core).
Axes of the slice: x: 2, y: 2, z: 1, core: 2. Of those that a mesh axis runs over, the one named last changes fastest.
Arguments:
- hidden: bfloat16 [120, 768], P('dp'), parts along dimension 0
- positions: int32 [120], P('dp'), parts along dimension 0
- self_keys: bfloat16 [2, 120, 448, 12, 64], P(None, 'dp', None, 'tp'), parts along dimension 1
- self_vals: bfloat16 [2, 120, 448, 12, 64], P(None, 'dp', None, 'tp'), parts along dimension 1
- cross_keys: bfloat16 [2, 24, 1500, 12, 64], P(None, 'dp', None, 'tp'), parts along dimension 1
- cross_vals: bfloat16 [2, 24, 1500, 12, 64], P(None, 'dp', None, 'tp'), parts along dimension 1
- ln_gain: bfloat16 [2, 3, 768], replicated
- ln_bias: bfloat16 [2, 3, 768], replicated
- w_query: bfloat16 [2, 768, 768], P(None, None, 'tp')
- b_query: bfloat16 [2, 768], P(None, 'tp')
- w_key: bfloat16 [2, 768, 768], P(None, None, 'tp')
- w_value: bfloat16 [2, 768, 768], P(None, None, 'tp')
- b_value: bfloat16 [2, 768], P(None, 'tp')
- w_out: bfloat16 [2, 768, 768], P(None, 'tp')
- b_out: bfloat16 [2, 768], replicated
- w_cquery: bfloat16 [2, 768, 768], P(None, None, 'tp')
- b_cquery: bfloat16 [2, 768], P(None, 'tp')
- w_cout: bfloat16 [2, 768, 768], P(None, 'tp')
- b_cout: bfloat16 [2, 768], replicated
- w_fc1: bfloat16 [2, 768, 3072], P(None, None, 'tp')
- b_fc1: bfloat16 [2, 3072], P(None, 'tp')
- w_fc2: bfloat16 [2, 3072, 768], P(None, 'tp')
- b_fc2: bfloat16 [2, 768], replicated
Outputs:
- output 1: bfloat16 [120, 768], P('dp'), parts along dimension 0
- output 2: bfloat16 [2, 120, 448, 12, 64], P(None, 'dp', None, 'tp'), parts along dimension 1
- output 3: bfloat16 [2, 120, 448, 12, 64], P(None, 'dp', None, 'tp'), parts along dimension 1
There are 2 independent parts. A program takes and returns all parts, laid end to end along the dimension named above; an argument that names none is the same for every part.
All inputs are finite; a program needn't handle non-finite values.
Results may differ from a plain program's by a relative error of at most 0.02.
Values are sent between devices in bfloat16 or wider.
A program may use at most 1 GiB of HBM per device.

v0:
```python
import jax
import jax.numpy as jnp
from jax import lax
from jax.sharding import PartitionSpec as P

EPS = 1e-5
PARAM_NAMES = ('ln_gain', 'ln_bias', 'w_query', 'b_query', 'w_key', 'w_value', 'b_value', 'w_out', 'b_out', 'w_cquery', 'b_cquery', 'w_cout', 'b_cout', 'w_fc1', 'b_fc1', 'w_fc2', 'b_fc2')


def layer_norm(values, gain_row, bias_row):
    wide_vals = values.astype(jnp.float32)
    center = wide_vals - jnp.mean(wide_vals, axis=-1, keepdims=True)
    var_est = jnp.mean(center * center, axis=-1, keepdims=True)
    return (center * lax.rsqrt(var_est + EPS) * gain_row + bias_row).astype(jnp.bfloat16)


def tp_sum(part_out):
    return lax.psum(part_out.astype(jnp.bfloat16), 'tp')


def decoder_layer(hidden, positions, cache_k, cache_v, cross_k, cross_v, layer_w, group_sum):
    batch_size = hidden.shape[0]
    head_count = cache_k.shape[2]
    head_dim = cache_k.shape[3]
    audios = cross_k.shape[0]
    beam_count = batch_size // audios
    qk_scale = head_dim ** -0.25
    slot_ids = lax.broadcasted_iota(jnp.int32, (1, cache_k.shape[1]), 1)
    slot_hit = (slot_ids == positions[:, None])[:, :, None, None]
    slot_mask = (slot_ids <= positions[:, None])[:, None, :]

    normed = layer_norm(hidden, layer_w['ln_gain'][0], layer_w['ln_bias'][0])
    query_heads = ((jnp.dot(normed, layer_w['w_query'], preferred_element_type=jnp.float32) + layer_w['b_query']) * qk_scale).astype(jnp.bfloat16).reshape(batch_size, head_count, head_dim)
    new_key = (jnp.dot(normed, layer_w['w_key'], preferred_element_type=jnp.float32) * qk_scale).astype(jnp.bfloat16).reshape(batch_size, 1, head_count, head_dim)
    new_val = (jnp.dot(normed, layer_w['w_value'], preferred_element_type=jnp.float32) + layer_w['b_value']).astype(jnp.bfloat16).reshape(batch_size, 1, head_count, head_dim)
    cache_k = jnp.where(slot_hit, new_key, cache_k)
    cache_v = jnp.where(slot_hit, new_val, cache_v)
    raw_scores = jnp.einsum('bhd,bshd->bhs', query_heads, cache_k, preferred_element_type=jnp.float32)
    attn_probs = jax.nn.softmax(jnp.where(slot_mask, raw_scores, -1e30), axis=-1).astype(jnp.bfloat16)
    attn_out = jnp.einsum('bhs,bshd->bhd', attn_probs, cache_v, preferred_element_type=jnp.float32).astype(jnp.bfloat16).reshape(batch_size, head_count * head_dim)
    attn_sum = group_sum(jnp.dot(attn_out, layer_w['w_out'], preferred_element_type=jnp.float32))
    hidden = (hidden.astype(jnp.float32) + attn_sum + layer_w['b_out']).astype(jnp.bfloat16)

    normed = layer_norm(hidden, layer_w['ln_gain'][1], layer_w['ln_bias'][1])
    cross_query = ((jnp.dot(normed, layer_w['w_cquery'], preferred_element_type=jnp.float32) + layer_w['b_cquery']) * qk_scale).astype(jnp.bfloat16).reshape(audios, beam_count, head_count, head_dim)
    cross_scores = jnp.einsum('abhd,afhd->abhf', cross_query, cross_k, preferred_element_type=jnp.float32)
    cross_probs = jax.nn.softmax(cross_scores, axis=-1).astype(jnp.bfloat16)
    cross_out = jnp.einsum('abhf,afhd->abhd', cross_probs, cross_v, preferred_element_type=jnp.float32).astype(jnp.bfloat16).reshape(batch_size, head_count * head_dim)
    cross_sum = group_sum(jnp.dot(cross_out, layer_w['w_cout'], preferred_element_type=jnp.float32))
    hidden = (hidden.astype(jnp.float32) + cross_sum + layer_w['b_cout']).astype(jnp.bfloat16)

    normed = layer_norm(hidden, layer_w['ln_gain'][2], layer_w['ln_bias'][2])
    mlp_inner = jax.nn.gelu(jnp.dot(normed, layer_w['w_fc1'], preferred_element_type=jnp.float32) + layer_w['b_fc1'], approximate=False).astype(jnp.bfloat16)
    mlp_sum = group_sum(jnp.dot(mlp_inner, layer_w['w_fc2'], preferred_element_type=jnp.float32))
    hidden = (hidden.astype(jnp.float32) + mlp_sum + layer_w['b_fc2']).astype(jnp.bfloat16)
    return hidden, cache_k, cache_v


def solution(mesh):
    cache_spec = P(None, 'dp', None, 'tp', None)
    col_spec = P(None, None, 'tp')
    row_spec = P(None, 'tp', None)
    vec_spec = P(None, 'tp')
    param_specs = {'ln_gain': P(), 'ln_bias': P(), 'w_query': col_spec, 'b_query': vec_spec, 'w_key': col_spec, 'w_value': col_spec, 'b_value': vec_spec, 'w_out': row_spec, 'b_out': P(), 'w_cquery': col_spec, 'b_cquery': vec_spec, 'w_cout': row_spec, 'b_cout': P(), 'w_fc1': col_spec, 'b_fc1': vec_spec, 'w_fc2': row_spec, 'b_fc2': P()}
    in_specs = (P('dp', None), P('dp'), cache_spec, cache_spec, cache_spec, cache_spec) + tuple(param_specs[param_name] for param_name in PARAM_NAMES)

    def local_step(hidden, positions, self_keys, self_vals, cross_keys, cross_vals, *layer_params):
        keys_out = []
        vals_out = []
        for layer_idx in range(self_keys.shape[0]):
            layer_w = {param_name: stacked[layer_idx] for param_name, stacked in zip(PARAM_NAMES, layer_params)}
            hidden, cache_k, cache_v = decoder_layer(hidden, positions, self_keys[layer_idx], self_vals[layer_idx], cross_keys[layer_idx], cross_vals[layer_idx], layer_w, tp_sum)
            keys_out.append(cache_k)
            vals_out.append(cache_v)
        return hidden, jnp.stack(keys_out), jnp.stack(vals_out)

    return jax.shard_map(local_step, mesh=mesh, in_specs=in_specs, out_specs=(P('dp', None), cache_spec, cache_spec), check_vma=False)
```

profile of v0, /device:TPU:0, one launch (start us, length us, event | category | flops | bytes accessed | tf_op | source)
XLA Modules:
  0.0 257.9 jit_solution(16267441918301158979)
XLA Ops:
  7.2 1.0 convert_reduce_fusion.5
  8.2 1.1 fusion.164
  9.3 0.8 slice_convert_fusion.2
  10.1 0.8 slice_convert_fusion.4
  10.9 0.9 convert_reduce_fusion.8
  11.8 1.3 fusion.96
  13.3 1.3 fusion.94
  14.7 1.3 fusion.95
  16.4 0.8 iota_compare_fusion.1
  17.2 5.4 %fusion.9 = f32[60,3,1,448]{3,2,1,0:T(1,128)S(1)} fusion(bf16[60,3,64,1]{2,3,1,0:T(2,128)(2,1)S(1)} %copy.64, pred[60,448]{1,0:T(8,128)(4,1)S(1)} %get-tuple-element.46, bf16[2,60,448,3,64]{2,4,3,1,0:T(8,128)(2,1)} %param.25, bf16[60,3,64]{2,1,0:T(4,128)(2,1)S(1)} %copy.48), kind=kOutput, calls=%fused_computation.15 | convolution fusion | flops 15482880 | bytes 12192000 | tf_op jit(solution)/shard_map/bhd,bshd->bhs/dot_general | solution.py:38
  22.6 0.2 fusion.64
  22.9 6.7 %fusion.8 = bf16[60,3,1,64]{3,2,1,0:T(2,128)(2,1)S(1)} fusion(pred[60,448]{1,0:T(8,128)(4,1)S(1)} %get-tuple-element.46, bf16[2,60,448,3,64]{2,4,3,1,0:T(8,128)(2,1)} %param.26, bf16[60,3,64]{2,1,0:T(4,128)(2,1)S(1)} %copy.50, bf16[60,3,448,1]{2,0,1,3:T(8,128)(2,1)S(1)} %fusion.64), kind=kOutput, calls=%fused_computation.13 | convolution fusion | flops 15482880 | bytes 12030720 | tf_op jit(solution)/shard_map/bhs,bshd->bhd/dot_general | solution.py:40
  29.8 0.9 convolution_convert_fusion.3
  30.8 28.9 %all-reduce.7.cloned.1.call-done = bf16[60,768]{1,0:T(8,128)(2,1)} async-done(((bf16[60,768]{1,0:T(8,128)(2,1)}), bf16[60,768]{1,0:T(8,128)(2,1)}) %all-reduce.7.cloned.1.call-update) | async-done | bytes 92176 | tf_op jit(solution)/shard_map/psum | solution.py:18
  59.7 1.0 convert_reduce_fusion.4
  61.0 0.3 fusion.97
  61.4 4.3 %fusion.385 = (f32[12,5,3]{1,2,0:T(4,128)S(1)}, f32[12,5,3,1500]{3,1,2,0:T(8,128)S(1)}) fusion(bf16[2,12,1500,3,64]{2,4,3,1,0:T(8,128)(2,1)} %param.27, bf16[12,5,3,64]{3,2,1,0:T(4,128)(2,1)S(1)} %reshape.264), kind=kOutput, calls=%fused_computation.434 | convolution fusion | flops 35101500 | bytes 8181648 | tf_op jit(solution)/shard_map/sub | solution.py:47
  65.7 5.0 %fusion.87 = bf16[12,5,3,64]{3,1,2,0:T(8,128)(2,1)S(1)} fusion(bf16[2,12,1500,3,64]{2,4,3,1,0:T(8,128)(2,1)} %param.28, f32[12,5,3,1500]{3,1,2,0:T(8,128)S(1)} %get-tuple-element.48, f32[12,5,3]{1,2,0:T(4,128)S(1)} %get-tuple-element.47), kind=kOutput, calls=%fused_computation.85 | convolution fusion | flops 35111520 | bytes 8181648 | tf_op jit(solution)/shard_map/abhf,afhd->abhd/dot_general | solution.py:48
  70.8 0.8 convolution_convert_fusion.2
  71.8 26.1 %all-reduce.9.cloned.1.call-done = bf16[60,768]{1,0:T(8,128)(2,1)} async-done(((bf16[60,768]{1,0:T(8,128)(2,1)}), bf16[60,768]{1,0:T(8,128)(2,1)}) %all-reduce.9.cloned.1.call-update) | async-done | bytes 92176 | tf_op jit(solution)/shard_map/psum | solution.py:18
  97.9 1.0 convert_reduce_fusion.3
  98.9 0.2 fusion.156
  99.1 3.3 %fusion.72 = bf16[60,768]{1,0:T(8,128)(2,1)} fusion(bf16[2,768,768]{2,1,0:T(8,128)(2,1)} %param.44, bf16[2,768,768]{2,1,0:T(8,128)(2,1)} %param.42, bf16[60,768]{1,0:T(8,128)(2,1)S(1)} %get-tuple-element.30, f32[768]{0:T(1024)S(1)} %get-tuple-element.18, f32[768]{0:T(1024)S(1)} %get-tuple-element.11, f32[768]{0:T(1024)S(1)} %get-tuple-element.54, ...), kind=kOutput, calls=%fused_computation.76 | convolution fusion | flops 144921600 | bytes 2553312 | tf_op jit(solution)/shard_map/dot_general | solution.py:54
  102.5 26.1 %all-reduce.11.cloned.1.call-done = bf16[60,768]{1,0:T(8,128)(2,1)} async-done(((bf16[60,768]{1,0:T(8,128)(2,1)}), bf16[60,768]{1,0:T(8,128)(2,1)}) %all-reduce.11.cloned.1.call-update) | async-done | bytes 92176 | tf_op jit(solution)/shard_map/psum | solution.py:18
  128.7 1.0 convert_reduce_fusion.2
  129.7 0.2 fusion.152
  129.9 1.2 fusion.99
  131.1 1.2 fusion.100
  132.6 1.2 fusion.98
  134.4 5.4 %fusion.7 = f32[60,3,1,448]{3,2,1,0:T(1,128)S(1)} fusion(bf16[60,3,64,1]{2,3,1,0:T(2,128)(2,1)S(1)} %copy.68, pred[60,448]{1,0:T(8,128)(4,1)S(1)} %get-tuple-element.46, bf16[2,60,448,3,64]{2,4,3,1,0:T(8,128)(2,1)} %param.25, bf16[60,3,64]{2,1,0:T(4,128)(2,1)S(1)} %copy.55), kind=kOutput, calls=%fused_computation.11 | convolution fusion | flops 15482880 | bytes 12192000 | tf_op jit(solution)/shard_map/bhd,bshd->bhs/dot_general | solution.py:38
  139.8 0.2 fusion.65
  140.0 6.6 %fusion.6 = bf16[60,3,1,64]{3,2,1,0:T(2,128)(2,1)S(1)} fusion(pred[60,448]{1,0:T(8,128)(4,1)S(1)} %get-tuple-element.46, bf16[2,60,448,3,64]{2,4,3,1,0:T(8,128)(2,1)} %param.26, bf16[60,3,64]{2,1,0:T(4,128)(2,1)S(1)} %copy.57, bf16[60,3,448,1]{2,0,1,3:T(8,128)(2,1)S(1)} %fusion.65), kind=kOutput, calls=%fused_computation.9 | convolution fusion | flops 15482880 | bytes 12030720 | tf_op jit(solution)/shard_map/bhs,bshd->bhd/dot_general | solution.py:40
  146.8 0.9 convolution_convert_fusion.1
  147.7 0.2 all-reduce.15.cloned.1.call-start
  147.9 32.6 %broadcast_select_fusion.1 = (bf16[1,60,448,3,64]{2,4,3,1,0:T(8,128)(2,1)}, bf16[1,60,448,3,64]{2,4,3,1,0:T(8,128)(2,1)}, bf16[1,60,448,3,64]{2,4,3,1,0:T(8,128)(2,1)}, bf16[1,60,448,3,64]{2,4,3,1,0:T(8,128)(2,1)}) fusion(pred[60,448]{1,0:T(8,128)(4,1)S(1)} %get-tuple-element.46, bf16[2,60,448,3,64]{2,4,3,1,0:T(8,128)(2,1)} %param.26, ...), kind=kLoop, calls=%fused_computation.17 | loop fusion | flops 20643840 | bytes 82694400 | tf_op jit(solution)/shard_map/jit(_where)/select_n | solution.py:37
  180.5 1.0 convert_reduce_fusion.1
  181.8 0.3 fusion.101
  182.2 4.3 %fusion.386 = (f32[12,5,3]{1,2,0:T(4,128)S(1)}, f32[12,5,3,1500]{3,1,2,0:T(8,128)S(1)}) fusion(bf16[2,12,1500,3,64]{2,4,3,1,0:T(8,128)(2,1)} %param.27, bf16[12,5,3,64]{3,2,1,0:T(4,128)(2,1)S(1)} %reshape.268), kind=kOutput, calls=%fused_computation.435 | convolution fusion | flops 35101500 | bytes 8181648 | tf_op jit(solution)/shard_map/sub | solution.py:47
  186.5 5.0 %fusion.84 = bf16[12,5,3,64]{3,1,2,0:T(8,128)(2,1)S(1)} fusion(bf16[2,12,1500,3,64]{2,4,3,1,0:T(8,128)(2,1)} %param.28, f32[12,5,3,1500]{3,1,2,0:T(8,128)S(1)} %get-tuple-element.50, f32[12,5,3]{1,2,0:T(4,128)S(1)} %get-tuple-element.49), kind=kOutput, calls=%fused_computation.84 | convolution fusion | flops 35111520 | bytes 8181648 | tf_op jit(solution)/shard_map/abhf,afhd->abhd/dot_general | solution.py:48
  191.6 0.8 convolution_convert_fusion
  192.5 19.8 %pad_maximum_fusion.1 = bf16[2,60,448,3,64]{2,4,3,1,0:T(8,128)(2,1)} fusion(bf16[1,60,448,3,64]{2,4,3,1,0:T(8,128)(2,1)} %get-tuple-element.34, bf16[1,60,448,3,64]{2,4,3,1,0:T(8,128)(2,1)} %get-tuple-element.33), kind=kLoop, calls=%fused_computation.7 | loop fusion | flops 10321920 | bytes 41287680 | tf_op jit(solution)/shard_map/stack | solution.py:75
  212.3 6.4 %all-reduce.15.cloned.1.call-done = bf16[60,768]{1,0:T(8,128)(2,1)} async-done(((bf16[60,768]{1,0:T(8,128)(2,1)}), bf16[60,768]{1,0:T(8,128)(2,1)}) %all-reduce.15.cloned.1.call-update) | async-done | bytes 92176 | tf_op jit(solution)/shard_map/psum | solution.py:18
  218.7 1.0 convert_reduce_fusion
  219.7 0.2 fusion.144
  219.9 3.3 %fusion.75 = bf16[60,768]{1,0:T(8,128)(2,1)} fusion(bf16[2,768,768]{2,1,0:T(8,128)(2,1)} %param.44, bf16[2,768,768]{2,1,0:T(8,128)(2,1)} %param.42, bf16[60,768]{1,0:T(8,128)(2,1)S(1)} %get-tuple-element.24, f32[768]{0:T(1024)S(1)} %get-tuple-element.17, f32[768]{0:T(1024)S(1)} %get-tuple-element.9, f32[768]{0:T(1024)S(1)} %get-tuple-element.56, ...), kind=kOutput, calls=%fused_computation.77 | convolution fusion | flops 144921600 | bytes 2553312 | tf_op jit(solution)/shard_map/dot_general | solution.py:54
  223.2 19.8 %pad_maximum_fusion = bf16[2,60,448,3,64]{2,4,3,1,0:T(8,128)(2,1)} fusion(bf16[1,60,448,3,64]{2,4,3,1,0:T(8,128)(2,1)} %get-tuple-element.37, bf16[1,60,448,3,64]{2,4,3,1,0:T(8,128)(2,1)} %get-tuple-element.38), kind=kLoop, calls=%fused_computation.6 | loop fusion | flops 10321920 | bytes 41287680 | tf_op jit(solution)/shard_map/stack | solution.py:75
  243.0 6.4 %all-reduce.17.cloned.1.call-done = bf16[60,768]{1,0:T(8,128)(2,1)} async-done(((bf16[60,768]{1,0:T(8,128)(2,1)}), bf16[60,768]{1,0:T(8,128)(2,1)}) %all-reduce.17.cloned.1.call-update) | async-done | bytes 92176 | tf_op jit(solution)/shard_map/psum | solution.py:18
  249.4 1.6 fusion.182
  (71 shorter events, 3.2 us)
Async XLA Ops:
  7.2 52.6 %all-reduce.7.cloned.1.call-start = ((), (), s32[]{:S(2)}) async-start(), calls=%async_computation | async-start | bytes 196608 | tf_op jit(solution)/shard_map/psum | solution.py:18
  22.8 7.0 %copy-start.1 = (bf16[2,192,768]{2,1,0:T(8,128)(2,1)S(1)}, bf16[2,192,768]{2,1,0:T(8,128)(2,1)}, u32[]{:S(2)}) copy-start(bf16[2,192,768]{2,1,0:T(8,128)(2,1)} %param.36) | copy-start | bytes 1769476
  22.9 7.9 %copy-start.7 = (bf16[2,192]{1,0:T(2,128)(2,1)S(1)}, bf16[2,192]{1,0:T(2,128)(2,1)}, u32[]{:S(2)}) copy-start(bf16[2,192]{1,0:T(2,128)(2,1)} %param.39) | copy-start | bytes 2308
  22.9 7.9 %copy-start.3 = (bf16[2,768]{1,0:T(2,128)(2,1)S(1)}, bf16[2,768]{1,0:T(2,128)(2,1)}, u32[]{:S(2)}) copy-start(bf16[2,768]{1,0:T(2,128)(2,1)} %param.37) | copy-start | bytes 9220
  22.9 7.9 %copy-start.4 = (bf16[2,768]{1,0:T(2,128)(2,1)S(1)}, bf16[2,768]{1,0:T(2,128)(2,1)}, u32[]{:S(2)}) copy-start(bf16[2,768]{1,0:T(2,128)(2,1)} %param.41) | copy-start | bytes 9220
  22.9 36.8 %copy-start = (bf16[60,768]{1,0:T(8,128)(2,1)S(1)}, bf16[60,768]{1,0:T(8,128)(2,1)}, u32[]{:S(2)}) copy-start(bf16[60,768]{1,0:T(8,128)(2,1)} %param.23) | copy-start | bytes 276484
  22.9 38.1 %copy-start.8 = (bf16[2,768,192]{1,2,0:T(8,128)(2,1)S(1)}, bf16[2,768,192]{1,2,0:T(8,128)(2,1)}, u32[]{:S(2)}) copy-start(bf16[2,768,192]{1,2,0:T(8,128)(2,1)} %param.38) | copy-start | bytes 1769476
  30.7 67.2 %all-reduce.9.cloned.1.call-start = ((), (), s32[]{:S(2)}) async-start(), calls=%async_computation.1 | async-start | bytes 196608 | tf_op jit(solution)/shard_map/psum | solution.py:18
  60.8 10.1 %copy-start.2 = (bf16[2,192,768]{2,1,0:T(8,128)(2,1)S(1)}, bf16[2,192,768]{2,1,0:T(8,128)(2,1)}, u32[]{:S(2)}) copy-start(bf16[2,192,768]{2,1,0:T(8,128)(2,1)} %param.40) | copy-start | bytes 1769476
  61.3 10.5 %copy-start.5 = (bf16[2,768]{1,0:T(2,128)(2,1)S(1)}, bf16[2,768]{1,0:T(2,128)(2,1)}, u32[]{:S(2)}) copy-start(bf16[2,768]{1,0:T(2,128)(2,1)} %param.43) | copy-start | bytes 9220
  65.7 36.8 %copy-start.6 = (bf16[2,768]{1,0:T(2,128)(2,1)S(1)}, bf16[2,768]{1,0:T(2,128)(2,1)}, u32[]{:S(2)}) copy-start(bf16[2,768]{1,0:T(2,128)(2,1)} %param.45) | copy-start | bytes 9220
  71.7 57.0 %all-reduce.11.cloned.1.call-start = ((), (), s32[]{:S(2)}) async-start(), calls=%async_computation.2 | async-start | bytes 196608 | tf_op jit(solution)/shard_map/psum | solution.py:18
  102.5 78.1 %all-reduce.13.cloned.1.call-start = ((), (), s32[]{:S(2)}) async-start(), calls=%async_computation.3 | async-start | bytes 196608 | tf_op jit(solution)/shard_map/psum | solution.py:18
  147.7 34.1 %copy-start.9 = (bf16[2,768,192]{1,2,0:T(8,128)(2,1)S(1)}, bf16[2,768,192]{1,2,0:T(8,128)(2,1)}, u32[]{:S(2)}) copy-start(bf16[2,768,192]{1,2,0:T(8,128)(2,1)} %param.38) | copy-start | bytes 1769476
  147.7 71.0 %all-reduce.15.cloned.1.call-start = ((), (), s32[]{:S(2)}) async-start(), calls=%async_computation.4 | async-start | bytes 196608 | tf_op jit(solution)/shard_map/psum | solution.py:18
  192.5 57.0 %all-reduce.17.cloned.1.call-start = ((), (), s32[]{:S(2)}) async-start(), calls=%async_computation.5 | async-start | bytes 196608 | tf_op jit(solution)/shard_map/psum | solution.py:18
Sparse Core Ops, SparseCore 0:
  30.8 28.8 all-reduce.6
  71.8 26.0 all-reduce.8
  102.6 26.0 all-reduce.10
  147.8 26.0 all-reduce.12
  192.6 26.0 all-reduce.14
  223.4 26.0 all-reduce.16
where the time goes:
time: 259 us; the launch traced here: 258 us
  waiting for transfers between devices  94 us (36%)
  other arithmetic  85.8 us (33%)
  matrix products  60.7 us (23%)
  between operations  14.5 us (6%)
    psum x6, waiting for transfers between devices, tp_sum(): return lax.psum(part_out.astype(jnp.bfloat16), 'tp')  93.9 us
    another operation x2, other arithmetic, local_step(): return (hidden, jnp.stack(keys_out), jnp.stack(vals_out))  39.6 us
    select_n x1, other arithmetic, decoder_layer(): cache_v = jnp.where(slot_hit, new_val, cache_v)  32.6 us
    dot_general x2, matrix products, decoder_layer(): jnp.einsum('bhs,bshd->bhd', attn_probs, cache_v, preferred_element_type=j...  13.4 us
    dot_general x2, matrix products, decoder_layer(): jnp.einsum('bhd,bshd->bhs', query_heads, cache_k, preferred_element_type=...  10.8 us
    dot_general x2, matrix products, decoder_layer(): jnp.einsum('abhf,afhd->abhd', cross_probs, cross_v, preferred_element_typ...  10 us
    sub x2, matrix products, decoder_layer(): cross_probs = jax.nn.softmax(cross_scores, axis=-1).astype(jnp.bfloat16)  8.64 us
    dot_general x2, matrix products, decoder_layer(): jnp.dot(mlp_inner, layer_w['w_fc2'], preferred_element_type=jnp.float32)  6.56 us
  transfers between devices with their start and end apart: 6, of which 5 were waited for; matrix products, arithmetic and copies ran while one was open for 28% of the time, Pallas kernels for 0%

commit v1 on v0

v1 whole, which is shorter than its diff:
```python
import functools

import jax
import jax.numpy as jnp
from jax import lax
from jax.experimental import pallas as pl
from jax.experimental.pallas import tpu as pltpu
from jax.sharding import PartitionSpec as P

EPS = 1e-5
BF = jnp.bfloat16
F32 = jnp.float32
MESH = pl.DeviceIdType.MESH
ANY = pl.BlockSpec(memory_space=pl.ANY)
VM = pl.BlockSpec(memory_space=pltpu.VMEM)
NT = (((1,), (1,)), ((), ()))
VMEM_LIMIT = 60 * 1024 * 1024


def layer_norm(wide, gain_row, bias_row):
    center = wide - jnp.mean(wide, axis=-1, keepdims=True)
    var_est = jnp.mean(center * center, axis=-1, keepdims=True)
    return (center * lax.rsqrt(var_est + EPS) * gain_row.astype(F32) + bias_row.astype(F32)).astype(BF)


def dot(a, b):
    return jnp.dot(a, b, preferred_element_type=F32)


def dot_nt(a, b):
    return lax.dot_general(a, b, NT, preferred_element_type=F32)


def iota(shape, dim):
    return lax.broadcasted_iota(jnp.int32, shape, dim)


def self_kernel(layer, n_in, beams, *refs):
    h_hbm, pos_ref, g_hbm, b_hbm, wq_hbm, wk_hbm, wv_hbm, bq_hbm, bv_hbm, k_hbm, v_hbm = refs[:11]
    o_ref, ko_hbm, vo_hbm = refs[n_in:n_in + 3]
    h, g, b, wq, wk, wv, bq, bv, kbuf, vbuf, qs, kt, vt, os, psem, ksem, vsem, kosem, vosem = refs[n_in + 3:]
    rows = h.shape[0]
    audios = rows // beams
    slots = kbuf.shape[-1]
    scale = 64 ** -0.25

    small = [(h_hbm, h), (g_hbm, g), (b_hbm, b), (wq_hbm.at[layer], wq), (wk_hbm.at[layer], wk), (wv_hbm.at[layer], wv), (bq_hbm, bq), (bv_hbm, bv)]
    small = [pltpu.make_async_copy(s, d, psem.at[i]) for i, (s, d) in enumerate(small)]
    for c in small:
        c.start()

    def k_in(a):
        r = pl.ds(a * beams, beams)
        return pltpu.make_async_copy(k_hbm.at[layer, r], kbuf.at[r], ksem.at[a])

    def v_in(a):
        r = pl.ds(a * beams, beams)
        return pltpu.make_async_copy(v_hbm.at[layer, r], vbuf.at[r], vsem.at[a])

    def k_out(a):
        r = pl.ds(a * beams, beams)
        return pltpu.make_async_copy(kbuf.at[r], ko_hbm.at[layer, r], kosem.at[a])

    def v_out(a):
        r = pl.ds(a * beams, beams)
        return pltpu.make_async_copy(vbuf.at[r], vo_hbm.at[layer, r], vosem.at[a])

    @pl.loop(0, audios)
    def _(a):
        k_in(a).start()
        v_in(a).start()

    for c in small:
        c.wait()
    normed = layer_norm(h[...].astype(F32), g[layer, 0:1, :], b[layer, 0:1, :])
    q = ((dot_nt(normed, wq[...]) + bq[layer:layer + 1, :].astype(F32)) * scale).astype(BF)
    k = (dot_nt(normed, wk[...]) * scale).astype(BF).astype(F32)
    v = (dot_nt(normed, wv[...]) + bv[layer:layer + 1, :].astype(F32)).astype(BF).astype(F32)
    pad = jnp.zeros((128 - rows, k.shape[1]), F32)
    kt[...] = jnp.concatenate([k, pad], axis=0).T
    vt[...] = jnp.concatenate([v, pad], axis=0).T
    spread = (iota((rows * 8, rows), 0) // 8 == iota((rows * 8, rows), 1)).astype(F32).astype(BF)
    q8 = dot(spread, q)
    own = iota(q8.shape, 1) // 64 == iota(q8.shape, 0) % 8
    qs[...] = jnp.where(own, q8, 0.0)

    width = kbuf.shape[1]
    last = (slots // 128) * 128

    @pl.loop(0, audios)
    def _(a):
        k_in(a).wait()
        v_in(a).wait()
        pos = pos_ref[a * beams]
        tile = pos // 128

        def insert(start, size):
            hit = iota((width, size), 1) == pos - start
            for i in range(beams):
                r = a * beams + i
                pick = jnp.full((width, 128), r, jnp.int32)
                for buf, cols in ((kbuf, kt), (vbuf, vt)):
                    col = jnp.take_along_axis(cols[...], pick, axis=1)[:, :size]
                    old = buf[r, :, pl.ds(start, size)].astype(F32)
                    buf[r, :, pl.ds(start, size)] = jnp.where(hit, col, old).astype(BF)

        @pl.when(tile * 128 < last)
        def _():
            insert(pl.multiple_of(tile * 128, 128), 128)

        if slots > last:
            @pl.when(tile * 128 >= last)
            def _():
                insert(last, slots - last)

        k_out(a).start()
        v_out(a).start()
        scores = []
        for i in range(beams):
            r = a * beams + i
            scores.append(dot(qs[pl.ds(pl.multiple_of(r * 8, 8), 8), :].astype(BF), kbuf[r]))
        scores = jnp.concatenate(scores, axis=0)
        scores = jnp.where(iota(scores.shape, 1) <= pos, scores, -1e30)
        e = jnp.exp(scores - jnp.max(scores, axis=-1, keepdims=True))
        probs = (e * (1.0 / jnp.sum(e, axis=-1, keepdims=True))).astype(F32)
        for i in range(beams):
            r = a * beams + i
            out = dot_nt(probs[i * 8:i * 8 + 8].astype(BF), vbuf[r])
            mine = iota(out.shape, 1) // 64 == iota(out.shape, 0)
            os[pl.ds(r, 1), :] = jnp.sum(jnp.where(mine, out, 0.0), axis=0, keepdims=True)

    o_ref[...] = os[...].astype(BF)

    @pl.loop(0, audios)
    def _(a):
        k_out(a).wait()
        v_out(a).wait()


def self_call(layer, beams, h, pos, g, b, wq, wk, wv, bq, bv, k, v, outs):
    rows = h.shape[0]
    audios = rows // beams
    _, _, width, slots = k.shape
    args = (h, pos, g, b, wq, wk, wv, bq, bv, k, v) + outs
    n_in = len(args)
    return pl.pallas_call(
        functools.partial(self_kernel, layer, n_in, beams),
        out_shape=(jax.ShapeDtypeStruct((rows, width), BF), jax.ShapeDtypeStruct(k.shape, BF), jax.ShapeDtypeStruct(v.shape, BF)),
        in_specs=[ANY, pl.BlockSpec(memory_space=pltpu.SMEM)] + [ANY] * (n_in - 2),
        out_specs=(VM, ANY, ANY),
        input_output_aliases={11: 1, 12: 2} if outs else {},
        scratch_shapes=[
            pltpu.VMEM(h.shape, BF), pltpu.VMEM(g.shape, BF), pltpu.VMEM(b.shape, BF),
            pltpu.VMEM(wq.shape[1:], BF), pltpu.VMEM(wk.shape[1:], BF), pltpu.VMEM(wv.shape[1:], BF),
            pltpu.VMEM(bq.shape, BF), pltpu.VMEM(bv.shape, BF),
            pltpu.VMEM((rows, width, slots), BF), pltpu.VMEM((rows, width, slots), BF),
            pltpu.VMEM((rows * 8, width), F32), pltpu.VMEM((width, 128), F32), pltpu.VMEM((width, 128), F32), pltpu.VMEM((rows, width), F32),
            pltpu.SemaphoreType.DMA((8,)), pltpu.SemaphoreType.DMA((audios,)), pltpu.SemaphoreType.DMA((audios,)),
            pltpu.SemaphoreType.DMA((audios,)), pltpu.SemaphoreType.DMA((audios,)),
        ],
        compiler_params=pltpu.CompilerParams(vmem_limit_bytes=VMEM_LIMIT),
        name=f"self_{layer}",
    )(*args)


def rest_kernel(layer, beams, o_hbm, h_hbm, g_hbm, b_hbm, wo_hbm, bo_hbm, wc_hbm, bc_hbm, wco_hbm, bco_hbm, w1_hbm, b1_hbm, w2_hbm, b2_hbm, k_hbm, v_hbm, out_ref,
                o, h, g, b, wo, bo, wc, bc, wco, bco, w1, b1, w2, b2, kbuf, vbuf, qpad, opad, near, near_in, far, far_in, psem, ksem, vsem, near_s, near_r, far_s, far_r):
    rows = h.shape[0]
    audios = rows // beams
    width = o.shape[1]
    scale = 64 ** -0.25
    dp = lax.axis_index('dp')
    me = lax.axis_index('tp')
    core = me % 2
    mate = me + 1 - 2 * core
    others = ((me + 2) % 4, (mate + 2) % 4)

    small = [(o_hbm, o), (h_hbm, h), (g_hbm, g), (b_hbm, b), (wo_hbm.at[layer], wo), (bo_hbm, bo), (wc_hbm.at[layer], wc), (bc_hbm, bc),
             (wco_hbm.at[layer], wco), (bco_hbm, bco), (w1_hbm.at[layer], w1), (b1_hbm, b1), (w2_hbm.at[layer], w2), (b2_hbm, b2)]
    small = [pltpu.make_async_copy(s, d, psem.at[i]) for i, (s, d) in enumerate(small)]
    for c in small[:8]:
        c.start()

    def k_in(a):
        return pltpu.make_async_copy(k_hbm.at[layer, a], kbuf.at[a], ksem.at[a])

    def v_in(a):
        return pltpu.make_async_copy(v_hbm.at[layer, a], vbuf.at[a], vsem.at[a])

    @pl.loop(0, audios)
    def _(a):
        k_in(a).start()
        v_in(a).start()

    for c in small[8:]:
        c.start()
    barrier = pltpu.get_barrier_semaphore()
    for peer in (mate,) + others:
        pl.semaphore_signal(barrier, inc=1, device_id=(dp, peer), device_id_type=MESH)
    pl.semaphore_wait(barrier, 3)

    half = h.shape[1] // 2

    def all_sum(step, part):
        near[step] = part.astype(BF)
        c = pltpu.make_async_remote_copy(near.at[step], near_in.at[step], near_s.at[step], near_r.at[step], device_id=(dp, mate), device_id_type=MESH)
        c.start()
        c.wait()
        chip = (near[step].astype(F32) + near_in[step].astype(F32)).astype(BF)
        far[step, 0] = chip[:, :half]
        far[step, 1] = chip[:, half:]
        sends = [pltpu.make_async_remote_copy(far.at[step, core], far_in.at[step, core], far_s.at[step, j], far_r.at[step, core], device_id=(dp, others[j]), device_id_type=MESH) for j in range(2)]
        for c in sends:
            c.start()
        for j in range(2):
            pltpu.make_async_remote_copy(far.at[step, j], far_in.at[step, j], far_s.at[step, j], far_r.at[step, j], device_id=(dp, others[j]), device_id_type=MESH).wait_recv()
        for c in sends:
            c.wait_send()
        return chip.astype(F32) + jnp.concatenate([far_in[step, 0], far_in[step, 1]], axis=1).astype(F32)

    for c in small[:8]:
        c.wait()
    total = all_sum(0, dot(o[...], wo[...]))
    hid = (h[...].astype(F32) + total + bo[layer:layer + 1, :].astype(F32)).astype(BF)
    normed = layer_norm(hid.astype(F32), g[layer, 1:2, :], b[layer, 1:2, :])
    q = ((dot_nt(normed, wc[...]) + bc[layer:layer + 1, :].astype(F32)) * scale).astype(BF)
    r_pad, r_row = iota((audios * 8, rows), 0), iota((audios * 8, rows), 1)
    spread = ((r_pad // 8 == r_row // beams) & (r_pad % 8 == r_row % beams)).astype(F32).astype(BF)
    qpad[...] = dot(spread, q)

    @pl.loop(0, audios)
    def _(a):
        k_in(a).wait()
        v_in(a).wait()
        r = pl.ds(pl.multiple_of(a * 8, 8), 8)
        qa = qpad[r, :]
        qa = jnp.concatenate([qa] * (width // 64), axis=0)
        own = iota(qa.shape, 1) // 64 == iota(qa.shape, 0) // 8
        scores = dot(jnp.where(own, qa, 0.0).astype(BF), kbuf[a])
        e = jnp.exp(scores - jnp.max(scores, axis=-1, keepdims=True))
        probs = (e * (1.0 / jnp.sum(e, axis=-1, keepdims=True))).astype(BF)
        out = jnp.where(own, dot_nt(probs, vbuf[a]), 0.0)
        acc = out[0:8]
        for j in range(1, width // 64):
            acc = acc + out[j * 8:j * 8 + 8]
        opad[r, :] = acc

    for c in small[8:]:
        c.wait()
    c_pad, c_row = iota((rows, audios * 8), 1), iota((rows, audios * 8), 0)
    gather = ((c_pad // 8 == c_row // beams) & (c_pad % 8 == c_row % beams)).astype(F32).astype(BF)
    cross = dot(gather, opad[...].astype(BF)).astype(BF)
    total = all_sum(1, dot(cross, wco[...]))
    hid = (hid.astype(F32) + total + bco[layer:layer + 1, :].astype(F32)).astype(BF)
    normed = layer_norm(hid.astype(F32), g[layer, 2:3, :], b[layer, 2:3, :])
    inner = dot(normed, w1[...]) + b1[layer:layer + 1, :].astype(F32)
    inner = (0.5 * inner * (1.0 + lax.erf(inner * (2.0 ** -0.5)))).astype(BF)
    total = all_sum(2, dot(inner, w2[...]))
    out_ref[...] = (hid.astype(F32) + total + b2[layer:layer + 1, :].astype(F32)).astype(BF)


def rest_call(layer, beams, o, h, g, b, wo, bo, wc, bc, wco, bco, w1, b1, w2, b2, k, v):
    rows, dim = h.shape
    _, audios, width, frames = k.shape
    args = (o, h, g, b, wo, bo, wc, bc, wco, bco, w1, b1, w2, b2, k, v)
    return pl.pallas_call(
        functools.partial(rest_kernel, layer, beams),
        out_shape=jax.ShapeDtypeStruct(h.shape, BF),
        in_specs=[ANY] * len(args),
        out_specs=VM,
        scratch_shapes=[
            pltpu.VMEM(o.shape, BF), pltpu.VMEM(h.shape, BF), pltpu.VMEM(g.shape, BF), pltpu.VMEM(b.shape, BF),
            pltpu.VMEM(wo.shape[1:], BF), pltpu.VMEM(bo.shape, BF), pltpu.VMEM(wc.shape[1:], BF), pltpu.VMEM(bc.shape, BF),
            pltpu.VMEM(wco.shape[1:], BF), pltpu.VMEM(bco.shape, BF), pltpu.VMEM(w1.shape[1:], BF), pltpu.VMEM(b1.shape, BF),
            pltpu.VMEM(w2.shape[1:], BF), pltpu.VMEM(b2.shape, BF),
            pltpu.VMEM((audios, width, frames), BF), pltpu.VMEM((audios, width, frames), BF),
            pltpu.VMEM((audios * 8, width), F32), pltpu.VMEM((audios * 8, width), F32),
            pltpu.VMEM((3, rows, dim), BF), pltpu.VMEM((3, rows, dim), BF),
            pltpu.VMEM((3, 2, rows, dim // 2), BF), pltpu.VMEM((3, 2, rows, dim // 2), BF),
            pltpu.SemaphoreType.DMA((14,)), pltpu.SemaphoreType.DMA((audios,)), pltpu.SemaphoreType.DMA((audios,)),
            pltpu.SemaphoreType.DMA((3,)), pltpu.SemaphoreType.DMA((3,)), pltpu.SemaphoreType.DMA((3, 2)), pltpu.SemaphoreType.DMA((3, 2)),
        ],
        compiler_params=pltpu.CompilerParams(collective_id=layer, has_side_effects=True, vmem_limit_bytes=VMEM_LIMIT),
        name=f"rest_{layer}",
    )(*args)


def solution(mesh):
    cache_spec = P(None, 'dp', None, 'tp', None)
    col_spec = P(None, None, 'tp')
    row_spec = P(None, 'tp', None)
    vec_spec = P(None, 'tp')
    in_specs = (P('dp', None), P('dp'), cache_spec, cache_spec, cache_spec, cache_spec,
                P(), P(), col_spec, vec_spec, col_spec, col_spec, vec_spec, row_spec, P(), col_spec, vec_spec, row_spec, P(), col_spec, vec_spec, row_spec, P())

    def heads_first(cache):
        cache = jnp.transpose(cache, (0, 1, 3, 4, 2))
        return cache.reshape(cache.shape[:2] + (-1, cache.shape[-1]))

    def heads_last(cache, like):
        layers, batch, slots, heads, dim = like.shape
        return jnp.transpose(cache.reshape(layers, batch, heads, dim, slots), (0, 1, 4, 2, 3))

    def local_step(hidden, positions, self_keys, self_vals, cross_keys, cross_vals, g, b, wq, bq, wk, wv, bv, wo, bo, wc, bc, wco, bco, w1, b1, w2, b2):
        beams = hidden.shape[0] // cross_keys.shape[1]
        sk, sv, ck, cv = (heads_first(x) for x in (self_keys, self_vals, cross_keys, cross_vals))
        wq, wk, wv, wc = (jnp.swapaxes(w, 1, 2) for w in (wq, wk, wv, wc))
        outs = ()
        for layer in range(sk.shape[0]):
            o, *outs = self_call(layer, beams, hidden, positions, g, b, wq, wk, wv, bq, bv, sk, sv, tuple(outs))
            hidden = rest_call(layer, beams, o, hidden, g, b, wo, bo, wc, bc, wco, bco, w1, b1, w2, b2, ck, cv)
        return hidden, heads_last(outs[0], self_keys), heads_last(outs[1], self_vals)

    return jax.shard_map(local_step, mesh=mesh, in_specs=in_specs, out_specs=(P('dp', None), cache_spec, cache_spec), check_vma=False)
```

time: 259 us -> 97.7 us (0.38)
  waiting for transfers between devices: 94 us -> 0 us
  Pallas kernels: 0 us -> 92.7 us
  other arithmetic: 85.8 us -> 0 us
  matrix products: 60.7 us -> 0 us
  between operations: 14.5 us -> 0.66 us
    psum x6 -> x0, waiting for transfers between devices: 93.9 us -> none  [tp_sum(): return lax.psum(part_out.astype(jnp.bfloat16), 'tp')]
    pallas_call x0 -> x4, Pallas kernels: none -> 92.7 us  [the longest x2 55.7 us: rest_call(): pl.pallas_call(functools.partial(rest_kernel, layer, beams), out_shape=ja...]
    dot_general x20 -> x0, matrix products: 52.1 us -> none  [the longest x2 13.4 us: decoder_layer(): jnp.einsum('bhs,bshd->bhd', attn_probs, cache_v, preferred_element_type=j...]
    another operation x2 -> x0, other arithmetic: 39.6 us -> none  [local_step(): return (hidden, jnp.stack(keys_out), jnp.stack(vals_out))]
    select_n x1 -> x0, other arithmetic: 32.6 us -> none  [decoder_layer(): cache_v = jnp.where(slot_hit, new_val, cache_v)]
    sub x2 -> x0, matrix products: 8.64 us -> none  [decoder_layer(): cross_probs = jax.nn.softmax(cross_scores, axis=-1).astype(jnp.bfloat16)]
    reduce_sum x12 -> x0, other arithmetic: 8.21 us -> none  [the longest x6 6.17 us: layer_norm(): center = wide_vals - jnp.mean(wide_vals, axis=-1, keepdims=True)]
    unnamed x20 -> x3, local copies, waits for them, and re-layouts: 0.06 us -> 4.14 us
  transfers between devices with their start and end apart: 6 -> 0, of which waited for: 5 -> 0; matrix products, arithmetic and copies ran while one was open for 28% -> 0% of each run, Pallas kernels for 0% -> 0%
where the time goes in v1:
time: 97.7 us; the launch traced here: 97.5 us
  Pallas kernels  92.7 us (95%)
  local copies, waits for them, and re-layouts  4.14 us (4%)
    pallas_call x2, Pallas kernels, rest_call(): pl.pallas_call(functools.partial(rest_kernel, layer, beams), out_shape=ja...  55.7 us
    pallas_call x2, Pallas kernels, self_call(): pl.pallas_call(functools.partial(self_kernel, layer, n_in, beams), out_sh...  37 us
    unnamed x3, local copies, waits for them, and re-layouts  4.14 us

profile of v1, /device:TPU:0, one launch (start us, length us, event | category | flops | bytes accessed | tf_op | source)
XLA Modules:
  0.0 97.5 jit_solution(15180833674839771582)
XLA Ops:
  0.6 1.3 %copy.28.refs_2_.g_hbm = bf16[2,3,768]{2,1,0:T(4,128)(2,1)} copy(bf16[2,3,768]{2,0,1:T(2,128)(2,1)} %param.29) | data formatting | bytes 18432 | tf_op args[6]
  1.9 1.3 %copy.29.refs_3_.b_hbm = bf16[2,3,768]{2,1,0:T(4,128)(2,1)} copy(bf16[2,3,768]{2,0,1:T(2,128)(2,1)} %param.30) | data formatting | bytes 18432 | tf_op args[7]
  3.2 18.5 %self_0.1 = (bf16[60,192]{1,0:T(8,128)(2,1)}, bf16[2,60,192,448]{3,2,1,0:T(8,128)(2,1)}, bf16[2,60,192,448]{3,2,1,0:T(8,128)(2,1)}) custom-call(bf16[60,768]{1,0:T(8,128)(2,1)} %h_hbm.1, s32[60]{0:T(128)} %refs_1_.3, bf16[2,3,768]{2,1,0:T(4,128)(2,1)} %copy.28.refs_2_.g_hbm, bf16[2,3,768]{2,1,0:T(4,128)(2,1)} %copy.29.refs_3_.b_hbm, ...), custom_call_target="tpu_custom_call" | custom-call | tf_op jit(solution)/shard_map/self_0/pallas_call | solution.py:146
  21.8 29.0 %rest_0.1.refs_0_.h_hbm = bf16[60,768]{1,0:T(8,128)(2,1)} custom-call(bf16[60,192]{1,0:T(8,128)(2,1)} %get-tuple-element.9.o_hbm, bf16[60,768]{1,0:T(8,128)(2,1)} %h_hbm.1, bf16[2,3,768]{2,1,0:T(4,128)(2,1)} %copy.28.refs_2_.g_hbm, bf16[2,3,768]{2,1,0:T(4,128)(2,1)} %copy.29.refs_3_.b_hbm, bf16[2,192,768]{2,1,0:T(8,128)(2,1)} %wo_hbm.3, ...), custom_call_target="tpu_custom_call" | custom-call | tf_op jit(solution)/shard_map/rest_0/pallas_call | solution.py:266
  50.7 18.4 %self_1.1 = (bf16[60,192]{1,0:T(8,128)(2,1)}, bf16[2,60,192,448]{3,2,1,0:T(8,128)(2,1)}, bf16[2,60,192,448]{3,2,1,0:T(8,128)(2,1)}) custom-call(bf16[60,768]{1,0:T(8,128)(2,1)} %rest_0.1.refs_0_.h_hbm, s32[60]{0:T(128)} %refs_1_.3, bf16[2,3,768]{2,1,0:T(4,128)(2,1)} %copy.28.refs_2_.g_hbm, ...), custom_call_target="tpu_custom_call", output_to_operand_aliasing={{1}: (11, {}), {2}: (12, {})} | custom-call | tf_op jit(solution)/shard_map/self_1/pallas_call | solution.py:146
  69.2 26.7 %rest_1.1 = bf16[60,768]{1,0:T(8,128)(2,1)} custom-call(bf16[60,192]{1,0:T(8,128)(2,1)} %get-tuple-element.12.o_hbm, bf16[60,768]{1,0:T(8,128)(2,1)} %rest_0.1.refs_0_.h_hbm, bf16[2,3,768]{2,1,0:T(4,128)(2,1)} %copy.28.refs_2_.g_hbm, bf16[2,3,768]{2,1,0:T(4,128)(2,1)} %copy.29.refs_3_.b_hbm, bf16[2,192,768]{2,1,0:T(8,128)(2,1)} %wo_hbm.3, ...), custom_call_target="tpu_custom_call" | custom-call | tf_op jit(solution)/shard_map/rest_1/pallas_call | solution.py:266
  95.9 1.5 %copy.39 = bf16[60,768]{1,0:T(8,128)(2,1)} copy(bf16[60,768]{1,0:T(8,128)(2,1)} %rest_1.1) | data formatting | bytes 184320

commit v2 on v0

v2 whole, which is shorter than its diff:
```python
import functools

import jax
import jax.numpy as jnp
from jax import lax
from jax.experimental import pallas as pl
from jax.experimental.pallas import tpu as pltpu
from jax.sharding import PartitionSpec as P

EPS = 1e-5
BF = jnp.bfloat16
F32 = jnp.float32
MESH = pl.DeviceIdType.MESH
ANY = pl.BlockSpec(memory_space=pl.ANY)
VM = pl.BlockSpec(memory_space=pltpu.VMEM)
SMEM = pl.BlockSpec(memory_space=pltpu.SMEM)
DMA = pltpu.SemaphoreType.DMA
NT = (((1,), (1,)), ((), ()))
VMEM_LIMIT = 60 * 1024 * 1024
REST_LIMIT = 38 * 1024 * 1024


def layer_norm(wide, gain_row, bias_row):
    center = wide - jnp.mean(wide, axis=-1, keepdims=True)
    var_est = jnp.mean(center * center, axis=-1, keepdims=True)
    return (center * lax.rsqrt(var_est + EPS) * gain_row.astype(F32) + bias_row.astype(F32)).astype(BF)


def dot(a, b):
    return jnp.dot(a, b, preferred_element_type=F32)


def dot_nt(a, b):
    return lax.dot_general(a, b, NT, preferred_element_type=F32)


def iota(shape, dim):
    return lax.broadcasted_iota(jnp.int32, shape, dim)


def column_insert(buf, lead, cols, row, pos, slots):
    width = cols.shape[0]
    last = (slots // 128) * 128
    tile = pos // 128

    def insert(start, size):
        hit = iota((width, size), 1) == pos - start
        col = jnp.take_along_axis(cols[...], jnp.full((width, 128), row, jnp.int32), axis=1)[:, :size]
        old = buf[lead + (slice(None), pl.ds(start, size))].astype(F32)
        buf[lead + (slice(None), pl.ds(start, size))] = jnp.where(hit, col, old).astype(BF)

    @pl.when(tile * 128 < last)
    def _():
        insert(pl.multiple_of(tile * 128, 128), 128)

    if slots > last:
        @pl.when(tile * 128 >= last)
        def _():
            insert(last, slots - last)


def as_columns(rows):
    pad = jnp.zeros((128 - rows.shape[0], rows.shape[1]), F32)
    return jnp.concatenate([rows, pad], axis=0).T


def copies(pairs, sem):
    return [pltpu.make_async_copy(s, d, sem.at[i]) for i, (s, d) in enumerate(pairs)]


def self_kernel(layer, beams, h_hbm, pos_ref, g_hbm, b_hbm, wq_hbm, wk_hbm, wv_hbm, bq_hbm, bv_hbm, k_hbm, v_hbm, o_ref, ko_hbm, vo_hbm,
                h, g, b, wq, wk, wv, bq, bv, kbuf, vbuf, qs, kt, vt, os, psem, ksem, vsem, kosem, vosem):
    rows = h.shape[0]
    audios = rows // beams
    slots = kbuf.shape[-1]
    scale = 64 ** -0.25

    small = copies([(h_hbm, h), (g_hbm, g), (b_hbm, b), (wq_hbm.at[layer], wq), (wk_hbm.at[layer], wk), (wv_hbm.at[layer], wv), (bq_hbm, bq), (bv_hbm, bv)], psem)
    for c in small:
        c.start()

    def block(a, src, dst, sem):
        return pltpu.make_async_copy(src, dst, sem.at[a])

    def at(a):
        return pl.ds(a * beams, beams)

    def k_in(a):
        return block(a, k_hbm.at[layer, at(a)], kbuf.at[at(a)], ksem)

    def v_in(a):
        return block(a, v_hbm.at[layer, at(a)], vbuf.at[at(a)], vsem)

    def k_out(a):
        return block(a, kbuf.at[at(a)], ko_hbm.at[layer, at(a)], kosem)

    def v_out(a):
        return block(a, vbuf.at[at(a)], vo_hbm.at[layer, at(a)], vosem)

    @pl.loop(0, audios)
    def _(a):
        k_in(a).start()
        v_in(a).start()

    for c in small:
        c.wait()
    normed = layer_norm(h[...].astype(F32), g[layer, 0:1, :], b[layer, 0:1, :])
    q = ((dot_nt(normed, wq[...]) + bq[layer:layer + 1, :].astype(F32)) * scale).astype(BF)
    kt[...] = as_columns((dot_nt(normed, wk[...]) * scale).astype(BF).astype(F32))
    vt[...] = as_columns((dot_nt(normed, wv[...]) + bv[layer:layer + 1, :].astype(F32)).astype(BF).astype(F32))
    spread = (iota((rows * 8, rows), 0) // 8 == iota((rows * 8, rows), 1)).astype(F32).astype(BF)
    q8 = dot(spread, q)
    qs[...] = jnp.where(iota(q8.shape, 1) // 64 == iota(q8.shape, 0) % 8, q8, 0.0)

    @pl.loop(0, audios // 2)
    def _(pair):
        group = (pair * 2, pair * 2 + 1)
        for a in group:
            k_in(a).wait()
            v_in(a).wait()
            for i in range(beams):
                r = a * beams + i
                column_insert(kbuf, (r,), kt, r, pos_ref[a * beams], slots)
                column_insert(vbuf, (r,), vt, r, pos_ref[a * beams], slots)
            k_out(a).start()
            v_out(a).start()
        probs = []
        for a in group:
            scores = []
            for i in range(beams):
                r = a * beams + i
                scores.append(dot(qs[pl.ds(pl.multiple_of(r * 8, 8), 8), :].astype(BF), kbuf[r]))
            scores = jnp.concatenate(scores, axis=0)
            scores = jnp.where(iota(scores.shape, 1) <= pos_ref[a * beams], scores, -1e30)
            e = jnp.exp(scores - jnp.max(scores, axis=-1, keepdims=True))
            probs.append(e * (1.0 / jnp.sum(e, axis=-1, keepdims=True)))
        for a, p in zip(group, probs):
            for i in range(beams):
                r = a * beams + i
                out = dot_nt(p[i * 8:i * 8 + 8].astype(BF), vbuf[r])
                mine = iota(out.shape, 1) // 64 == iota(out.shape, 0)
                os[pl.ds(r, 1), :] = jnp.sum(jnp.where(mine, out, 0.0), axis=0, keepdims=True)

    o_ref[...] = os[...].astype(BF)

    @pl.loop(0, audios)
    def _(a):
        k_out(a).wait()
        v_out(a).wait()


def self_call(layer, beams, h, pos, g, b, wq, wk, wv, bq, bv, k, v):
    rows = h.shape[0]
    audios = rows // beams
    _, _, width, slots = k.shape
    args = (h, pos, g, b, wq, wk, wv, bq, bv, k, v)
    return pl.pallas_call(
        functools.partial(self_kernel, layer, beams),
        out_shape=(jax.ShapeDtypeStruct((rows, width), BF), jax.ShapeDtypeStruct(k.shape, BF), jax.ShapeDtypeStruct(v.shape, BF)),
        in_specs=[ANY, SMEM] + [ANY] * 9,
        out_specs=(VM, ANY, ANY),
        scratch_shapes=[
            pltpu.VMEM(h.shape, BF), pltpu.VMEM(g.shape, BF), pltpu.VMEM(b.shape, BF),
            pltpu.VMEM(wq.shape[1:], BF), pltpu.VMEM(wk.shape[1:], BF), pltpu.VMEM(wv.shape[1:], BF),
            pltpu.VMEM(bq.shape, BF), pltpu.VMEM(bv.shape, BF),
            pltpu.VMEM((rows, width, slots), BF), pltpu.VMEM((rows, width, slots), BF),
            pltpu.VMEM((rows * 8, width), F32), pltpu.VMEM((width, 128), F32), pltpu.VMEM((width, 128), F32), pltpu.VMEM((rows, width), F32),
            DMA((8,)), DMA((audios,)), DMA((audios,)), DMA((audios,)), DMA((audios,)),
        ],
        compiler_params=pltpu.CompilerParams(vmem_limit_bytes=VMEM_LIMIT),
        name=f"self_{layer}",
    )(*args)


def rest_kernel(beams, parts, o_hbm, h_hbm, pos_ref, g_hbm, b_hbm, wq_hbm, bq_hbm, wk_hbm, wv_hbm, bv_hbm, wo_hbm, bo_hbm, wc_hbm, bc_hbm, wco_hbm, bco_hbm, w1_hbm, b1_hbm, w2_hbm, b2_hbm,
                sk_hbm, sv_hbm, ck_hbm, cv_hbm, out_ref, sk, sv, kn_ref, vn_ref,
                o, h, g, b, wq, bq, wk, wv, bv, wo, bo, wc, bc, wco, bco, w1, b1, w2, b2, ck, cv, hid, qc, oc, qs, vs, sn, os, snd, rcv,
                psem, wsem, skem, svem, ckem, cvem, ssem, rsem):
    rows = h.shape[0]
    audios = rows // beams
    group = audios // parts
    prow = rows // parts
    width = o.shape[1]
    heads = width // 64
    scale = 64 ** -0.25
    dp = lax.axis_index('dp')
    me = lax.axis_index('tp')
    mate = me + 1 - 2 * (me % 2)
    peers = ((me + 2) % 4, (mate + 2) % 4, mate)

    small = copies([(o_hbm, o), (h_hbm, h), (g_hbm, g), (b_hbm, b), (bq_hbm, bq), (bv_hbm, bv), (bo_hbm, bo), (bc_hbm, bc), (bco_hbm, bco), (b1_hbm, b1), (b2_hbm, b2)], psem)
    first = copies([(x.at[0], y.at[0]) for x, y in ((wo_hbm, wo), (wc_hbm, wc), (wco_hbm, wco), (w1_hbm, w1), (w2_hbm, w2))], wsem.at[0])
    second = copies([(x.at[1], y.at[1]) for x, y in ((wo_hbm, wo), (wc_hbm, wc), (wco_hbm, wco), (w1_hbm, w1), (w2_hbm, w2))]
                    + [(x.at[1], y) for x, y in ((wq_hbm, wq), (wk_hbm, wk), (wv_hbm, wv))], wsem.at[1])

    def cross_in(layer, a):
        return pltpu.make_async_copy(ck_hbm.at[layer, a], ck.at[a], ckem.at[a]), pltpu.make_async_copy(cv_hbm.at[layer, a], cv.at[a], cvem.at[a])

    def self_in(a):
        r = pl.ds(a * beams, beams)
        return pltpu.make_async_copy(sk_hbm.at[1, r], sk.at[r], skem.at[a]), pltpu.make_async_copy(sv_hbm.at[1, r], sv.at[r], svem.at[a])

    def start(pair):
        for c in pair:
            c.start()

    def wait(pair):
        for c in pair:
            c.wait()

    start(small)
    start(first[:2])

    @pl.loop(0, audios)
    def _(a):
        start(cross_in(0, a))

    start(first[2:])
    barrier = pltpu.get_barrier_semaphore()
    for peer in peers:
        pl.semaphore_signal(barrier, inc=1, device_id=(dp, peer), device_id_type=MESH)

    start(second)

    @pl.loop(0, audios)
    def _(a):
        start(self_in(a))

    pl.semaphore_wait(barrier, 3)

    def sends(step, m):
        return [pltpu.make_async_remote_copy(snd.at[step, m], rcv.at[step, m, j], ssem.at[step, m, j], rsem.at[step, m, j], device_id=(dp, peer), device_id_type=MESH) for j, peer in enumerate(peers)]

    def push(step, m, part):
        snd[step, m] = part.astype(BF)
        start(sends(step, m))

    def total(step, m):
        wait(sends(step, m))
        mine = snd[step, m].astype(F32) + rcv[step, m, 2].astype(F32)
        return mine + (rcv[step, m, 0].astype(F32) + rcv[step, m, 1].astype(F32))

    def settle(step, m, bias):
        new = (hid[m].astype(F32) + total(step, m) + bias.astype(F32)).astype(BF)
        hid[m] = new
        return new.astype(F32)

    def flags(shape, rule):
        return rule(iota(shape, 0), iota(shape, 1)).astype(F32).astype(BF)

    def pick(m):
        return flags((prow, rows), lambda r, c: c == r + m * prow)

    def cross_half(layer, m, wide):
        normed = layer_norm(wide, g[layer, 1:2, :], b[layer, 1:2, :])
        q = ((dot_nt(normed, wc[layer]) + bc[layer:layer + 1, :].astype(F32)) * scale).astype(BF)
        qc[m] = dot(flags((group * 8, prow), lambda r, c: (r // 8 == c // beams) & (r % 8 == c % beams)), q)

        @pl.loop(0, group // 2)
        def _(i):
            probs = []
            local = (i * 2, i * 2 + 1)
            for n in local:
                a = m * group + n
                wait(cross_in(layer, a))
                qa = qc[m, pl.ds(pl.multiple_of(n * 8, 8), 8), :]
                qa = jnp.concatenate([qa] * heads, axis=0)
                own = iota(qa.shape, 1) // 64 == iota(qa.shape, 0) // 8
                scores = dot(jnp.where(own, qa, 0.0).astype(BF), ck[a])
                e = jnp.exp(scores - jnp.max(scores, axis=-1, keepdims=True))
                probs.append((e * (1.0 / jnp.sum(e, axis=-1, keepdims=True))).astype(BF))
            for n, p in zip(local, probs):
                out = dot_nt(p, cv[m * group + n])
                own = iota(out.shape, 1) // 64 == iota(out.shape, 0) // 8
                out = jnp.where(own, out, 0.0)
                acc = out[0:8]
                for j in range(1, heads):
                    acc = acc + out[j * 8:j * 8 + 8]
                oc[m, pl.ds(pl.multiple_of(n * 8, 8), 8), :] = acc

        if layer == 0:
            @pl.loop(0, group)
            def _(n):
                start(cross_in(1, m * group + n))
        cross = dot(flags((prow, group * 8), lambda r, c: (c // 8 == r // beams) & (c % 8 == r % beams)), oc[m].astype(BF)).astype(BF)
        return dot(cross, wco[layer])

    def mlp_half(layer, m, wide):
        normed = layer_norm(wide, g[layer, 2:3, :], b[layer, 2:3, :])
        inner = dot(normed, w1[layer]) + b1[layer:layer + 1, :].astype(F32)
        inner = (0.5 * inner * (1.0 + lax.erf(inner * (2.0 ** -0.5)))).astype(BF)
        return dot(inner, w2[layer])

    def self_half(m, wide):
        normed = layer_norm(wide, g[1, 0:1, :], b[1, 0:1, :])
        q = ((dot_nt(normed, wq[...]) + bq[1:2, :].astype(F32)) * scale).astype(BF)
        k = (dot_nt(normed, wk[...]) * scale).astype(BF)
        v = (dot_nt(normed, wv[...]) + bv[1:2, :].astype(F32)).astype(BF)
        kn_ref[m] = k
        vn_ref[m] = v
        spread = flags((prow * 8, prow), lambda r, c: r // 8 == c)
        q8 = dot(spread, q)
        own = iota(q8.shape, 1) // 64 == iota(q8.shape, 0) % 8
        q8 = jnp.where(own, q8, 0.0)
        qs[m] = q8
        vs[m] = jnp.where(own, dot(spread, v), 0.0)
        sn[m] = jnp.broadcast_to(jnp.sum(q8 * dot(spread, k), axis=-1, keepdims=True), sn.shape[1:])

        @pl.loop(0, group // 2)
        def _(i):
            local = (i * 2, i * 2 + 1)
            probs, news = [], []
            for n in local:
                a = m * group + n
                wait(self_in(a))
                pos = pos_ref[a * beams]
                scores = []
                for j in range(beams):
                    row = pl.ds(pl.multiple_of((n * beams + j) * 8, 8), 8)
                    scores.append(dot(qs[m, row, :].astype(BF), sk[a * beams + j]))
                scores = jnp.concatenate(scores, axis=0)
                fresh = sn[m, pl.ds(pl.multiple_of(n * beams * 8, 8), beams * 8), 0:1]
                slot = iota(scores.shape, 1)
                scores = jnp.where(slot < pos, scores, -1e30)
                top = jnp.maximum(jnp.max(scores, axis=-1, keepdims=True), fresh)
                e = jnp.where(slot < pos, jnp.exp(scores - top), 0.0)
                e_new = jnp.exp(fresh - top)
                inv = 1.0 / (jnp.sum(e, axis=-1, keepdims=True) + e_new)
                probs.append(e * inv)
                news.append((e_new * inv).astype(BF).astype(F32))
            for n, p, p_new in zip(local, probs, news):
                a = m * group + n
                for j in range(beams):
                    row = pl.ds(pl.multiple_of((n * beams + j) * 8, 8), 8)
                    out = dot_nt(p[j * 8:j * 8 + 8].astype(BF), sv[a * beams + j])
                    mine = iota(out.shape, 1) // 64 == iota(out.shape, 0)
                    out = jnp.where(mine, out, 0.0) + p_new[j * 8:j * 8 + 8] * vs[m, row, :]
                    os[m, pl.ds(n * beams + j, 1), :] = jnp.sum(out, axis=0, keepdims=True)

        return dot(os[m].astype(BF), wo[1])

    wait(small)
    wait(first[:1])
    for m in range(parts):
        push(0, m, dot(dot(pick(m), o[...]).astype(BF), wo[0]))
        hid[m] = dot(pick(m), h[...]).astype(BF)
    wait(first[1:3])
    for m in range(parts):
        push(1, m, cross_half(0, m, settle(0, m, bo[0:1, :])))
        if m == 0:
            wait(first[3:])
    for m in range(parts):
        push(2, m, mlp_half(0, m, settle(1, m, bco[0:1, :])))
    wait(second)
    for m in range(parts):
        push(3, m, self_half(m, settle(2, m, b2[0:1, :])))
    for m in range(parts):
        push(4, m, cross_half(1, m, settle(3, m, bo[1:2, :])))
    for m in range(parts):
        push(5, m, mlp_half(1, m, settle(4, m, bco[1:2, :])))
    result = jnp.zeros((rows, h.shape[1]), F32)
    for m in range(parts):
        place = flags((rows, prow), lambda r, c: r == c + m * prow)
        result = result + dot(place, settle(5, m, b2[1:2, :]).astype(BF))
    out_ref[...] = result.astype(BF)


def rest_call(beams, parts, o, h, pos, g, b, wq, bq, wk, wv, bv, wo, bo, wc, bc, wco, bco, w1, b1, w2, b2, sk, sv, ck, cv):
    rows, dim = h.shape
    _, audios, width, frames = ck.shape
    slots = sk.shape[-1]
    prow = rows // parts
    prows8 = prow * 8
    args = (o, h, pos, g, b, wq, bq, wk, wv, bv, wo, bo, wc, bc, wco, bco, w1, b1, w2, b2, sk, sv, ck, cv)

    def whole(x):
        return pltpu.VMEM(x.shape, BF)

    def one(x):
        return pltpu.VMEM(x.shape[1:], BF)

    return pl.pallas_call(
        functools.partial(rest_kernel, beams, parts),
        out_shape=(pltpu.VMEM(h.shape, BF), pltpu.VMEM((rows, width, slots), BF), pltpu.VMEM((rows, width, slots), BF), pltpu.VMEM((parts, prow, width), BF), pltpu.VMEM((parts, prow, width), BF)),
        in_specs=[ANY, ANY, SMEM] + [ANY] * (len(args) - 3),
        out_specs=(VM,) * 5,
        scratch_shapes=[
            whole(o), whole(h), whole(g), whole(b), one(wq), whole(bq), one(wk), one(wv), whole(bv), whole(wo), whole(bo), whole(wc), whole(bc),
            whole(wco), whole(bco), whole(w1), whole(b1), whole(w2), whole(b2), one(ck), one(cv),
            pltpu.VMEM((parts, prow, dim), BF),
            pltpu.VMEM((parts, audios // parts * 8, width), F32), pltpu.VMEM((parts, audios // parts * 8, width), F32),
            pltpu.VMEM((parts, prows8, width), F32), pltpu.VMEM((parts, prows8, width), F32), pltpu.VMEM((parts, prows8, 128), F32), pltpu.VMEM((parts, prow, width), F32),
            pltpu.VMEM((6, parts, prow, dim), BF), pltpu.VMEM((6, parts, 3, prow, dim), BF),
            DMA((11,)), DMA((2, 8)), DMA((audios,)), DMA((audios,)), DMA((audios,)), DMA((audios,)), DMA((6, parts, 3)), DMA((6, parts, 3)),
        ],
        compiler_params=pltpu.CompilerParams(collective_id=0, has_side_effects=True, vmem_limit_bytes=REST_LIMIT),
        name="rest",
    )(*args)


def write_kernel(layer, beams, ring, hid, pos_ref, kn, vn, sk, sv, ki_hbm, vi_hbm, out_ref, ko_hbm, vo_hbm, kst, vst, kt, vt, kosem, vosem):
    parts, prow, width = kn.shape
    rows = parts * prow
    audios = rows // beams
    slots = sk.shape[-1]

    def k_out(a, s):
        return pltpu.make_async_copy(kst.at[s], ko_hbm.at[layer, pl.ds(a * beams, beams)], kosem.at[s])

    def v_out(a, s):
        return pltpu.make_async_copy(vst.at[s], vo_hbm.at[layer, pl.ds(a * beams, beams)], vosem.at[s])

    def columns(new):
        both = jnp.zeros((rows, width), F32)
        for m in range(parts):
            place = (iota((rows, prow), 0) == iota((rows, prow), 1) + m * prow).astype(F32).astype(BF)
            both = both + dot(place, new[m])
        return as_columns(both)

    kt[...] = columns(kn)
    vt[...] = columns(vn)
    out_ref[...] = hid[...]

    @pl.loop(0, audios)
    def _(a):
        s = lax.rem(a, ring)

        @pl.when(a >= ring)
        def _():
            k_out(a - ring, s).wait()
            v_out(a - ring, s).wait()

        for src, st, cols, out in ((sk, kst, kt, k_out), (sv, vst, vt, v_out)):
            for i in range(beams):
                r = a * beams + i
                st[s, i] = src[r]
                column_insert(st, (s, i), cols, r, pos_ref[a * beams], slots)
            out(a, s).start()

    @pl.loop(audios - ring, audios)
    def _(a):
        k_out(a, lax.rem(a, ring)).wait()
        v_out(a, lax.rem(a, ring)).wait()


def write_call(layer, beams, hid, pos, kn, vn, sk, sv, ko, vo):
    rows, width, slots = sk.shape
    ring = 4
    return pl.pallas_call(
        functools.partial(write_kernel, layer, beams, ring),
        out_shape=(jax.ShapeDtypeStruct(hid.shape, BF), jax.ShapeDtypeStruct(ko.shape, BF), jax.ShapeDtypeStruct(vo.shape, BF)),
        in_specs=[VM, SMEM, VM, VM, VM, VM, ANY, ANY],
        out_specs=(VM, ANY, ANY),
        input_output_aliases={6: 1, 7: 2},
        scratch_shapes=[
            pltpu.VMEM((ring, beams, width, slots), BF), pltpu.VMEM((ring, beams, width, slots), BF),
            pltpu.VMEM((width, 128), F32), pltpu.VMEM((width, 128), F32), DMA((ring,)), DMA((ring,)),
        ],
        compiler_params=pltpu.CompilerParams(vmem_limit_bytes=10 * 1024 * 1024),
        name="write",
    )(hid, pos, kn, vn, sk, sv, ko, vo)


def solution(mesh):
    cache_spec = P(None, 'dp', None, 'tp', None)
    col_spec = P(None, None, 'tp')
    row_spec = P(None, 'tp', None)
    vec_spec = P(None, 'tp')
    in_specs = (P('dp', None), P('dp'), cache_spec, cache_spec, cache_spec, cache_spec,
                P(), P(), col_spec, vec_spec, col_spec, col_spec, vec_spec, row_spec, P(), col_spec, vec_spec, row_spec, P(), col_spec, vec_spec, row_spec, P())

    def heads_first(cache):
        cache = jnp.transpose(cache, (0, 1, 3, 4, 2))
        return cache.reshape(cache.shape[:2] + (-1, cache.shape[-1]))

    def heads_last(cache, like):
        layers, batch, slots, heads, dim = like.shape
        return jnp.transpose(cache.reshape(layers, batch, heads, dim, slots), (0, 1, 4, 2, 3))

    def local_step(hidden, positions, self_keys, self_vals, cross_keys, cross_vals, g, b, wq, bq, wk, wv, bv, wo, bo, wc, bc, wco, bco, w1, b1, w2, b2):
        beams = hidden.shape[0] // cross_keys.shape[1]
        sk, sv, ck, cv = (heads_first(x) for x in (self_keys, self_vals, cross_keys, cross_vals))
        wq, wk, wv, wc = (jnp.swapaxes(w, 1, 2) for w in (wq, wk, wv, wc))
        o, ko, vo = self_call(0, beams, hidden, positions, g, b, wq, wk, wv, bq, bv, sk, sv)
        hidden, sk1, sv1, kn, vn = rest_call(beams, 2, o, hidden, positions, g, b, wq, bq, wk, wv, bv, wo, bo, wc, bc, wco, bco, w1, b1, w2, b2, sk, sv, ck, cv)
        hidden, ko, vo = write_call(1, beams, hidden, positions, kn, vn, sk1, sv1, ko, vo)
        return hidden, heads_last(ko, self_keys), heads_last(vo, self_vals)

    return jax.shard_map(local_step, mesh=mesh, in_specs=in_specs, out_specs=(P('dp', None), cache_spec, cache_spec), check_vma=False)
```

time: 259 us -> 94.7 us (0.37)
  waiting for transfers between devices: 94 us -> 0 us
  Pallas kernels: 0 us -> 91.2 us
  other arithmetic: 85.8 us -> 0 us
  matrix products: 60.7 us -> 0 us
  between operations: 14.5 us -> 0.66 us
    psum x6 -> x0, waiting for transfers between devices: 93.9 us -> none  [tp_sum(): return lax.psum(part_out.astype(jnp.bfloat16), 'tp')]
    pallas_call x0 -> x3, Pallas kernels: none -> 91.2 us  [the longest x1 54.7 us: rest_call(): pl.pallas_call(functools.partial(rest_kernel, beams, parts), out_shape=(p...]
    dot_general x20 -> x0, matrix products: 52.1 us -> none  [the longest x2 13.4 us: decoder_layer(): jnp.einsum('bhs,bshd->bhd', attn_probs, cache_v, preferred_element_type=j...]
    another operation x2 -> x0, other arithmetic: 39.6 us -> none  [local_step(): return (hidden, jnp.stack(keys_out), jnp.stack(vals_out))]
    select_n x1 -> x0, other arithmetic: 32.6 us -> none  [decoder_layer(): cache_v = jnp.where(slot_hit, new_val, cache_v)]
    sub x2 -> x0, matrix products: 8.64 us -> none  [decoder_layer(): cross_probs = jax.nn.softmax(cross_scores, axis=-1).astype(jnp.bfloat16)]
    reduce_sum x12 -> x0, other arithmetic: 8.21 us -> none  [the longest x6 6.17 us: layer_norm(): center = wide_vals - jnp.mean(wide_vals, axis=-1, keepdims=True)]
  transfers between devices with their start and end apart: 6 -> 0, of which waited for: 5 -> 0; matrix products, arithmetic and copies ran while one was open for 28% -> 0% of each run, Pallas kernels for 0% -> 0%
where the time goes in v2:
time: 94.7 us; the launch traced here: 94.5 us
  Pallas kernels  91.2 us (96%)
  local copies, waits for them, and re-layouts  2.61 us (3%)
    pallas_call x1, Pallas kernels, rest_call(): pl.pallas_call(functools.partial(rest_kernel, beams, parts), out_shape=(p...  54.7 us
    pallas_call x1, Pallas kernels, self_call(): pl.pallas_call(functools.partial(self_kernel, layer, beams), out_shape=(j...  22 us
    pallas_call x1, Pallas kernels, write_call(): pl.pallas_call(functools.partial(write_kernel, layer, beams, ring), out_s...  14.6 us
    unnamed x4, local copies, waits for them, and re-layouts  2.61 us

profile of v2, /device:TPU:0, one launch (start us, length us, event | category | flops | bytes accessed | tf_op | source)
XLA Modules:
  0.0 94.5 jit_solution(8512034026361948746)
XLA Ops:
  0.6 1.3 %copy.28.g_hbm = bf16[2,3,768]{2,1,0:T(4,128)(2,1)} copy(bf16[2,3,768]{2,0,1:T(2,128)(2,1)} %param.29) | data formatting | bytes 18432 | tf_op args[6]
  1.9 1.3 %copy.29.b_hbm = bf16[2,3,768]{2,1,0:T(4,128)(2,1)} copy(bf16[2,3,768]{2,0,1:T(2,128)(2,1)} %param.30) | data formatting | bytes 18432 | tf_op args[7]
  3.2 22.0 %self_0.1 = (bf16[60,192]{1,0:T(8,128)(2,1)}, bf16[2,60,192,448]{3,2,1,0:T(8,128)(2,1)}, bf16[2,60,192,448]{3,2,1,0:T(8,128)(2,1)}) custom-call(bf16[60,768]{1,0:T(8,128)(2,1)} %h_hbm.3, s32[60]{0:T(128)} %pos_ref.5, bf16[2,3,768]{2,1,0:T(4,128)(2,1)} %copy.28.g_hbm, bf16[2,3,768]{2,1,0:T(4,128)(2,1)} %copy.29.b_hbm, bf16[2,192,768]{2,1,0:T(8,128)(2,1)} %bitcast.30, ...), custom_call_target="tpu_custom_call" | custom-call | tf_op jit(solution)/shard_map/self_0/pallas_call | solution.py:157
  25.2 0.0 copy-start
  25.2 54.7 %rest.1 = (bf16[60,768]{1,0:T(8,128)(2,1)S(1)}, bf16[60,192,448]{2,1,0:T(8,128)(2,1)S(1)}, bf16[60,192,448]{2,1,0:T(8,128)(2,1)S(1)}, bf16[2,30,192]{2,1,0:T(8,128)(2,1)S(1)}, bf16[2,30,192]{2,1,0:T(8,128)(2,1)S(1)}) custom-call(bf16[60,192]{1,0:T(8,128)(2,1)} %get-tuple-element.14.o_hbm, bf16[60,768]{1,0:T(8,128)(2,1)} %h_hbm.3, s32[60]{0:T(128)} %pos_ref.5, ...), custom_call_target="tpu_custom_call" | custom-call | tf_op jit(solution)/shard_map/rest/pallas_call | solution.py:382
  79.9 0.0 copy-done
  79.9 14.6 %write.1 = (bf16[60,768]{1,0:T(8,128)(2,1)}, bf16[2,60,192,448]{3,2,1,0:T(8,128)(2,1)}, bf16[2,60,192,448]{3,2,1,0:T(8,128)(2,1)}) custom-call(bf16[60,768]{1,0:T(8,128)(2,1)S(1)} %get-tuple-element.15.hid, s32[60]{0:T(128)S(1)} %copy-done, bf16[2,30,192]{2,1,0:T(8,128)(2,1)S(1)} %get-tuple-element.16.kn, ...), custom_call_target="tpu_custom_call", output_to_operand_aliasing={{1}: (6, {}), {2}: (7, {})} | custom-call | tf_op jit(solution)/shard_map/write/pallas_call | solution.py:449
Async XLA Ops:
  25.2 54.7 %copy-start = (s32[60]{0:T(128)S(1)}, s32[60]{0:T(128)}, u32[]{:S(2)}) copy-start(s32[60]{0:T(128)} %pos_ref.5) | copy-start | bytes 724

commit v3 on v2

--- a/solution.py
+++ b/solution.py
@@ -38,16 +38,18 @@
     return lax.broadcasted_iota(jnp.int32, shape, dim)
 
 
-def column_insert(buf, lead, cols, row, pos, slots):
-    width = cols.shape[0]
+def insert_slot(places, row, beams, pos, slots):
     last = (slots // 128) * 128
     tile = pos // 128
 
     def insert(start, size):
-        hit = iota((width, size), 1) == pos - start
-        col = jnp.take_along_axis(cols[...], jnp.full((width, 128), row, jnp.int32), axis=1)[:, :size]
-        old = buf[lead + (slice(None), pl.ds(start, size))].astype(F32)
-        buf[lead + (slice(None), pl.ds(start, size))] = jnp.where(hit, col, old).astype(BF)
+        for buf, cols in places:
+            width = cols.shape[0]
+            hit = iota((width, size), 1) == pos - start
+            for i in range(beams):
+                col = jnp.take_along_axis(cols[...], jnp.full((width, 128), row + i, jnp.int32), axis=1)[:, :size]
+                span = (row + i, slice(None), pl.ds(start, size))
+                buf[span] = jnp.where(hit, col.astype(BF), buf[span])
 
     @pl.when(tile * 128 < last)
     def _():
@@ -104,7 +106,7 @@
 
     for c in small:
         c.wait()
-    normed = layer_norm(h[...].astype(F32), g[layer, 0:1, :], b[layer, 0:1, :])
+    normed = layer_norm(h[...].astype(F32), g[0, layer:layer + 1, :], b[0, layer:layer + 1, :])
     q = ((dot_nt(normed, wq[...]) + bq[layer:layer + 1, :].astype(F32)) * scale).astype(BF)
     kt[...] = as_columns((dot_nt(normed, wk[...]) * scale).astype(BF).astype(F32))
     vt[...] = as_columns((dot_nt(normed, wv[...]) + bv[layer:layer + 1, :].astype(F32)).astype(BF).astype(F32))
@@ -118,10 +120,7 @@
         for a in group:
             k_in(a).wait()
             v_in(a).wait()
-            for i in range(beams):
-                r = a * beams + i
-                column_insert(kbuf, (r,), kt, r, pos_ref[a * beams], slots)
-                column_insert(vbuf, (r,), vt, r, pos_ref[a * beams], slots)
+            insert_slot(((kbuf, kt), (vbuf, vt)), a * beams, beams, pos_ref[a * beams], slots)
             k_out(a).start()
             v_out(a).start()
         probs = []
@@ -252,31 +251,34 @@
         return flags((prow, rows), lambda r, c: c == r + m * prow)
 
     def cross_half(layer, m, wide):
-        normed = layer_norm(wide, g[layer, 1:2, :], b[layer, 1:2, :])
+        normed = layer_norm(wide, g[1, layer:layer + 1, :], b[1, layer:layer + 1, :])
         q = ((dot_nt(normed, wc[layer]) + bc[layer:layer + 1, :].astype(F32)) * scale).astype(BF)
         qc[m] = dot(flags((group * 8, prow), lambda r, c: (r // 8 == c // beams) & (r % 8 == c % beams)), q)
 
-        @pl.loop(0, group // 2)
-        def _(i):
-            probs = []
-            local = (i * 2, i * 2 + 1)
-            for n in local:
-                a = m * group + n
-                wait(cross_in(layer, a))
-                qa = qc[m, pl.ds(pl.multiple_of(n * 8, 8), 8), :]
-                qa = jnp.concatenate([qa] * heads, axis=0)
-                own = iota(qa.shape, 1) // 64 == iota(qa.shape, 0) // 8
-                scores = dot(jnp.where(own, qa, 0.0).astype(BF), ck[a])
-                e = jnp.exp(scores - jnp.max(scores, axis=-1, keepdims=True))
-                probs.append((e * (1.0 / jnp.sum(e, axis=-1, keepdims=True))).astype(BF))
-            for n, p in zip(local, probs):
-                out = dot_nt(p, cv[m * group + n])
-                own = iota(out.shape, 1) // 64 == iota(out.shape, 0) // 8
-                out = jnp.where(own, out, 0.0)
-                acc = out[0:8]
-                for j in range(1, heads):
-                    acc = acc + out[j * 8:j * 8 + 8]
-                oc[m, pl.ds(pl.multiple_of(n * 8, 8), 8), :] = acc
+        @pl.loop(0, group)
+        def _(n):
+            wait(cross_in(layer, m * group + n))
+
+        own = iota((heads * 8, width), 1) // 64 == iota((heads * 8, width), 0) // 8
+
+        def probs_of(n):
+            qa = jnp.concatenate([qc[m, n * 8:n * 8 + 8, :]] * heads, axis=0)
+            scores = dot(jnp.where(own, qa, 0.0).astype(BF), ck[m * group + n])
+            e = jnp.exp(scores - jnp.max(scores, axis=-1, keepdims=True))
+            return (e * (1.0 / jnp.sum(e, axis=-1, keepdims=True))).astype(BF)
+
+        def mix(n, p):
+            out = jnp.where(own, dot_nt(p, cv[m * group + n]), 0.0)
+            acc = out[0:8]
+            for j in range(1, heads):
+                acc = acc + out[j * 8:j * 8 + 8]
+            oc[m, n * 8:n * 8 + 8, :] = acc
+
+        p = probs_of(0)
+        for n in range(group):
+            p_next = probs_of(n + 1) if n + 1 < group else None
+            mix(n, p)
+            p = p_next
 
         if layer == 0:
             @pl.loop(0, group)
@@ -286,13 +288,13 @@
         return dot(cross, wco[layer])
 
     def mlp_half(layer, m, wide):
-        normed = layer_norm(wide, g[layer, 2:3, :], b[layer, 2:3, :])
+        normed = layer_norm(wide, g[2, layer:layer + 1, :], b[2, layer:layer + 1, :])
         inner = dot(normed, w1[layer]) + b1[layer:layer + 1, :].astype(F32)
         inner = (0.5 * inner * (1.0 + lax.erf(inner * (2.0 ** -0.5)))).astype(BF)
         return dot(inner, w2[layer])
 
     def self_half(m, wide):
-        normed = layer_norm(wide, g[1, 0:1, :], b[1, 0:1, :])
+        normed = layer_norm(wide, g[0, 1:1 + 1, :], b[0, 1:1 + 1, :])
         q = ((dot_nt(normed, wq[...]) + bq[1:2, :].astype(F32)) * scale).astype(BF)
         k = (dot_nt(normed, wk[...]) * scale).astype(BF)
         v = (dot_nt(normed, wv[...]) + bv[1:2, :].astype(F32)).astype(BF)
@@ -398,17 +400,19 @@
     )(*args)
 
 
-def write_kernel(layer, beams, ring, hid, pos_ref, kn, vn, sk, sv, ki_hbm, vi_hbm, out_ref, ko_hbm, vo_hbm, kst, vst, kt, vt, kosem, vosem):
+def write_kernel(layer, beams, hid, pos_ref, kn, vn, sk_in, sv_in, ki_hbm, vi_hbm, out_ref, ko_hbm, vo_hbm, sk, sv, kt, vt, kosem, vosem):
     parts, prow, width = kn.shape
     rows = parts * prow
     audios = rows // beams
     slots = sk.shape[-1]
 
-    def k_out(a, s):
-        return pltpu.make_async_copy(kst.at[s], ko_hbm.at[layer, pl.ds(a * beams, beams)], kosem.at[s])
-
-    def v_out(a, s):
-        return pltpu.make_async_copy(vst.at[s], vo_hbm.at[layer, pl.ds(a * beams, beams)], vosem.at[s])
+    def k_out(a):
+        r = pl.ds(a * beams, beams)
+        return pltpu.make_async_copy(sk.at[r], ko_hbm.at[layer, r], kosem.at[a])
+
+    def v_out(a):
+        r = pl.ds(a * beams, beams)
+        return pltpu.make_async_copy(sv.at[r], vo_hbm.at[layer, r], vosem.at[a])
 
     def columns(new):
         both = jnp.zeros((rows, width), F32)
@@ -423,42 +427,29 @@
 
     @pl.loop(0, audios)
     def _(a):
-        s = lax.rem(a, ring)
-
-        @pl.when(a >= ring)
-        def _():
-            k_out(a - ring, s).wait()
-            v_out(a - ring, s).wait()
-
-        for src, st, cols, out in ((sk, kst, kt, k_out), (sv, vst, vt, v_out)):
-            for i in range(beams):
-                r = a * beams + i
-                st[s, i] = src[r]
-                column_insert(st, (s, i), cols, r, pos_ref[a * beams], slots)
-            out(a, s).start()
-
-    @pl.loop(audios - ring, audios)
-    def _(a):
-        k_out(a, lax.rem(a, ring)).wait()
-        v_out(a, lax.rem(a, ring)).wait()
+        insert_slot(((sk, kt), (sv, vt)), a * beams, beams, pos_ref[a * beams], slots)
+        k_out(a).start()
+        v_out(a).start()
+
+    @pl.loop(0, audios)
+    def _(a):
+        k_out(a).wait()
+        v_out(a).wait()
 
 
 def write_call(layer, beams, hid, pos, kn, vn, sk, sv, ko, vo):
     rows, width, slots = sk.shape
-    ring = 4
+    audios = rows // beams
     return pl.pallas_call(
-        functools.partial(write_kernel, layer, beams, ring),
-        out_shape=(jax.ShapeDtypeStruct(hid.shape, BF), jax.ShapeDtypeStruct(ko.shape, BF), jax.ShapeDtypeStruct(vo.shape, BF)),
+        functools.partial(write_kernel, layer, beams),
+        out_shape=(jax.ShapeDtypeStruct(hid.shape, BF), jax.ShapeDtypeStruct(ko.shape, BF), jax.ShapeDtypeStruct(vo.shape, BF), pltpu.VMEM(sk.shape, BF), pltpu.VMEM(sv.shape, BF)),
         in_specs=[VM, SMEM, VM, VM, VM, VM, ANY, ANY],
-        out_specs=(VM, ANY, ANY),
-        input_output_aliases={6: 1, 7: 2},
-        scratch_shapes=[
-            pltpu.VMEM((ring, beams, width, slots), BF), pltpu.VMEM((ring, beams, width, slots), BF),
-            pltpu.VMEM((width, 128), F32), pltpu.VMEM((width, 128), F32), DMA((ring,)), DMA((ring,)),
-        ],
-        compiler_params=pltpu.CompilerParams(vmem_limit_bytes=10 * 1024 * 1024),
+        out_specs=(VM, ANY, ANY, VM, VM),
+        input_output_aliases={4: 3, 5: 4, 6: 1, 7: 2},
+        scratch_shapes=[pltpu.VMEM((width, 128), F32), pltpu.VMEM((width, 128), F32), DMA((audios,)), DMA((audios,))],
+        compiler_params=pltpu.CompilerParams(vmem_limit_bytes=4 * 1024 * 1024),
         name="write",
-    )(hid, pos, kn, vn, sk, sv, ko, vo)
+    )(hid, pos, kn, vn, sk, sv, ko, vo)[:3]
 
 
 def solution(mesh):
@@ -481,6 +472,7 @@
         beams = hidden.shape[0] // cross_keys.shape[1]
         sk, sv, ck, cv = (heads_first(x) for x in (self_keys, self_vals, cross_keys, cross_vals))
         wq, wk, wv, wc = (jnp.swapaxes(w, 1, 2) for w in (wq, wk, wv, wc))
+        g, b = (jnp.swapaxes(x, 0, 1) for x in (g, b))
         o, ko, vo = self_call(0, beams, hidden, positions, g, b, wq, wk, wv, bq, bv, sk, sv)
         hidden, sk1, sv1, kn, vn = rest_call(beams, 2, o, hidden, positions, g, b, wq, bq, wk, wv, bv, wo, bo, wc, bc, wco, bco, w1, b1, w2, b2, sk, sv, ck, cv)
         hidden, ko, vo = write_call(1, beams, hidden, positions, kn, vn, sk1, sv1, ko, vo)

time: 94.7 us -> 78.9 us (0.83)
  Pallas kernels: 91.2 us -> 77.9 us
  local copies, waits for them, and re-layouts: 2.61 us -> 0.01 us
    pallas_call x1, Pallas kernels: 54.7 us -> 49.3 us  [rest_call(): pl.pallas_call(functools.partial(rest_kernel, beams, parts), out_shape=(p...]
    pallas_call x1, Pallas kernels: 14.6 us -> 9.79 us  [write_call(): pl.pallas_call(functools.partial(write_kernel, layer, beams), out_shape=(...]
    pallas_call x1, Pallas kernels: 22 us -> 18.8 us  [self_call(): pl.pallas_call(functools.partial(self_kernel, layer, beams), out_shape=(j...]
    unnamed x4 -> x2, local copies, waits for them, and re-layouts: 2.61 us -> 0.01 us
where the time goes in v3:
time: 78.9 us; the launch traced here: 78.7 us
  Pallas kernels  77.9 us (99%)
  between operations  0.82 us (1%)
    pallas_call x1, Pallas kernels, rest_call(): pl.pallas_call(functools.partial(rest_kernel, beams, parts), out_shape=(p...  49.3 us
    pallas_call x1, Pallas kernels, self_call(): pl.pallas_call(functools.partial(self_kernel, layer, beams), out_shape=(j...  18.8 us
    pallas_call x1, Pallas kernels, write_call(): pl.pallas_call(functools.partial(write_kernel, layer, beams), out_shape=(...  9.79 us

profile of v3, /device:TPU:0, one launch (start us, length us, event | category | flops | bytes accessed | tf_op | source)
XLA Modules:
  0.0 78.7 jit_solution(10683614109884957624)
XLA Ops:
  0.6 18.8 %self_0.1 = (bf16[60,192]{1,0:T(8,128)(2,1)}, bf16[2,60,192,448]{3,2,1,0:T(8,128)(2,1)}, bf16[2,60,192,448]{3,2,1,0:T(8,128)(2,1)}) custom-call(bf16[60,768]{1,0:T(8,128)(2,1)} %h_hbm.3, s32[60]{0:T(128)} %pos_ref.5, bf16[3,2,768]{2,1,0:T(2,128)(2,1)} %bitcast.39, bf16[3,2,768]{2,1,0:T(2,128)(2,1)} %bitcast.41, bf16[2,192,768]{2,1,0:T(8,128)(2,1)} %bitcast.32, ...), custom_call_target="tpu_custom_call" | custom-call | tf_op jit(solution)/shard_map/self_0/pallas_call | solution.py:156
  19.5 0.0 copy-start
  19.5 49.3 %rest.1 = (bf16[60,768]{1,0:T(8,128)(2,1)S(1)}, bf16[60,192,448]{2,1,0:T(8,128)(2,1)S(1)}, bf16[60,192,448]{2,1,0:T(8,128)(2,1)S(1)}, bf16[2,30,192]{2,1,0:T(8,128)(2,1)S(1)}, bf16[2,30,192]{2,1,0:T(8,128)(2,1)S(1)}) custom-call(bf16[60,192]{1,0:T(8,128)(2,1)} %get-tuple-element.14.o_hbm, bf16[60,768]{1,0:T(8,128)(2,1)} %h_hbm.3, s32[60]{0:T(128)} %pos_ref.5, ...), custom_call_target="tpu_custom_call" | custom-call | tf_op jit(solution)/shard_map/rest/pallas_call | solution.py:384
  68.8 0.0 copy-done
  68.8 9.8 %write.1 = (bf16[60,768]{1,0:T(8,128)(2,1)}, bf16[2,60,192,448]{3,2,1,0:T(8,128)(2,1)}, bf16[2,60,192,448]{3,2,1,0:T(8,128)(2,1)}, bf16[60,192,448]{2,1,0:T(8,128)(2,1)S(1)}, bf16[60,192,448]{2,1,0:T(8,128)(2,1)S(1)}) custom-call(bf16[60,768]{1,0:T(8,128)(2,1)S(1)} %get-tuple-element.15.hid, ...), custom_call_target="tpu_custom_call", output_to_operand_aliasing={{3}: (4, {}), {4}: (5, {}), {1}: (6, {}), {2}: (7, {})} | custom-call | tf_op jit(solution)/shard_map/write/pallas_call | solution.py:443
Async XLA Ops:
  19.5 49.3 %copy-start = (s32[60]{0:T(128)S(1)}, s32[60]{0:T(128)}, u32[]{:S(2)}) copy-start(s32[60]{0:T(128)} %pos_ref.5) | copy-start | bytes 724

commit v4 on v3

--- a/solution.py
+++ b/solution.py
@@ -166,15 +166,16 @@
             pltpu.VMEM((rows * 8, width), F32), pltpu.VMEM((width, 128), F32), pltpu.VMEM((width, 128), F32), pltpu.VMEM((rows, width), F32),
             DMA((8,)), DMA((audios,)), DMA((audios,)), DMA((audios,)), DMA((audios,)),
         ],
+        cost_estimate=pl.CostEstimate(flops=0, bytes_accessed=4 * k.size, transcendentals=0),
         compiler_params=pltpu.CompilerParams(vmem_limit_bytes=VMEM_LIMIT),
         name=f"self_{layer}",
     )(*args)
 
 
 def rest_kernel(beams, parts, o_hbm, h_hbm, pos_ref, g_hbm, b_hbm, wq_hbm, bq_hbm, wk_hbm, wv_hbm, bv_hbm, wo_hbm, bo_hbm, wc_hbm, bc_hbm, wco_hbm, bco_hbm, w1_hbm, b1_hbm, w2_hbm, b2_hbm,
-                sk_hbm, sv_hbm, ck_hbm, cv_hbm, out_ref, sk, sv, kn_ref, vn_ref,
-                o, h, g, b, wq, bq, wk, wv, bv, wo, bo, wc, bc, wco, bco, w1, b1, w2, b2, ck, cv, hid, qc, oc, qs, vs, sn, os, snd, rcv,
-                psem, wsem, skem, svem, ckem, cvem, ssem, rsem):
+                wo_far, wco_far, sk_hbm, sv_hbm, ck_hbm, cv_hbm, part_ref, out_ref, sk, sv, kn_ref, vn_ref,
+                o, h, g, b, wq, bq, wk, wv, bv, wo, bo, wc, bc, wco, wco1, bco, w1, b1, w2, b2, ck, cv, hid, qc, oc, qs, vs, sn, os, got, snd, rcv,
+                psem, wsem, gsem, gssem, grsem, skem, svem, ckem, cvem, ssem, rsem):
     rows = h.shape[0]
     audios = rows // beams
     group = audios // parts
@@ -188,9 +189,16 @@
     peers = ((me + 2) % 4, (mate + 2) % 4, mate)
 
     small = copies([(o_hbm, o), (h_hbm, h), (g_hbm, g), (b_hbm, b), (bq_hbm, bq), (bv_hbm, bv), (bo_hbm, bo), (bc_hbm, bc), (bco_hbm, bco), (b1_hbm, b1), (b2_hbm, b2)], psem)
-    first = copies([(x.at[0], y.at[0]) for x, y in ((wo_hbm, wo), (wc_hbm, wc), (wco_hbm, wco), (w1_hbm, w1), (w2_hbm, w2))], wsem.at[0])
-    second = copies([(x.at[1], y.at[1]) for x, y in ((wo_hbm, wo), (wc_hbm, wc), (wco_hbm, wco), (w1_hbm, w1), (w2_hbm, w2))]
-                    + [(x.at[1], y) for x, y in ((wq_hbm, wq), (wk_hbm, wk), (wv_hbm, wv))], wsem.at[1])
+    matrices = ((wo_hbm.at[0], wo_far.at[0], wo.at[0]), (wco_hbm.at[0], wco_far, wco.at[0]), (wo_hbm.at[1], wo_far.at[1], wo.at[1]))
+    gathered = [copies([(own, rows_of.at[0])], gsem.at[i]) for i, (own, _, rows_of) in enumerate(matrices)]
+
+    def shared(i):
+        own, far, rows_of = matrices[i]
+        return [pltpu.make_async_remote_copy(src, rows_of.at[1 + j], gssem.at[i, j], grsem.at[i, j], device_id=(dp, mate), device_id_type=MESH) for j, src in enumerate((own, far))]
+
+    first = copies([(x.at[0], y.at[0]) for x, y in ((wc_hbm, wc), (w1_hbm, w1), (w2_hbm, w2))], wsem.at[0])
+    second = copies([(x.at[1], y.at[1]) for x, y in ((wc_hbm, wc), (w1_hbm, w1), (w2_hbm, w2))]
+                    + [(wco_hbm.at[1], wco1)] + [(x.at[1], y) for x, y in ((wq_hbm, wq), (wk_hbm, wk), (wv_hbm, wv))], wsem.at[1])
 
     def cross_in(layer, a):
         return pltpu.make_async_copy(ck_hbm.at[layer, a], ck.at[a], ckem.at[a]), pltpu.make_async_copy(cv_hbm.at[layer, a], cv.at[a], cvem.at[a])
@@ -208,17 +216,20 @@
             c.wait()
 
     start(small)
-    start(first[:2])
+    start(gathered[0])
+    start(first[:1])
 
     @pl.loop(0, audios)
     def _(a):
         start(cross_in(0, a))
 
-    start(first[2:])
+    start(gathered[1])
+    start(first[1:])
     barrier = pltpu.get_barrier_semaphore()
     for peer in peers:
         pl.semaphore_signal(barrier, inc=1, device_id=(dp, peer), device_id_type=MESH)
 
+    start(gathered[2])
     start(second)
 
     @pl.loop(0, audios)
@@ -226,6 +237,7 @@
         start(self_in(a))
 
     pl.semaphore_wait(barrier, 3)
+    start(shared(0))
 
     def sends(step, m):
         return [pltpu.make_async_remote_copy(snd.at[step, m], rcv.at[step, m, j], ssem.at[step, m, j], rsem.at[step, m, j], device_id=(dp, peer), device_id_type=MESH) for j, peer in enumerate(peers)]
@@ -239,8 +251,21 @@
         mine = snd[step, m].astype(F32) + rcv[step, m, 2].astype(F32)
         return mine + (rcv[step, m, 0].astype(F32) + rcv[step, m, 1].astype(F32))
 
-    def settle(step, m, bias):
-        new = (hid[m].astype(F32) + total(step, m) + bias.astype(F32)).astype(BF)
+    def heads_sends(step, m):
+        return [pltpu.make_async_remote_copy(got.at[step, m, 3], got.at[step, m, j], ssem.at[step, m, j], rsem.at[step, m, j], device_id=(dp, peer), device_id_type=MESH) for j, peer in enumerate(peers)]
+
+    def push_heads(step, m, out):
+        got[step, m, 3] = out
+        start(heads_sends(step, m))
+
+    def project(step, m, i):
+        wait(heads_sends(step, m))
+        _, far, rows_of = matrices[i]
+        here = dot(got[step, m, 3], rows_of[0]) + dot(got[step, m, 2], rows_of[1])
+        return here + (dot(got[step, m, 0], far[...]) + dot(got[step, m, 1], rows_of[2]))
+
+    def settle(m, update, bias):
+        new = (hid[m].astype(F32) + update + bias.astype(F32)).astype(BF)
         hid[m] = new
         return new.astype(F32)
 
@@ -285,7 +310,7 @@
             def _(n):
                 start(cross_in(1, m * group + n))
         cross = dot(flags((prow, group * 8), lambda r, c: (c // 8 == r // beams) & (c % 8 == r % beams)), oc[m].astype(BF)).astype(BF)
-        return dot(cross, wco[layer])
+        return cross
 
     def mlp_half(layer, m, wide):
         normed = layer_norm(wide, g[2, layer:layer + 1, :], b[2, layer:layer + 1, :])
@@ -339,41 +364,50 @@
                     out = jnp.where(mine, out, 0.0) + p_new[j * 8:j * 8 + 8] * vs[m, row, :]
                     os[m, pl.ds(n * beams + j, 1), :] = jnp.sum(out, axis=0, keepdims=True)
 
-        return dot(os[m].astype(BF), wo[1])
+        return os[m].astype(BF)
 
     wait(small)
+    for m in range(parts):
+        push_heads(0, m, dot(pick(m), o[...]).astype(BF))
+    start(shared(1))
+    start(shared(2))
+    for m in range(parts):
+        hid[m] = dot(pick(m), h[...]).astype(BF)
+    wait(gathered[0])
+    wait(shared(0))
     wait(first[:1])
     for m in range(parts):
-        push(0, m, dot(dot(pick(m), o[...]).astype(BF), wo[0]))
-        hid[m] = dot(pick(m), h[...]).astype(BF)
-    wait(first[1:3])
-    for m in range(parts):
-        push(1, m, cross_half(0, m, settle(0, m, bo[0:1, :])))
-        if m == 0:
-            wait(first[3:])
-    for m in range(parts):
-        push(2, m, mlp_half(0, m, settle(1, m, bco[0:1, :])))
+        push_heads(1, m, cross_half(0, m, settle(m, project(0, m, 0), bo[0:1, :])))
+    wait(gathered[1])
+    wait(shared(1))
+    wait(first[1:])
+    for m in range(parts):
+        push(2, m, mlp_half(0, m, settle(m, project(1, m, 1), bco[0:1, :])))
+    wait(gathered[2])
+    wait(shared(2))
     wait(second)
     for m in range(parts):
-        push(3, m, self_half(m, settle(2, m, b2[0:1, :])))
-    for m in range(parts):
-        push(4, m, cross_half(1, m, settle(3, m, bo[1:2, :])))
-    for m in range(parts):
-        push(5, m, mlp_half(1, m, settle(4, m, bco[1:2, :])))
-    result = jnp.zeros((rows, h.shape[1]), F32)
+        push_heads(3, m, self_half(m, settle(m, total(2, m), b2[0:1, :])))
+    for m in range(parts):
+        push(4, m, dot(cross_half(1, m, settle(m, project(3, m, 2), bo[1:2, :])), wco1[...]))
+    final = jnp.zeros((rows, h.shape[1]), F32)
+    resid = jnp.zeros((rows, h.shape[1]), F32)
     for m in range(parts):
         place = flags((rows, prow), lambda r, c: r == c + m * prow)
-        result = result + dot(place, settle(5, m, b2[1:2, :]).astype(BF))
-    out_ref[...] = result.astype(BF)
-
-
-def rest_call(beams, parts, o, h, pos, g, b, wq, bq, wk, wv, bv, wo, bo, wc, bc, wco, bco, w1, b1, w2, b2, sk, sv, ck, cv):
+        wide = settle(m, total(4, m), bco[1:2, :])
+        final = final + dot(place, mlp_half(1, m, wide).astype(BF))
+        resid = resid + dot(place, hid[m])
+    part_ref[...] = final.astype(BF)
+    out_ref[...] = resid.astype(BF)
+
+
+def rest_call(beams, parts, o, h, pos, g, b, wq, bq, wk, wv, bv, wo, bo, wc, bc, wco, bco, w1, b1, w2, b2, more, sk, sv, ck, cv):
     rows, dim = h.shape
     _, audios, width, frames = ck.shape
     slots = sk.shape[-1]
     prow = rows // parts
     prows8 = prow * 8
-    args = (o, h, pos, g, b, wq, bq, wk, wv, bv, wo, bo, wc, bc, wco, bco, w1, b1, w2, b2, sk, sv, ck, cv)
+    args = (o, h, pos, g, b, wq, bq, wk, wv, bv, wo, bo, wc, bc, wco, bco, w1, b1, w2, b2) + more + (sk, sv, ck, cv)
 
     def whole(x):
         return pltpu.VMEM(x.shape, BF)
@@ -383,24 +417,24 @@
 
     return pl.pallas_call(
         functools.partial(rest_kernel, beams, parts),
-        out_shape=(pltpu.VMEM(h.shape, BF), pltpu.VMEM((rows, width, slots), BF), pltpu.VMEM((rows, width, slots), BF), pltpu.VMEM((parts, prow, width), BF), pltpu.VMEM((parts, prow, width), BF)),
-        in_specs=[ANY, ANY, SMEM] + [ANY] * (len(args) - 3),
-        out_specs=(VM,) * 5,
+        out_shape=(pltpu.VMEM(h.shape, BF), pltpu.VMEM(h.shape, BF), pltpu.VMEM((rows, width, slots), BF), pltpu.VMEM((rows, width, slots), BF), pltpu.VMEM((parts, prow, width), BF), pltpu.VMEM((parts, prow, width), BF)),
+        in_specs=[ANY, ANY, SMEM] + [ANY] * (len(args) - 9) + [VM, VM] + [ANY] * 4,
+        out_specs=(VM,) * 6,
         scratch_shapes=[
-            whole(o), whole(h), whole(g), whole(b), one(wq), whole(bq), one(wk), one(wv), whole(bv), whole(wo), whole(bo), whole(wc), whole(bc),
-            whole(wco), whole(bco), whole(w1), whole(b1), whole(w2), whole(b2), one(ck), one(cv),
+            whole(o), whole(h), whole(g), whole(b), one(wq), whole(bq), one(wk), one(wv), whole(bv), pltpu.VMEM((2, 3, width, dim), BF), whole(bo), whole(wc), whole(bc),
+            pltpu.VMEM((1, 3, width, dim), BF), one(wco), whole(bco), whole(w1), whole(b1), whole(w2), whole(b2), one(ck), one(cv),
             pltpu.VMEM((parts, prow, dim), BF),
             pltpu.VMEM((parts, audios // parts * 8, width), F32), pltpu.VMEM((parts, audios // parts * 8, width), F32),
             pltpu.VMEM((parts, prows8, width), F32), pltpu.VMEM((parts, prows8, width), F32), pltpu.VMEM((parts, prows8, 128), F32), pltpu.VMEM((parts, prow, width), F32),
-            pltpu.VMEM((6, parts, prow, dim), BF), pltpu.VMEM((6, parts, 3, prow, dim), BF),
-            DMA((11,)), DMA((2, 8)), DMA((audios,)), DMA((audios,)), DMA((audios,)), DMA((audios,)), DMA((6, parts, 3)), DMA((6, parts, 3)),
+            pltpu.VMEM((6, parts, 4, prow, width), BF), pltpu.VMEM((6, parts, prow, dim), BF), pltpu.VMEM((6, parts, 3, prow, dim), BF),
+            DMA((11,)), DMA((2, 8)), DMA((3, 1)), DMA((3, 2)), DMA((3, 2)), DMA((audios,)), DMA((audios,)), DMA((audios,)), DMA((audios,)), DMA((6, parts, 3)), DMA((6, parts, 3)),
         ],
         compiler_params=pltpu.CompilerParams(collective_id=0, has_side_effects=True, vmem_limit_bytes=REST_LIMIT),
         name="rest",
     )(*args)
 
 
-def write_kernel(layer, beams, hid, pos_ref, kn, vn, sk_in, sv_in, ki_hbm, vi_hbm, out_ref, ko_hbm, vo_hbm, sk, sv, kt, vt, kosem, vosem):
+def write_kernel(layer, beams, pos_ref, kn, vn, sk_in, sv_in, ki_hbm, vi_hbm, ko_hbm, vo_hbm, sk, sv, kt, vt, kosem, vosem):
     parts, prow, width = kn.shape
     rows = parts * prow
     audios = rows // beams
@@ -423,7 +457,6 @@
 
     kt[...] = columns(kn)
     vt[...] = columns(vn)
-    out_ref[...] = hid[...]
 
     @pl.loop(0, audios)
     def _(a):
@@ -437,19 +470,20 @@
         v_out(a).wait()
 
 
-def write_call(layer, beams, hid, pos, kn, vn, sk, sv, ko, vo):
+def write_call(layer, beams, pos, kn, vn, sk, sv, ko, vo):
     rows, width, slots = sk.shape
     audios = rows // beams
     return pl.pallas_call(
         functools.partial(write_kernel, layer, beams),
-        out_shape=(jax.ShapeDtypeStruct(hid.shape, BF), jax.ShapeDtypeStruct(ko.shape, BF), jax.ShapeDtypeStruct(vo.shape, BF), pltpu.VMEM(sk.shape, BF), pltpu.VMEM(sv.shape, BF)),
-        in_specs=[VM, SMEM, VM, VM, VM, VM, ANY, ANY],
-        out_specs=(VM, ANY, ANY, VM, VM),
-        input_output_aliases={4: 3, 5: 4, 6: 1, 7: 2},
+        out_shape=(jax.ShapeDtypeStruct(ko.shape, BF), jax.ShapeDtypeStruct(vo.shape, BF), pltpu.VMEM(sk.shape, BF), pltpu.VMEM(sv.shape, BF)),
+        in_specs=[SMEM, VM, VM, VM, VM, ANY, ANY],
+        out_specs=(ANY, ANY, VM, VM),
+        input_output_aliases={3: 2, 4: 3, 5: 0, 6: 1},
+        cost_estimate=pl.CostEstimate(flops=0, bytes_accessed=4 * sk.size, transcendentals=0),
         scratch_shapes=[pltpu.VMEM((width, 128), F32), pltpu.VMEM((width, 128), F32), DMA((audios,)), DMA((audios,))],
         compiler_params=pltpu.CompilerParams(vmem_limit_bytes=4 * 1024 * 1024),
         name="write",
-    )(hid, pos, kn, vn, sk, sv, ko, vo)[:3]
+    )(pos, kn, vn, sk, sv, ko, vo)[:2]
 
 
 def solution(mesh):
@@ -473,9 +507,15 @@
         sk, sv, ck, cv = (heads_first(x) for x in (self_keys, self_vals, cross_keys, cross_vals))
         wq, wk, wv, wc = (jnp.swapaxes(w, 1, 2) for w in (wq, wk, wv, wc))
         g, b = (jnp.swapaxes(x, 0, 1) for x in (g, b))
+        def hop(x, flip):
+            return lax.ppermute(x, 'tp', [(i, i ^ flip) for i in range(4)])
+
+        more = (hop(wo, 2), hop(wco[0], 2))
         o, ko, vo = self_call(0, beams, hidden, positions, g, b, wq, wk, wv, bq, bv, sk, sv)
-        hidden, sk1, sv1, kn, vn = rest_call(beams, 2, o, hidden, positions, g, b, wq, bq, wk, wv, bv, wo, bo, wc, bc, wco, bco, w1, b1, w2, b2, sk, sv, ck, cv)
-        hidden, ko, vo = write_call(1, beams, hidden, positions, kn, vn, sk1, sv1, ko, vo)
+        part, hidden, sk1, sv1, kn, vn = rest_call(beams, 2, o, hidden, positions, g, b, wq, bq, wk, wv, bv, wo, bo, wc, bc, wco, bco, w1, b1, w2, b2, more, sk, sv, ck, cv)
+        ko, vo = write_call(1, beams, positions, kn, vn, sk1, sv1, ko, vo)
+        here, mate, far, diag = (x.astype(F32) for x in (part, hop(part, 1), hop(part, 2), hop(part, 3)))
+        hidden = (hidden.astype(F32) + ((here + mate) + (far + diag)) + b2[1].astype(F32)).astype(BF)
         return hidden, heads_last(ko, self_keys), heads_last(vo, self_vals)
 
     return jax.shard_map(local_step, mesh=mesh, in_specs=in_specs, out_specs=(P('dp', None), cache_spec, cache_spec), check_vma=False)

time: 78.9 us -> 77.8 us (0.986)
  Pallas kernels: 77.9 us -> 69 us
  starting transfers between devices: 0 us -> 5.28 us
  local copies, waits for them, and re-layouts: 0.01 us -> 1.88 us
    pallas_call x1, Pallas kernels: 49.3 us -> 41 us  [rest_call(): pl.pallas_call(functools.partial(rest_kernel, beams, parts), out_shape=(p...]
    ppermute x0 -> x5, starting transfers between devices: none -> 5.28 us  [hop(): return lax.ppermute(x, 'tp', [(i, i ^ flip) for i in range(4)])]
    squeeze x0 -> x1, local copies, waits for them, and re-layouts: none -> 0.98 us  [local_step(): more = (hop(wo, 2), hop(wco[0], 2))]
    unnamed x2 -> x8, local copies, waits for them, and re-layouts: 0.01 us -> 0.9 us
  transfers between devices with their start and end apart: 0 -> 5, of which waited for: 0 -> 0; matrix products, arithmetic and copies ran while one was open for 0% -> 1% of each run, Pallas kernels for 0% -> 36%
where the time goes in v4:
time: 77.8 us; the launch traced here: 77.6 us
  Pallas kernels  69 us (89%)
  starting transfers between devices  5.28 us (7%)
  local copies, waits for them, and re-layouts  1.88 us (2%)
    pallas_call x1, Pallas kernels, rest_call(): pl.pallas_call(functools.partial(rest_kernel, beams, parts), out_shape=(p...  41 us
    pallas_call x1, Pallas kernels, self_call(): pl.pallas_call(functools.partial(self_kernel, layer, beams), out_shape=(j...  18.8 us
    pallas_call x1, Pallas kernels, write_call(): pl.pallas_call(functools.partial(write_kernel, layer, beams), out_shape=(...  9.14 us
    ppermute x5, starting transfers between devices, hop(): return lax.ppermute(x, 'tp', [(i, i ^ flip) for i in range(4)])  5.28 us
  transfers between devices with their start and end apart: 5, of which 0 were waited for; matrix products, arithmetic and copies ran while one was open for 1% of the time, Pallas kernels for 36%

profile of v4, /device:TPU:0, one launch (start us, length us, event | category | flops | bytes accessed | tf_op | source)
XLA Modules:
  0.0 77.6 jit_solution(10886939601216551596)
XLA Ops:
  0.6 3.4 %collective-permute-start = (bf16[2,192,768]{2,1,0:T(8,128)(2,1)}, bf16[2,192,768]{2,1,0:T(8,128)(2,1)S(1)}, u32[]{:S(2)}, u32[]{:S(2)}) collective-permute-start(bf16[2,192,768]{2,1,0:T(8,128)(2,1)} %wo_hbm.1), channel_id=1, source_target_pairs={{0,2},{1,3},{2,0},{3,1},{4,6},{5,7},{6,4},{7,5}} | collective-permute-start | bytes 1769480 | tf_op jit(solution)/shard_map/ppermute | solution.py:511
  4.0 1.0 %slice_bitcast_fusion = bf16[192,768]{1,0:T(8,128)(2,1)S(1)} fusion(bf16[2,192,768]{2,1,0:T(8,128)(2,1)} %wco_hbm.1), kind=kLoop, calls=%fused_computation | loop fusion | bytes 589824 | tf_op jit(solution)/shard_map/squeeze | solution.py:513
  5.0 0.0 collective-permute-start.1
  5.0 18.8 %self_0.1 = (bf16[60,192]{1,0:T(8,128)(2,1)}, bf16[2,60,192,448]{3,2,1,0:T(8,128)(2,1)}, bf16[2,60,192,448]{3,2,1,0:T(8,128)(2,1)}) custom-call(bf16[60,768]{1,0:T(8,128)(2,1)} %h_hbm.3, s32[60]{0:T(128)} %pos_ref.5, bf16[3,2,768]{2,1,0:T(2,128)(2,1)} %bitcast.41, bf16[3,2,768]{2,1,0:T(2,128)(2,1)} %bitcast.43, bf16[2,192,768]{2,1,0:T(8,128)(2,1)} %bitcast.34, ...), custom_call_target="tpu_custom_call" | custom-call | bytes 41287680 | tf_op jit(solution)/shard_map/self_0/pallas_call | solution.py:156
  23.9 0.0 collective-permute-done.1.wco_far
  23.9 0.0 copy-start.2
  23.9 0.0 collective-permute-done.wo_far
  23.9 0.0 copy-start.1
  23.9 0.7 copy-done.2
  24.6 0.2 copy-done.1
  24.8 0.0 copy-start.3
  24.8 0.0 copy-start
  24.8 41.0 %rest.1 = (bf16[60,768]{1,0:T(8,128)(2,1)S(1)}, bf16[60,768]{1,0:T(8,128)(2,1)S(1)}, bf16[60,192,448]{2,1,0:T(8,128)(2,1)S(1)}, bf16[60,192,448]{2,1,0:T(8,128)(...) custom-call(bf16[60,192]{1,0:T(8,128)(2,1)} %get-tuple-element.14.o_hbm, ...), custom_call_target="tpu_custom_call" | custom-call | tf_op jit(solution)/shard_map/rest/pallas_call | solution.py:418
  65.8 1.2 %collective-permute-start.4 = (bf16[60,768]{1,0:T(8,128)(2,1)S(1)}, bf16[60,768]{1,0:T(8,128)(2,1)S(1)}, u32[]{:S(2)}, u32[]{:S(2)}) collective-permute-start(bf16[60,768]{1,0:T(8,128)(2,1)S(1)} %get-tuple-element.16), channel_id=1, source_target_pairs={{0,3},{1,2},{2,1},{3,0},{4,7},{5,6},{6,5},{7,4}} | collective-permute-start | bytes 276488 | tf_op jit(solution)/shard_map/ppermute | solution.py:511
  67.0 0.6 collective-permute-start.3
  67.6 0.1 collective-permute-start.2
  67.7 0.0 copy-done.3
  67.7 0.0 copy-done
  67.7 9.1 %write.1 = (bf16[2,60,192,448]{3,2,1,0:T(8,128)(2,1)}, bf16[2,60,192,448]{3,2,1,0:T(8,128)(2,1)}, bf16[60,192,448]{2,1,0:T(8,128)(2,1)S(1)}, bf16[60,192,448]{2,1,0:T(8,128)(2,1)S(1)}) custom-call(s32[60]{0:T(128)S(1)} %copy-done, ...), custom_call_target="tpu_custom_call", output_to_operand_aliasing={{2}: (3, {}), {3}: (4, {}), {0}: (5, {}), {1}: (6, {})} | custom-call | bytes 20643840 | tf_op jit(solution)/shard_map/write/pallas_call | solution.py:476
  76.8 0.0 collective-permute-done.4
  76.9 0.0 collective-permute-done.3
  76.9 0.0 collective-permute-done.2
  76.9 0.7 add_convert_fusion
  (1 shorter events, 0.0 us)
Async XLA Ops:
  0.6 23.3 %collective-permute-start = (bf16[2,192,768]{2,1,0:T(8,128)(2,1)}, bf16[2,192,768]{2,1,0:T(8,128)(2,1)S(1)}, u32[]{:S(2)}, u32[]{:S(2)}) collective-permute-start(bf16[2,192,768]{2,1,0:T(8,128)(2,1)} %wo_hbm.1), channel_id=1, source_target_pairs={{0,2},{1,3},{2,0},{3,1},{4,6},{5,7},{6,4},{7,5}} | collective-permute-start | bytes 1769480 | tf_op jit(solution)/shard_map/ppermute | solution.py:511
  5.0 18.9 %collective-permute-start.1 = (bf16[192,768]{1,0:T(8,128)(2,1)S(1)}, bf16[192,768]{1,0:T(8,128)(2,1)S(1)}, u32[]{:S(2)}, u32[]{:S(2)}) collective-permute-start(bf16[192,768]{1,0:T(8,128)(2,1)S(1)} %slice_bitcast_fusion), channel_id=1, source_target_pairs={{0,2},{1,3},{2,0},{3,1},{4,6},{5,7},{6,4},{7,5}} | collective-permute-start | bytes 884744 | tf_op jit(solution)/shard_map/ppermute | solution.py:511
  23.9 0.7 copy-start.2
  23.9 0.9 %copy-start.1 = (bf16[2,192,768]{2,1,0:T(8,128)(2,1)}, bf16[2,192,768]{2,1,0:T(8,128)(2,1)S(1)}, u32[]{:S(2)}) copy-start(bf16[2,192,768]{2,1,0:T(8,128)(2,1)S(1)} %collective-permute-done.wo_far) | copy-start | bytes 1769476
  24.8 42.9 %copy-start.3 = (bf16[2,768]{1,0:T(2,128)(2,1)S(1)}, bf16[2,768]{1,0:T(2,128)(2,1)}, u32[]{:S(2)}) copy-start(bf16[2,768]{1,0:T(2,128)(2,1)} %b2_hbm.1) | copy-start | bytes 9220
  24.8 42.9 %copy-start = (s32[60]{0:T(128)S(1)}, s32[60]{0:T(128)}, u32[]{:S(2)}) copy-start(s32[60]{0:T(128)} %pos_ref.5) | copy-start | bytes 724
  65.8 11.1 %collective-permute-start.4 = (bf16[60,768]{1,0:T(8,128)(2,1)S(1)}, bf16[60,768]{1,0:T(8,128)(2,1)S(1)}, u32[]{:S(2)}, u32[]{:S(2)}) collective-permute-start(bf16[60,768]{1,0:T(8,128)(2,1)S(1)} %get-tuple-element.16), channel_id=1, source_target_pairs={{0,3},{1,2},{2,1},{3,0},{4,7},{5,6},{6,5},{7,4}} | collective-permute-start | bytes 276488 | tf_op jit(solution)/shard_map/ppermute | solution.py:511
  67.0 9.9 %collective-permute-start.3 = (bf16[60,768]{1,0:T(8,128)(2,1)S(1)}, bf16[60,768]{1,0:T(8,128)(2,1)S(1)}, u32[]{:S(2)}, u32[]{:S(2)}) collective-permute-start(bf16[60,768]{1,0:T(8,128)(2,1)S(1)} %get-tuple-element.16), channel_id=1, source_target_pairs={{0,2},{1,3},{2,0},{3,1},{4,6},{5,7},{6,4},{7,5}} | collective-permute-start | bytes 276488 | tf_op jit(solution)/shard_map/ppermute | solution.py:511
  67.6 9.3 %collective-permute-start.2 = (bf16[60,768]{1,0:T(8,128)(2,1)S(1)}, bf16[60,768]{1,0:T(8,128)(2,1)S(1)}, u32[]{:S(2)}, u32[]{:S(2)}) collective-permute-start(bf16[60,768]{1,0:T(8,128)(2,1)S(1)} %get-tuple-element.16), channel_id=1, source_target_pairs={{0,1},{1,0},{2,3},{3,2},{4,5},{5,4},{6,7},{7,6}} | collective-permute-start | bytes 276488 | tf_op jit(solution)/shard_map/ppermute | solution.py:511

commit v5 on v4

--- a/solution.py
+++ b/solution.py
@@ -107,28 +107,37 @@
     for c in small:
         c.wait()
     normed = layer_norm(h[...].astype(F32), g[0, layer:layer + 1, :], b[0, layer:layer + 1, :])
-    q = ((dot_nt(normed, wq[...]) + bq[layer:layer + 1, :].astype(F32)) * scale).astype(BF)
+    qs[...] = ((dot_nt(normed, wq[...]) + bq[layer:layer + 1, :].astype(F32)) * scale).astype(BF).astype(F32)
     kt[...] = as_columns((dot_nt(normed, wk[...]) * scale).astype(BF).astype(F32))
     vt[...] = as_columns((dot_nt(normed, wv[...]) + bv[layer:layer + 1, :].astype(F32)).astype(BF).astype(F32))
-    spread = (iota((rows * 8, rows), 0) // 8 == iota((rows * 8, rows), 1)).astype(F32).astype(BF)
-    q8 = dot(spread, q)
-    qs[...] = jnp.where(iota(q8.shape, 1) // 64 == iota(q8.shape, 0) % 8, q8, 0.0)
-
-    @pl.loop(0, audios // 2)
+    own = iota((8, qs.shape[1]), 1) // 64 == iota((8, qs.shape[1]), 0)
+    pairs = audios // 2
+    hold = pairs // 2
+
+    def release(pair):
+        for a in (pair * 2, pair * 2 + 1):
+            k_out(a).start()
+            v_out(a).start()
+
+    @pl.loop(0, pairs)
     def _(pair):
         group = (pair * 2, pair * 2 + 1)
         for a in group:
             k_in(a).wait()
             v_in(a).wait()
+        for a in group:
             insert_slot(((kbuf, kt), (vbuf, vt)), a * beams, beams, pos_ref[a * beams], slots)
-            k_out(a).start()
-            v_out(a).start()
+
+        @pl.when(pair >= hold)
+        def _():
+            release(pair - hold)
+
         probs = []
         for a in group:
             scores = []
             for i in range(beams):
-                r = a * beams + i
-                scores.append(dot(qs[pl.ds(pl.multiple_of(r * 8, 8), 8), :].astype(BF), kbuf[r]))
+                q = jnp.broadcast_to(qs[pl.ds(a * beams + i, 1), :], own.shape)
+                scores.append(dot(jnp.where(own, q, 0.0).astype(BF), kbuf[a * beams + i]))
             scores = jnp.concatenate(scores, axis=0)
             scores = jnp.where(iota(scores.shape, 1) <= pos_ref[a * beams], scores, -1e30)
             e = jnp.exp(scores - jnp.max(scores, axis=-1, keepdims=True))
@@ -137,8 +146,11 @@
             for i in range(beams):
                 r = a * beams + i
                 out = dot_nt(p[i * 8:i * 8 + 8].astype(BF), vbuf[r])
-                mine = iota(out.shape, 1) // 64 == iota(out.shape, 0)
-                os[pl.ds(r, 1), :] = jnp.sum(jnp.where(mine, out, 0.0), axis=0, keepdims=True)
+                os[pl.ds(r, 1), :] = jnp.sum(jnp.where(own, out, 0.0), axis=0, keepdims=True)
+
+    @pl.loop(pairs - hold, pairs)
+    def _(pair):
+        release(pair)
 
     o_ref[...] = os[...].astype(BF)
 
@@ -163,7 +175,7 @@
             pltpu.VMEM(wq.shape[1:], BF), pltpu.VMEM(wk.shape[1:], BF), pltpu.VMEM(wv.shape[1:], BF),
             pltpu.VMEM(bq.shape, BF), pltpu.VMEM(bv.shape, BF),
             pltpu.VMEM((rows, width, slots), BF), pltpu.VMEM((rows, width, slots), BF),
-            pltpu.VMEM((rows * 8, width), F32), pltpu.VMEM((width, 128), F32), pltpu.VMEM((width, 128), F32), pltpu.VMEM((rows, width), F32),
+            pltpu.VMEM((rows, width), F32), pltpu.VMEM((width, 128), F32), pltpu.VMEM((width, 128), F32), pltpu.VMEM((rows, width), F32),
             DMA((8,)), DMA((audios,)), DMA((audios,)), DMA((audios,)), DMA((audios,)),
         ],
         cost_estimate=pl.CostEstimate(flops=0, bytes_accessed=4 * k.size, transcendentals=0),
@@ -173,9 +185,9 @@
 
 
 def rest_kernel(beams, parts, o_hbm, h_hbm, pos_ref, g_hbm, b_hbm, wq_hbm, bq_hbm, wk_hbm, wv_hbm, bv_hbm, wo_hbm, bo_hbm, wc_hbm, bc_hbm, wco_hbm, bco_hbm, w1_hbm, b1_hbm, w2_hbm, b2_hbm,
-                wo_far, wco_far, sk_hbm, sv_hbm, ck_hbm, cv_hbm, part_ref, out_ref, sk, sv, kn_ref, vn_ref,
-                o, h, g, b, wq, bq, wk, wv, bv, wo, bo, wc, bc, wco, wco1, bco, w1, b1, w2, b2, ck, cv, hid, qc, oc, qs, vs, sn, os, got, snd, rcv,
-                psem, wsem, gsem, gssem, grsem, skem, svem, ckem, cvem, ssem, rsem):
+                sk_hbm, sv_hbm, ck_hbm, cv_hbm, part_ref, out_ref, sk, sv, kn_ref, vn_ref,
+                o, h, g, b, wq, bq, wk, wv, bv, wo, bo, wc, bc, wco, bco, w1, b1, w2, b2, ck, cv, hid, qr, kr, vr, os, snd, rcv,
+                psem, wsem, skem, svem, ckem, cvem, ssem, rsem):
     rows = h.shape[0]
     audios = rows // beams
     group = audios // parts
@@ -189,16 +201,13 @@
     peers = ((me + 2) % 4, (mate + 2) % 4, mate)
 
     small = copies([(o_hbm, o), (h_hbm, h), (g_hbm, g), (b_hbm, b), (bq_hbm, bq), (bv_hbm, bv), (bo_hbm, bo), (bc_hbm, bc), (bco_hbm, bco), (b1_hbm, b1), (b2_hbm, b2)], psem)
-    matrices = ((wo_hbm.at[0], wo_far.at[0], wo.at[0]), (wco_hbm.at[0], wco_far, wco.at[0]), (wo_hbm.at[1], wo_far.at[1], wo.at[1]))
-    gathered = [copies([(own, rows_of.at[0])], gsem.at[i]) for i, (own, _, rows_of) in enumerate(matrices)]
-
-    def shared(i):
-        own, far, rows_of = matrices[i]
-        return [pltpu.make_async_remote_copy(src, rows_of.at[1 + j], gssem.at[i, j], grsem.at[i, j], device_id=(dp, mate), device_id_type=MESH) for j, src in enumerate((own, far))]
-
-    first = copies([(x.at[0], y.at[0]) for x, y in ((wc_hbm, wc), (w1_hbm, w1), (w2_hbm, w2))], wsem.at[0])
-    second = copies([(x.at[1], y.at[1]) for x, y in ((wc_hbm, wc), (w1_hbm, w1), (w2_hbm, w2))]
-                    + [(wco_hbm.at[1], wco1)] + [(x.at[1], y) for x, y in ((wq_hbm, wq), (wk_hbm, wk), (wv_hbm, wv))], wsem.at[1])
+    def layer_copies(layer, arrays, sem):
+        return copies([(x.at[layer], y.at[layer]) for x, y in arrays], sem)
+
+    early = layer_copies(0, ((wo_hbm, wo),), wsem.at[0])
+    first = layer_copies(0, ((wc_hbm, wc), (wco_hbm, wco), (w1_hbm, w1), (w2_hbm, w2)), wsem.at[1])
+    second = layer_copies(1, ((wo_hbm, wo), (wc_hbm, wc), (wco_hbm, wco), (w1_hbm, w1), (w2_hbm, w2)), wsem.at[2])
+    extra = copies([(x.at[1], y) for x, y in ((wq_hbm, wq), (wk_hbm, wk), (wv_hbm, wv))], wsem.at[3])
 
     def cross_in(layer, a):
         return pltpu.make_async_copy(ck_hbm.at[layer, a], ck.at[a], ckem.at[a]), pltpu.make_async_copy(cv_hbm.at[layer, a], cv.at[a], cvem.at[a])
@@ -215,21 +224,20 @@
         for c in pair:
             c.wait()
 
+    start(early)
     start(small)
-    start(gathered[0])
     start(first[:1])
 
     @pl.loop(0, audios)
     def _(a):
         start(cross_in(0, a))
 
-    start(gathered[1])
     start(first[1:])
     barrier = pltpu.get_barrier_semaphore()
     for peer in peers:
         pl.semaphore_signal(barrier, inc=1, device_id=(dp, peer), device_id_type=MESH)
 
-    start(gathered[2])
+    start(extra)
     start(second)
 
     @pl.loop(0, audios)
@@ -237,7 +245,6 @@
         start(self_in(a))
 
     pl.semaphore_wait(barrier, 3)
-    start(shared(0))
 
     def sends(step, m):
         return [pltpu.make_async_remote_copy(snd.at[step, m], rcv.at[step, m, j], ssem.at[step, m, j], rsem.at[step, m, j], device_id=(dp, peer), device_id_type=MESH) for j, peer in enumerate(peers)]
@@ -251,19 +258,6 @@
         mine = snd[step, m].astype(F32) + rcv[step, m, 2].astype(F32)
         return mine + (rcv[step, m, 0].astype(F32) + rcv[step, m, 1].astype(F32))
 
-    def heads_sends(step, m):
-        return [pltpu.make_async_remote_copy(got.at[step, m, 3], got.at[step, m, j], ssem.at[step, m, j], rsem.at[step, m, j], device_id=(dp, peer), device_id_type=MESH) for j, peer in enumerate(peers)]
-
-    def push_heads(step, m, out):
-        got[step, m, 3] = out
-        start(heads_sends(step, m))
-
-    def project(step, m, i):
-        wait(heads_sends(step, m))
-        _, far, rows_of = matrices[i]
-        here = dot(got[step, m, 3], rows_of[0]) + dot(got[step, m, 2], rows_of[1])
-        return here + (dot(got[step, m, 0], far[...]) + dot(got[step, m, 1], rows_of[2]))
-
     def settle(m, update, bias):
         new = (hid[m].astype(F32) + update + bias.astype(F32)).astype(BF)
         hid[m] = new
@@ -278,7 +272,7 @@
     def cross_half(layer, m, wide):
         normed = layer_norm(wide, g[1, layer:layer + 1, :], b[1, layer:layer + 1, :])
         q = ((dot_nt(normed, wc[layer]) + bc[layer:layer + 1, :].astype(F32)) * scale).astype(BF)
-        qc[m] = dot(flags((group * 8, prow), lambda r, c: (r // 8 == c // beams) & (r % 8 == c % beams)), q)
+        qr[m, 0:prow, :] = q.astype(F32)
 
         @pl.loop(0, group)
         def _(n):
@@ -287,7 +281,7 @@
         own = iota((heads * 8, width), 1) // 64 == iota((heads * 8, width), 0) // 8
 
         def probs_of(n):
-            qa = jnp.concatenate([qc[m, n * 8:n * 8 + 8, :]] * heads, axis=0)
+            qa = jnp.concatenate([qr[m, n * beams:n * beams + 8, :]] * heads, axis=0)
             scores = dot(jnp.where(own, qa, 0.0).astype(BF), ck[m * group + n])
             e = jnp.exp(scores - jnp.max(scores, axis=-1, keepdims=True))
             return (e * (1.0 / jnp.sum(e, axis=-1, keepdims=True))).astype(BF)
@@ -297,7 +291,7 @@
             acc = out[0:8]
             for j in range(1, heads):
                 acc = acc + out[j * 8:j * 8 + 8]
-            oc[m, n * 8:n * 8 + 8, :] = acc
+            os[m, n * beams:(n + 1) * beams, :] = acc[0:beams]
 
         p = probs_of(0)
         for n in range(group):
@@ -309,8 +303,7 @@
             @pl.loop(0, group)
             def _(n):
                 start(cross_in(1, m * group + n))
-        cross = dot(flags((prow, group * 8), lambda r, c: (c // 8 == r // beams) & (c % 8 == r % beams)), oc[m].astype(BF)).astype(BF)
-        return cross
+        return dot(os[m].astype(BF), wco[layer])
 
     def mlp_half(layer, m, wide):
         normed = layer_norm(wide, g[2, layer:layer + 1, :], b[2, layer:layer + 1, :])
@@ -325,71 +318,69 @@
         v = (dot_nt(normed, wv[...]) + bv[1:2, :].astype(F32)).astype(BF)
         kn_ref[m] = k
         vn_ref[m] = v
-        spread = flags((prow * 8, prow), lambda r, c: r // 8 == c)
-        q8 = dot(spread, q)
-        own = iota(q8.shape, 1) // 64 == iota(q8.shape, 0) % 8
-        q8 = jnp.where(own, q8, 0.0)
-        qs[m] = q8
-        vs[m] = jnp.where(own, dot(spread, v), 0.0)
-        sn[m] = jnp.broadcast_to(jnp.sum(q8 * dot(spread, k), axis=-1, keepdims=True), sn.shape[1:])
-
-        @pl.loop(0, group // 2)
-        def _(i):
-            local = (i * 2, i * 2 + 1)
-            probs, news = [], []
-            for n in local:
-                a = m * group + n
-                wait(self_in(a))
-                pos = pos_ref[a * beams]
-                scores = []
-                for j in range(beams):
-                    row = pl.ds(pl.multiple_of((n * beams + j) * 8, 8), 8)
-                    scores.append(dot(qs[m, row, :].astype(BF), sk[a * beams + j]))
-                scores = jnp.concatenate(scores, axis=0)
-                fresh = sn[m, pl.ds(pl.multiple_of(n * beams * 8, 8), beams * 8), 0:1]
-                slot = iota(scores.shape, 1)
-                scores = jnp.where(slot < pos, scores, -1e30)
-                top = jnp.maximum(jnp.max(scores, axis=-1, keepdims=True), fresh)
-                e = jnp.where(slot < pos, jnp.exp(scores - top), 0.0)
-                e_new = jnp.exp(fresh - top)
-                inv = 1.0 / (jnp.sum(e, axis=-1, keepdims=True) + e_new)
-                probs.append(e * inv)
-                news.append((e_new * inv).astype(BF).astype(F32))
-            for n, p, p_new in zip(local, probs, news):
-                a = m * group + n
-                for j in range(beams):
-                    row = pl.ds(pl.multiple_of((n * beams + j) * 8, 8), 8)
-                    out = dot_nt(p[j * 8:j * 8 + 8].astype(BF), sv[a * beams + j])
-                    mine = iota(out.shape, 1) // 64 == iota(out.shape, 0)
-                    out = jnp.where(mine, out, 0.0) + p_new[j * 8:j * 8 + 8] * vs[m, row, :]
-                    os[m, pl.ds(n * beams + j, 1), :] = jnp.sum(out, axis=0, keepdims=True)
-
-        return os[m].astype(BF)
-
+        qr[m, 0:prow, :] = q.astype(F32)
+        kr[m] = k.astype(F32)
+        vr[m] = v.astype(F32)
+        own = iota((8, width), 1) // 64 == iota((8, width), 0)
+
+        @pl.loop(0, group)
+        def _(n):
+            wait(self_in(m * group + n))
+
+        def row(ref, r):
+            return jnp.where(own, jnp.broadcast_to(ref[m, r:r + 1, :], own.shape), 0.0)
+
+        def probs_of(n):
+            pos = pos_ref[(m * group + n) * beams]
+            scores, fresh = [], []
+            for j in range(beams):
+                r = n * beams + j
+                q8 = row(qr, r)
+                scores.append(dot(q8.astype(BF), sk[m * prow + r]))
+                fresh.append(jnp.sum(q8 * row(kr, r), axis=-1, keepdims=True))
+            scores = jnp.concatenate(scores, axis=0)
+            fresh = jnp.concatenate(fresh, axis=0)
+            old = iota(scores.shape, 1) < pos
+            scores = jnp.where(old, scores, -1e30)
+            top = jnp.maximum(jnp.max(scores, axis=-1, keepdims=True), fresh)
+            e = jnp.where(old, jnp.exp(scores - top), 0.0)
+            e_new = jnp.exp(fresh - top)
+            inv = 1.0 / (jnp.sum(e, axis=-1, keepdims=True) + e_new)
+            return (e * inv), (e_new * inv).astype(BF).astype(F32)
+
+        def mix(n, p, p_new):
+            for j in range(beams):
+                r = n * beams + j
+                out = dot_nt(p[j * 8:j * 8 + 8].astype(BF), sv[m * prow + r])
+                out = jnp.where(own, out, 0.0) + p_new[j * 8:j * 8 + 8] * row(vr, r)
+                os[m, r:r + 1, :] = jnp.sum(out, axis=0, keepdims=True)
+
+        p = probs_of(0)
+        for n in range(group):
+            p_next = probs_of(n + 1) if n + 1 < group else None
+            mix(n, *p)
+            p = p_next
+
+        return dot(os[m].astype(BF), wo[1])
+
+    wait(early)
     wait(small)
     for m in range(parts):
-        push_heads(0, m, dot(pick(m), o[...]).astype(BF))
-    start(shared(1))
-    start(shared(2))
+        push(0, m, dot(dot(pick(m), o[...]).astype(BF), wo[0]))
     for m in range(parts):
         hid[m] = dot(pick(m), h[...]).astype(BF)
-    wait(gathered[0])
-    wait(shared(0))
-    wait(first[:1])
-    for m in range(parts):
-        push_heads(1, m, cross_half(0, m, settle(m, project(0, m, 0), bo[0:1, :])))
-    wait(gathered[1])
-    wait(shared(1))
-    wait(first[1:])
-    for m in range(parts):
-        push(2, m, mlp_half(0, m, settle(m, project(1, m, 1), bco[0:1, :])))
-    wait(gathered[2])
-    wait(shared(2))
+        qr[m, prow:, :] = jnp.zeros((qr.shape[1] - prow, width), F32)
+    wait(first)
+    for m in range(parts):
+        push(1, m, cross_half(0, m, settle(m, total(0, m), bo[0:1, :])))
+    for m in range(parts):
+        push(2, m, mlp_half(0, m, settle(m, total(1, m), bco[0:1, :])))
     wait(second)
-    for m in range(parts):
-        push_heads(3, m, self_half(m, settle(m, total(2, m), b2[0:1, :])))
-    for m in range(parts):
-        push(4, m, dot(cross_half(1, m, settle(m, project(3, m, 2), bo[1:2, :])), wco1[...]))
+    wait(extra)
+    for m in range(parts):
+        push(3, m, self_half(m, settle(m, total(2, m), b2[0:1, :])))
+    for m in range(parts):
+        push(4, m, cross_half(1, m, settle(m, total(3, m), bo[1:2, :])))
     final = jnp.zeros((rows, h.shape[1]), F32)
     resid = jnp.zeros((rows, h.shape[1]), F32)
     for m in range(parts):
@@ -401,13 +392,12 @@
     out_ref[...] = resid.astype(BF)
 
 
-def rest_call(beams, parts, o, h, pos, g, b, wq, bq, wk, wv, bv, wo, bo, wc, bc, wco, bco, w1, b1, w2, b2, more, sk, sv, ck, cv):
+def rest_call(beams, parts, o, h, pos, g, b, wq, bq, wk, wv, bv, wo, bo, wc, bc, wco, bco, w1, b1, w2, b2, sk, sv, ck, cv):
     rows, dim = h.shape
     _, audios, width, frames = ck.shape
     slots = sk.shape[-1]
     prow = rows // parts
-    prows8 = prow * 8
-    args = (o, h, pos, g, b, wq, bq, wk, wv, bv, wo, bo, wc, bc, wco, bco, w1, b1, w2, b2) + more + (sk, sv, ck, cv)
+    args = (o, h, pos, g, b, wq, bq, wk, wv, bv, wo, bo, wc, bc, wco, bco, w1, b1, w2, b2, sk, sv, ck, cv)
 
     def whole(x):
         return pltpu.VMEM(x.shape, BF)
@@ -418,16 +408,14 @@
     return pl.pallas_call(
         functools.partial(rest_kernel, beams, parts),
         out_shape=(pltpu.VMEM(h.shape, BF), pltpu.VMEM(h.shape, BF), pltpu.VMEM((rows, width, slots), BF), pltpu.VMEM((rows, width, slots), BF), pltpu.VMEM((parts, prow, width), BF), pltpu.VMEM((parts, prow, width), BF)),
-        in_specs=[ANY, ANY, SMEM] + [ANY] * (len(args) - 9) + [VM, VM] + [ANY] * 4,
+        in_specs=[ANY, ANY, SMEM] + [ANY] * (len(args) - 3),
         out_specs=(VM,) * 6,
         scratch_shapes=[
-            whole(o), whole(h), whole(g), whole(b), one(wq), whole(bq), one(wk), one(wv), whole(bv), pltpu.VMEM((2, 3, width, dim), BF), whole(bo), whole(wc), whole(bc),
-            pltpu.VMEM((1, 3, width, dim), BF), one(wco), whole(bco), whole(w1), whole(b1), whole(w2), whole(b2), one(ck), one(cv),
+            whole(o), whole(h), whole(g), whole(b), one(wq), whole(bq), one(wk), one(wv), whole(bv), whole(wo), whole(bo), whole(wc), whole(bc), whole(wco), whole(bco), whole(w1), whole(b1), whole(w2), whole(b2), one(ck), one(cv),
             pltpu.VMEM((parts, prow, dim), BF),
-            pltpu.VMEM((parts, audios // parts * 8, width), F32), pltpu.VMEM((parts, audios // parts * 8, width), F32),
-            pltpu.VMEM((parts, prows8, width), F32), pltpu.VMEM((parts, prows8, width), F32), pltpu.VMEM((parts, prows8, 128), F32), pltpu.VMEM((parts, prow, width), F32),
-            pltpu.VMEM((6, parts, 4, prow, width), BF), pltpu.VMEM((6, parts, prow, dim), BF), pltpu.VMEM((6, parts, 3, prow, dim), BF),
-            DMA((11,)), DMA((2, 8)), DMA((3, 1)), DMA((3, 2)), DMA((3, 2)), DMA((audios,)), DMA((audios,)), DMA((audios,)), DMA((audios,)), DMA((6, parts, 3)), DMA((6, parts, 3)),
+            pltpu.VMEM((parts, prow + 8, width), F32), pltpu.VMEM((parts, prow, width), F32), pltpu.VMEM((parts, prow, width), F32), pltpu.VMEM((parts, prow, width), F32),
+            pltpu.VMEM((5, parts, prow, dim), BF), pltpu.VMEM((5, parts, 3, prow, dim), BF),
+            DMA((11,)), DMA((4, 8)), DMA((audios,)), DMA((audios,)), DMA((audios,)), DMA((audios,)), DMA((5, parts, 3)), DMA((5, parts, 3)),
         ],
         compiler_params=pltpu.CompilerParams(collective_id=0, has_side_effects=True, vmem_limit_bytes=REST_LIMIT),
         name="rest",
@@ -510,9 +498,8 @@
         def hop(x, flip):
             return lax.ppermute(x, 'tp', [(i, i ^ flip) for i in range(4)])
 
-        more = (hop(wo, 2), hop(wco[0], 2))
         o, ko, vo = self_call(0, beams, hidden, positions, g, b, wq, wk, wv, bq, bv, sk, sv)
-        part, hidden, sk1, sv1, kn, vn = rest_call(beams, 2, o, hidden, positions, g, b, wq, bq, wk, wv, bv, wo, bo, wc, bc, wco, bco, w1, b1, w2, b2, more, sk, sv, ck, cv)
+        part, hidden, sk1, sv1, kn, vn = rest_call(beams, 2, o, hidden, positions, g, b, wq, bq, wk, wv, bv, wo, bo, wc, bc, wco, bco, w1, b1, w2, b2, sk, sv, ck, cv)
         ko, vo = write_call(1, beams, positions, kn, vn, sk1, sv1, ko, vo)
         here, mate, far, diag = (x.astype(F32) for x in (part, hop(part, 1), hop(part, 2), hop(part, 3)))
         hidden = (hidden.astype(F32) + ((here + mate) + (far + diag)) + b2[1].astype(F32)).astype(BF)

time: 77.8 us -> 72.6 us (0.933)
  starting transfers between devices: 5.28 us -> 2 us
  local copies, waits for them, and re-layouts: 1.88 us -> 0.01 us
    ppermute x5 -> x3, starting transfers between devices: 5.28 us -> 2 us  [hop(): return lax.ppermute(x, 'tp', [(i, i ^ flip) for i in range(4)])]
    pallas_call x1, Pallas kernels: 41 us -> 42.5 us  [rest_call(): pl.pallas_call(functools.partial(rest_kernel, beams, parts), out_shape=(p...]
    pallas_call x1, Pallas kernels: 18.8 us -> 17.3 us  [self_call(): pl.pallas_call(functools.partial(self_kernel, layer, beams), out_shape=(j...]
    squeeze x1 -> x0, local copies, waits for them, and re-layouts: 0.98 us -> none  [local_step(): more = (hop(wo, 2), hop(wco[0], 2))]
    unnamed x8 -> x4, local copies, waits for them, and re-layouts: 0.9 us -> 0.01 us
  transfers between devices with their start and end apart: 5 -> 3, of which waited for: 0 -> 0; matrix products, arithmetic and copies ran while one was open for 1% -> 0% of each run, Pallas kernels for 36% -> 13%
where the time goes in v5:
time: 72.6 us; the launch traced here: 72.4 us
  Pallas kernels  69 us (95%)
  starting transfers between devices  2 us (3%)
  other arithmetic  0.74 us (1%)
    pallas_call x1, Pallas kernels, rest_call(): pl.pallas_call(functools.partial(rest_kernel, beams, parts), out_shape=(p...  42.5 us
    pallas_call x1, Pallas kernels, self_call(): pl.pallas_call(functools.partial(self_kernel, layer, beams), out_shape=(j...  17.3 us
    pallas_call x1, Pallas kernels, write_call(): pl.pallas_call(functools.partial(write_kernel, layer, beams), out_shape=(...  9.14 us
    ppermute x3, starting transfers between devices, hop(): return lax.ppermute(x, 'tp', [(i, i ^ flip) for i in range(4)])  2 us
  transfers between devices with their start and end apart: 3, of which 0 were waited for; matrix products, arithmetic and copies ran while one was open for 0% of the time, Pallas kernels for 13%

profile of v5, /device:TPU:0, one launch (start us, length us, event | category | flops | bytes accessed | tf_op | source)
XLA Modules:
  0.0 72.4 jit_solution(3034456749390828712)
XLA Ops:
  0.6 17.3 %self_0.1 = (bf16[60,192]{1,0:T(8,128)(2,1)}, bf16[2,60,192,448]{3,2,1,0:T(8,128)(2,1)}, bf16[2,60,192,448]{3,2,1,0:T(8,128)(2,1)}) custom-call(bf16[60,768]{1,0:T(8,128)(2,1)} %h_hbm.3, s32[60]{0:T(128)} %pos_ref.5, bf16[3,2,768]{2,1,0:T(2,128)(2,1)} %bitcast.39, bf16[3,2,768]{2,1,0:T(2,128)(2,1)} %bitcast.41, bf16[2,192,768]{2,1,0:T(8,128)(2,1)} %bitcast.32, ...), custom_call_target="tpu_custom_call" | custom-call | bytes 41287680 | tf_op jit(solution)/shard_map/self_0/pallas_call | solution.py:168
  18.0 0.0 copy-start
  18.0 42.5 %rest.1 = (bf16[60,768]{1,0:T(8,128)(2,1)S(1)}, bf16[60,768]{1,0:T(8,128)(2,1)S(1)}, bf16[60,192,448]{2,1,0:T(8,128)(2,1)S(1)}, bf16[60,192,448]{2,1,0:T(8,128)(...) custom-call(bf16[60,192]{1,0:T(8,128)(2,1)} %get-tuple-element.14.o_hbm, ...), custom_call_target="tpu_custom_call" | custom-call | tf_op jit(solution)/shard_map/rest/pallas_call | solution.py:408
  60.5 0.1 collective-permute-start.2
  60.6 1.9 %collective-permute-start.1 = (bf16[60,768]{1,0:T(8,128)(2,1)S(1)}, bf16[60,768]{1,0:T(8,128)(2,1)S(1)}, u32[]{:S(2)}, u32[]{:S(2)}) collective-permute-start(bf16[60,768]{1,0:T(8,128)(2,1)S(1)} %get-tuple-element.16), channel_id=1, source_target_pairs={{0,2},{1,3},{2,0},{3,1},{4,6},{5,7},{6,4},{7,5}} | collective-permute-start | bytes 276488 | tf_op jit(solution)/shard_map/ppermute | solution.py:499
  62.5 0.0 collective-permute-start
  62.5 0.0 copy-done
  62.5 0.0 copy-start.1
  62.5 9.1 %write.1 = (bf16[2,60,192,448]{3,2,1,0:T(8,128)(2,1)}, bf16[2,60,192,448]{3,2,1,0:T(8,128)(2,1)}, bf16[60,192,448]{2,1,0:T(8,128)(2,1)S(1)}, bf16[60,192,448]{2,1,0:T(8,128)(2,1)S(1)}) custom-call(s32[60]{0:T(128)S(1)} %copy-done, ...), custom_call_target="tpu_custom_call", output_to_operand_aliasing={{2}: (3, {}), {3}: (4, {}), {0}: (5, {}), {1}: (6, {})} | custom-call | bytes 20643840 | tf_op jit(solution)/shard_map/write/pallas_call | solution.py:464
  71.6 0.0 copy-done.1
  71.7 0.0 collective-permute-done.2
  71.7 0.0 collective-permute-done.1
  71.7 0.0 collective-permute-done
  71.7 0.7 add_convert_fusion
  (1 shorter events, 0.0 us)
Async XLA Ops:
  18.0 44.5 %copy-start = (s32[60]{0:T(128)S(1)}, s32[60]{0:T(128)}, u32[]{:S(2)}) copy-start(s32[60]{0:T(128)} %pos_ref.5) | copy-start | bytes 724
  60.5 11.2 %collective-permute-start.2 = (bf16[60,768]{1,0:T(8,128)(2,1)S(1)}, bf16[60,768]{1,0:T(8,128)(2,1)S(1)}, u32[]{:S(2)}, u32[]{:S(2)}) collective-permute-start(bf16[60,768]{1,0:T(8,128)(2,1)S(1)} %get-tuple-element.16), channel_id=1, source_target_pairs={{0,3},{1,2},{2,1},{3,0},{4,7},{5,6},{6,5},{7,4}} | collective-permute-start | bytes 276488 | tf_op jit(solution)/shard_map/ppermute | solution.py:499
  60.6 11.1 %collective-permute-start.1 = (bf16[60,768]{1,0:T(8,128)(2,1)S(1)}, bf16[60,768]{1,0:T(8,128)(2,1)S(1)}, u32[]{:S(2)}, u32[]{:S(2)}) collective-permute-start(bf16[60,768]{1,0:T(8,128)(2,1)S(1)} %get-tuple-element.16), channel_id=1, source_target_pairs={{0,2},{1,3},{2,0},{3,1},{4,6},{5,7},{6,4},{7,5}} | collective-permute-start | bytes 276488 | tf_op jit(solution)/shard_map/ppermute | solution.py:499
  62.5 9.2 %collective-permute-start = (bf16[60,768]{1,0:T(8,128)(2,1)S(1)}, bf16[60,768]{1,0:T(8,128)(2,1)S(1)}, u32[]{:S(2)}, u32[]{:S(2)}) collective-permute-start(bf16[60,768]{1,0:T(8,128)(2,1)S(1)} %get-tuple-element.16), channel_id=1, source_target_pairs={{0,1},{1,0},{2,3},{3,2},{4,5},{5,4},{6,7},{7,6}} | collective-permute-start | bytes 276488 | tf_op jit(solution)/shard_map/ppermute | solution.py:499
  62.5 9.2 %copy-start.1 = (bf16[2,768]{1,0:T(2,128)(2,1)S(1)}, bf16[2,768]{1,0:T(2,128)(2,1)}, u32[]{:S(2)}) copy-start(bf16[2,768]{1,0:T(2,128)(2,1)} %b2_hbm.1) | copy-start | bytes 9220

commit v6 on v5

--- a/solution.py
+++ b/solution.py
@@ -70,14 +70,14 @@
     return [pltpu.make_async_copy(s, d, sem.at[i]) for i, (s, d) in enumerate(pairs)]
 
 
-def self_kernel(layer, beams, h_hbm, pos_ref, g_hbm, b_hbm, wq_hbm, wk_hbm, wv_hbm, bq_hbm, bv_hbm, k_hbm, v_hbm, o_ref, ko_hbm, vo_hbm,
-                h, g, b, wq, wk, wv, bq, bv, kbuf, vbuf, qs, kt, vt, os, psem, ksem, vsem, kosem, vosem):
+def self_kernel(layer, beams, h_hbm, pos_hbm, g_hbm, b_hbm, wq_hbm, wk_hbm, wv_hbm, bq_hbm, bv_hbm, k_hbm, v_hbm, o_hbm, ko_hbm, vo_hbm,
+                h, pos_ref, g, b, wq, wk, wv, bq, bv, kbuf, vbuf, qs, kt, vt, os, o, psem, ksem, vsem, kosem, vosem):
     rows = h.shape[0]
     audios = rows // beams
     slots = kbuf.shape[-1]
     scale = 64 ** -0.25
 
-    small = copies([(h_hbm, h), (g_hbm, g), (b_hbm, b), (wq_hbm.at[layer], wq), (wk_hbm.at[layer], wk), (wv_hbm.at[layer], wv), (bq_hbm, bq), (bv_hbm, bv)], psem)
+    small = copies([(h_hbm, h), (g_hbm, g), (b_hbm, b), (wq_hbm.at[layer], wq), (wk_hbm.at[layer], wk), (wv_hbm.at[layer], wv), (bq_hbm, bq), (bv_hbm, bv), (pos_hbm, pos_ref)], psem)
     for c in small:
         c.start()
 
@@ -152,12 +152,16 @@
     def _(pair):
         release(pair)
 
-    o_ref[...] = os[...].astype(BF)
+    o[...] = os[...].astype(BF)
+    last = pltpu.make_async_copy(o, o_hbm, psem.at[0])
+    last.start()
 
     @pl.loop(0, audios)
     def _(a):
         k_out(a).wait()
         v_out(a).wait()
+
+    last.wait()
 
 
 def self_call(layer, beams, h, pos, g, b, wq, wk, wv, bq, bv, k, v):
@@ -168,15 +172,15 @@
     return pl.pallas_call(
         functools.partial(self_kernel, layer, beams),
         out_shape=(jax.ShapeDtypeStruct((rows, width), BF), jax.ShapeDtypeStruct(k.shape, BF), jax.ShapeDtypeStruct(v.shape, BF)),
-        in_specs=[ANY, SMEM] + [ANY] * 9,
-        out_specs=(VM, ANY, ANY),
+        in_specs=[ANY] * 11,
+        out_specs=(ANY, ANY, ANY),
         scratch_shapes=[
-            pltpu.VMEM(h.shape, BF), pltpu.VMEM(g.shape, BF), pltpu.VMEM(b.shape, BF),
+            pltpu.VMEM(h.shape, BF), pltpu.SMEM(pos.shape, jnp.int32), pltpu.VMEM(g.shape, BF), pltpu.VMEM(b.shape, BF),
             pltpu.VMEM(wq.shape[1:], BF), pltpu.VMEM(wk.shape[1:], BF), pltpu.VMEM(wv.shape[1:], BF),
             pltpu.VMEM(bq.shape, BF), pltpu.VMEM(bv.shape, BF),
             pltpu.VMEM((rows, width, slots), BF), pltpu.VMEM((rows, width, slots), BF),
-            pltpu.VMEM((rows, width), F32), pltpu.VMEM((width, 128), F32), pltpu.VMEM((width, 128), F32), pltpu.VMEM((rows, width), F32),
-            DMA((8,)), DMA((audios,)), DMA((audios,)), DMA((audios,)), DMA((audios,)),
+            pltpu.VMEM((rows, width), F32), pltpu.VMEM((width, 128), F32), pltpu.VMEM((width, 128), F32), pltpu.VMEM((rows, width), F32), pltpu.VMEM((rows, width), BF),
+            DMA((9,)), DMA((audios,)), DMA((audios,)), DMA((audios,)), DMA((audios,)),
         ],
         cost_estimate=pl.CostEstimate(flops=0, bytes_accessed=4 * k.size, transcendentals=0),
         compiler_params=pltpu.CompilerParams(vmem_limit_bytes=VMEM_LIMIT),
@@ -184,9 +188,9 @@
     )(*args)
 
 
-def rest_kernel(beams, parts, o_hbm, h_hbm, pos_ref, g_hbm, b_hbm, wq_hbm, bq_hbm, wk_hbm, wv_hbm, bv_hbm, wo_hbm, bo_hbm, wc_hbm, bc_hbm, wco_hbm, bco_hbm, w1_hbm, b1_hbm, w2_hbm, b2_hbm,
-                sk_hbm, sv_hbm, ck_hbm, cv_hbm, part_ref, out_ref, sk, sv, kn_ref, vn_ref,
-                o, h, g, b, wq, bq, wk, wv, bv, wo, bo, wc, bc, wco, bco, w1, b1, w2, b2, ck, cv, hid, qr, kr, vr, os, snd, rcv,
+def rest_kernel(beams, parts, o_hbm, h_hbm, pos_hbm, g_hbm, b_hbm, wq_hbm, bq_hbm, wk_hbm, wv_hbm, bv_hbm, wo_hbm, bo_hbm, wc_hbm, bc_hbm, wco_hbm, bco_hbm, w1_hbm, b1_hbm, w2_hbm, b2_hbm,
+                sk_hbm, sv_hbm, ck_hbm, cv_hbm, part_ref, out_ref, sk, sv, kt, vt, spot,
+                o, h, pos_ref, g, b, wq, bq, wk, wv, bv, wo, bo, wc, bc, wco, bco, w1, b1, w2, b2, ck, cv, hid, qr, kr, vr, kall, vall, os, snd, rcv,
                 psem, wsem, skem, svem, ckem, cvem, ssem, rsem):
     rows = h.shape[0]
     audios = rows // beams
@@ -200,7 +204,7 @@
     mate = me + 1 - 2 * (me % 2)
     peers = ((me + 2) % 4, (mate + 2) % 4, mate)
 
-    small = copies([(o_hbm, o), (h_hbm, h), (g_hbm, g), (b_hbm, b), (bq_hbm, bq), (bv_hbm, bv), (bo_hbm, bo), (bc_hbm, bc), (bco_hbm, bco), (b1_hbm, b1), (b2_hbm, b2)], psem)
+    small = copies([(o_hbm, o), (h_hbm, h), (g_hbm, g), (b_hbm, b), (bq_hbm, bq), (bv_hbm, bv), (bo_hbm, bo), (bc_hbm, bc), (bco_hbm, bco), (b1_hbm, b1), (b2_hbm, b2), (pos_hbm, pos_ref)], psem)
     def layer_copies(layer, arrays, sem):
         return copies([(x.at[layer], y.at[layer]) for x, y in arrays], sem)
 
@@ -316,8 +320,8 @@
         q = ((dot_nt(normed, wq[...]) + bq[1:2, :].astype(F32)) * scale).astype(BF)
         k = (dot_nt(normed, wk[...]) * scale).astype(BF)
         v = (dot_nt(normed, wv[...]) + bv[1:2, :].astype(F32)).astype(BF)
-        kn_ref[m] = k
-        vn_ref[m] = v
+        kall[m * prow:(m + 1) * prow, :] = k.astype(F32)
+        vall[m * prow:(m + 1) * prow, :] = v.astype(F32)
         qr[m, 0:prow, :] = q.astype(F32)
         kr[m] = k.astype(F32)
         vr[m] = v.astype(F32)
@@ -370,6 +374,8 @@
     for m in range(parts):
         hid[m] = dot(pick(m), h[...]).astype(BF)
         qr[m, prow:, :] = jnp.zeros((qr.shape[1] - prow, width), F32)
+    kall[rows:, :] = jnp.zeros((128 - rows, width), F32)
+    vall[rows:, :] = jnp.zeros((128 - rows, width), F32)
     wait(first)
     for m in range(parts):
         push(1, m, cross_half(0, m, settle(m, total(0, m), bo[0:1, :])))
@@ -379,6 +385,10 @@
     wait(extra)
     for m in range(parts):
         push(3, m, self_half(m, settle(m, total(2, m), b2[0:1, :])))
+    kt[...] = kall[...].T
+    vt[...] = vall[...].T
+    for a in range(audios):
+        spot[a] = jnp.full(spot.shape[1:], pos_ref[a * beams], jnp.int32)
     for m in range(parts):
         push(4, m, cross_half(1, m, settle(m, total(3, m), bo[1:2, :])))
     final = jnp.zeros((rows, h.shape[1]), F32)
@@ -407,26 +417,25 @@
 
     return pl.pallas_call(
         functools.partial(rest_kernel, beams, parts),
-        out_shape=(pltpu.VMEM(h.shape, BF), pltpu.VMEM(h.shape, BF), pltpu.VMEM((rows, width, slots), BF), pltpu.VMEM((rows, width, slots), BF), pltpu.VMEM((parts, prow, width), BF), pltpu.VMEM((parts, prow, width), BF)),
-        in_specs=[ANY, ANY, SMEM] + [ANY] * (len(args) - 3),
-        out_specs=(VM,) * 6,
+        out_shape=(pltpu.VMEM(h.shape, BF), pltpu.VMEM(h.shape, BF), pltpu.VMEM((rows, width, slots), BF), pltpu.VMEM((rows, width, slots), BF), pltpu.VMEM((width, 128), F32), pltpu.VMEM((width, 128), F32), pltpu.VMEM((audios, 8, 128), jnp.int32)),
+        in_specs=[ANY] * len(args),
+        out_specs=(VM,) * 7,
         scratch_shapes=[
-            whole(o), whole(h), whole(g), whole(b), one(wq), whole(bq), one(wk), one(wv), whole(bv), whole(wo), whole(bo), whole(wc), whole(bc), whole(wco), whole(bco), whole(w1), whole(b1), whole(w2), whole(b2), one(ck), one(cv),
+            whole(o), whole(h), pltpu.SMEM(pos.shape, jnp.int32), whole(g), whole(b), one(wq), whole(bq), one(wk), one(wv), whole(bv), whole(wo), whole(bo), whole(wc), whole(bc), whole(wco), whole(bco), whole(w1), whole(b1), whole(w2), whole(b2), one(ck), one(cv),
             pltpu.VMEM((parts, prow, dim), BF),
-            pltpu.VMEM((parts, prow + 8, width), F32), pltpu.VMEM((parts, prow, width), F32), pltpu.VMEM((parts, prow, width), F32), pltpu.VMEM((parts, prow, width), F32),
+            pltpu.VMEM((parts, prow + 8, width), F32), pltpu.VMEM((parts, prow, width), F32), pltpu.VMEM((parts, prow, width), F32),
+            pltpu.VMEM((128, width), F32), pltpu.VMEM((128, width), F32), pltpu.VMEM((parts, prow, width), F32),
             pltpu.VMEM((5, parts, prow, dim), BF), pltpu.VMEM((5, parts, 3, prow, dim), BF),
-            DMA((11,)), DMA((4, 8)), DMA((audios,)), DMA((audios,)), DMA((audios,)), DMA((audios,)), DMA((5, parts, 3)), DMA((5, parts, 3)),
+            DMA((12,)), DMA((4, 8)), DMA((audios,)), DMA((audios,)), DMA((audios,)), DMA((audios,)), DMA((5, parts, 3)), DMA((5, parts, 3)),
         ],
         compiler_params=pltpu.CompilerParams(collective_id=0, has_side_effects=True, vmem_limit_bytes=REST_LIMIT),
         name="rest",
     )(*args)
 
 
-def write_kernel(layer, beams, pos_ref, kn, vn, sk_in, sv_in, ki_hbm, vi_hbm, ko_hbm, vo_hbm, sk, sv, kt, vt, kosem, vosem):
-    parts, prow, width = kn.shape
-    rows = parts * prow
+def write_kernel(layer, beams, spot, kt, vt, sk_in, sv_in, ki_hbm, vi_hbm, ko_hbm, vo_hbm, sk, sv, kosem, vosem):
+    rows, width, slots = sk.shape
     audios = rows // beams
-    slots = sk.shape[-1]
 
     def k_out(a):
         r = pl.ds(a * beams, beams)
@@ -436,21 +445,18 @@
         r = pl.ds(a * beams, beams)
         return pltpu.make_async_copy(sv.at[r], vo_hbm.at[layer, r], vosem.at[a])
 
-    def columns(new):
-        both = jnp.zeros((rows, width), F32)
-        for m in range(parts):
-            place = (iota((rows, prow), 0) == iota((rows, prow), 1) + m * prow).astype(F32).astype(BF)
-            both = both + dot(place, new[m])
-        return as_columns(both)
-
-    kt[...] = columns(kn)
-    vt[...] = columns(vn)
-
     @pl.loop(0, audios)
     def _(a):
-        insert_slot(((sk, kt), (sv, vt)), a * beams, beams, pos_ref[a * beams], slots)
-        k_out(a).start()
-        v_out(a).start()
+        hits = [iota((width, min(128, slots - t)), 1) + t == spot[a, 0:1, :min(128, slots - t)] for t in range(0, slots, 128)]
+        for buf, cols, out in ((sk, kt, k_out), (sv, vt, v_out)):
+            for i in range(beams):
+                r = a * beams + i
+                col = jnp.take_along_axis(cols[...], jnp.full((width, 128), r, jnp.int32), axis=1).astype(BF)
+                for n, hit in enumerate(hits):
+                    size = hit.shape[1]
+                    span = (r, slice(None), slice(n * 128, n * 128 + size))
+                    buf[span] = jnp.where(hit, col[:, :size], buf[span])
+            out(a).start()
 
     @pl.loop(0, audios)
     def _(a):
@@ -458,20 +464,19 @@
         v_out(a).wait()
 
 
-def write_call(layer, beams, pos, kn, vn, sk, sv, ko, vo):
-    rows, width, slots = sk.shape
-    audios = rows // beams
+def write_call(layer, beams, spot, kt, vt, sk, sv, ko, vo):
+    audios = sk.shape[0] // beams
     return pl.pallas_call(
         functools.partial(write_kernel, layer, beams),
         out_shape=(jax.ShapeDtypeStruct(ko.shape, BF), jax.ShapeDtypeStruct(vo.shape, BF), pltpu.VMEM(sk.shape, BF), pltpu.VMEM(sv.shape, BF)),
-        in_specs=[SMEM, VM, VM, VM, VM, ANY, ANY],
+        in_specs=[VM, VM, VM, VM, VM, ANY, ANY],
         out_specs=(ANY, ANY, VM, VM),
         input_output_aliases={3: 2, 4: 3, 5: 0, 6: 1},
         cost_estimate=pl.CostEstimate(flops=0, bytes_accessed=4 * sk.size, transcendentals=0),
-        scratch_shapes=[pltpu.VMEM((width, 128), F32), pltpu.VMEM((width, 128), F32), DMA((audios,)), DMA((audios,))],
+        scratch_shapes=[DMA((audios,)), DMA((audios,))],
         compiler_params=pltpu.CompilerParams(vmem_limit_bytes=4 * 1024 * 1024),
         name="write",
-    )(pos, kn, vn, sk, sv, ko, vo)[:2]
+    )(spot, kt, vt, sk, sv, ko, vo)[:2]
 
 
 def solution(mesh):
@@ -499,8 +504,8 @@
             return lax.ppermute(x, 'tp', [(i, i ^ flip) for i in range(4)])
 
         o, ko, vo = self_call(0, beams, hidden, positions, g, b, wq, wk, wv, bq, bv, sk, sv)
-        part, hidden, sk1, sv1, kn, vn = rest_call(beams, 2, o, hidden, positions, g, b, wq, bq, wk, wv, bv, wo, bo, wc, bc, wco, bco, w1, b1, w2, b2, sk, sv, ck, cv)
-        ko, vo = write_call(1, beams, positions, kn, vn, sk1, sv1, ko, vo)
+        part, hidden, sk1, sv1, kt, vt, spot = rest_call(beams, 3, o, hidden, positions, g, b, wq, bq, wk, wv, bv, wo, bo, wc, bc, wco, bco, w1, b1, w2, b2, sk, sv, ck, cv)
+        ko, vo = write_call(1, beams, spot, kt, vt, sk1, sv1, ko, vo)
         here, mate, far, diag = (x.astype(F32) for x in (part, hop(part, 1), hop(part, 2), hop(part, 3)))
         hidden = (hidden.astype(F32) + ((here + mate) + (far + diag)) + b2[1].astype(F32)).astype(BF)
         return hidden, heads_last(ko, self_keys), heads_last(vo, self_vals)

time: 72.6 us -> 70.8 us (0.975)
  Pallas kernels: 69 us -> 66.6 us
  starting transfers between devices: 2 us -> 2.73 us
    pallas_call x1, Pallas kernels: 17.3 us -> 16.1 us  [self_call(): pl.pallas_call(functools.partial(self_kernel, layer, beams), out_shape=(j...]
    pallas_call x1, Pallas kernels: 9.14 us -> 8.4 us  [write_call(): pl.pallas_call(functools.partial(write_kernel, layer, beams), out_shape=(...]
    ppermute x3, starting transfers between devices: 2 us -> 2.73 us  [hop(): return lax.ppermute(x, 'tp', [(i, i ^ flip) for i in range(4)])]
  transfers between devices with their start and end apart: 3 -> 3, of which waited for: 0 -> 0; matrix products, arithmetic and copies ran while one was open for 0% -> 0% of each run, Pallas kernels for 13% -> 12%
where the time goes in v6:
time: 70.8 us; the launch traced here: 70.7 us
  Pallas kernels  66.6 us (94%)
  starting transfers between devices  2.73 us (4%)
  other arithmetic  0.74 us (1%)
    pallas_call x1, Pallas kernels, rest_call(): pl.pallas_call(functools.partial(rest_kernel, beams, parts), out_shape=(p...  42.1 us
    pallas_call x1, Pallas kernels, self_call(): pl.pallas_call(functools.partial(self_kernel, layer, beams), out_shape=(j...  16.1 us
    pallas_call x1, Pallas kernels, write_call(): pl.pallas_call(functools.partial(write_kernel, layer, beams), out_shape=(...  8.4 us
    ppermute x3, starting transfers between devices, hop(): return lax.ppermute(x, 'tp', [(i, i ^ flip) for i in range(4)])  2.73 us
  transfers between devices with their start and end apart: 3, of which 0 were waited for; matrix products, arithmetic and copies ran while one was open for 0% of the time, Pallas kernels for 12%

profile of v6, /device:TPU:0, one launch (start us, length us, event | category | flops | bytes accessed | tf_op | source)
XLA Modules:
  0.0 70.7 jit_solution(13124623189254978664)
XLA Ops:
  0.6 16.1 %self_0.1 = (bf16[60,192]{1,0:T(8,128)(2,1)}, bf16[2,60,192,448]{3,2,1,0:T(8,128)(2,1)}, bf16[2,60,192,448]{3,2,1,0:T(8,128)(2,1)}) custom-call(bf16[60,768]{1,0:T(8,128)(2,1)} %h_hbm.3, s32[60]{0:T(128)} %pos_hbm.3, bf16[3,2,768]{2,1,0:T(2,128)(2,1)} %bitcast.39, bf16[3,2,768]{2,1,0:T(2,128)(2,1)} %bitcast.41, bf16[2,192,768]{2,1,0:T(8,128)(2,1)} %bitcast.32, ...), custom_call_target="tpu_custom_call" | custom-call | bytes 41287680 | tf_op jit(solution)/shard_map/self_0/pallas_call | solution.py:172
  16.7 42.1 %rest.1 = (bf16[60,768]{1,0:T(8,128)(2,1)S(1)}, bf16[60,768]{1,0:T(8,128)(2,1)S(1)}, bf16[60,192,448]{2,1,0:T(8,128)(2,1)S(1)}, bf16[60,192,448]{2,1,0:T(8,128)(...) custom-call(bf16[60,192]{1,0:T(8,128)(2,1)} %get-tuple-element.15.o_hbm, ...), custom_call_target="tpu_custom_call" | custom-call | tf_op jit(solution)/shard_map/rest/pallas_call | solution.py:418
  58.8 2.2 %collective-permute-start.2 = (bf16[60,768]{1,0:T(8,128)(2,1)S(1)}, bf16[60,768]{1,0:T(8,128)(2,1)S(1)}, u32[]{:S(2)}, u32[]{:S(2)}) collective-permute-start(bf16[60,768]{1,0:T(8,128)(2,1)S(1)} %get-tuple-element.17), channel_id=1, source_target_pairs={{0,3},{1,2},{2,1},{3,0},{4,7},{5,6},{6,5},{7,4}} | collective-permute-start | bytes 276488 | tf_op jit(solution)/shard_map/ppermute | solution.py:504
  61.1 0.4 collective-permute-start.1
  61.5 0.1 collective-permute-start
  61.5 0.0 copy-start
  61.6 8.4 %write.1 = (bf16[2,60,192,448]{3,2,1,0:T(8,128)(2,1)}, bf16[2,60,192,448]{3,2,1,0:T(8,128)(2,1)}, bf16[60,192,448]{2,1,0:T(8,128)(2,1)S(1)}, bf16[60,192,448]{2,1,0:T(8,128)(2,1)S(1)}) custom-call(s32[12,8,128]{2,1,0:T(8,128)S(1)} %get-tuple-element.18.spot, ...), custom_call_target="tpu_custom_call", output_to_operand_aliasing={{2}: (3, {}), {3}: (4, {}), {0}: (5, {}), {1}: (6, {})} | custom-call | bytes 20643840 | tf_op jit(solution)/shard_map/write/pallas_call | solution.py:469
  70.0 0.0 copy-done
  70.0 0.0 collective-permute-done.2
  70.0 0.0 collective-permute-done.1
  70.0 0.0 collective-permute-done
  70.0 0.7 %add_convert_fusion = bf16[60,768]{1,0:T(8,128)(2,1)} fusion(bf16[60,768]{1,0:T(8,128)(2,1)S(1)} %collective-permute-done.2, bf16[60,768]{1,0:T(8,128)(2,1)S(1)} %collective-permute-done.1, bf16[60,768]{1,0:T(8,128)(2,1)S(1)} %collective-permute-done, bf16[60,768]{1,0:T(8,128)(2,1)S(1)} %get-tuple-element.17, bf16[60,768]{1,0:T(8,128)(2,1)S(1)} %get-tuple-element.16, ...), kind=kLoop, calls=%fused_computation | loop fusion | flops 506880 | bytes 556032 | tf_op jit(solution)/shard_map/convert_element_type | solution.py:510
  (1 shorter events, 0.0 us)
Async XLA Ops:
  58.8 11.2 %collective-permute-start.2 = (bf16[60,768]{1,0:T(8,128)(2,1)S(1)}, bf16[60,768]{1,0:T(8,128)(2,1)S(1)}, u32[]{:S(2)}, u32[]{:S(2)}) collective-permute-start(bf16[60,768]{1,0:T(8,128)(2,1)S(1)} %get-tuple-element.17), channel_id=1, source_target_pairs={{0,3},{1,2},{2,1},{3,0},{4,7},{5,6},{6,5},{7,4}} | collective-permute-start | bytes 276488 | tf_op jit(solution)/shard_map/ppermute | solution.py:504
  61.1 8.9 %collective-permute-start.1 = (bf16[60,768]{1,0:T(8,128)(2,1)S(1)}, bf16[60,768]{1,0:T(8,128)(2,1)S(1)}, u32[]{:S(2)}, u32[]{:S(2)}) collective-permute-start(bf16[60,768]{1,0:T(8,128)(2,1)S(1)} %get-tuple-element.17), channel_id=1, source_target_pairs={{0,2},{1,3},{2,0},{3,1},{4,6},{5,7},{6,4},{7,5}} | collective-permute-start | bytes 276488 | tf_op jit(solution)/shard_map/ppermute | solution.py:504
  61.5 8.5 %collective-permute-start = (bf16[60,768]{1,0:T(8,128)(2,1)S(1)}, bf16[60,768]{1,0:T(8,128)(2,1)S(1)}, u32[]{:S(2)}, u32[]{:S(2)}) collective-permute-start(bf16[60,768]{1,0:T(8,128)(2,1)S(1)} %get-tuple-element.17), channel_id=1, source_target_pairs={{0,1},{1,0},{2,3},{3,2},{4,5},{5,4},{6,7},{7,6}} | collective-permute-start | bytes 276488 | tf_op jit(solution)/shard_map/ppermute | solution.py:504
  61.5 8.4 %copy-start = (bf16[2,768]{1,0:T(2,128)(2,1)S(1)}, bf16[2,768]{1,0:T(2,128)(2,1)}, u32[]{:S(2)}) copy-start(bf16[2,768]{1,0:T(2,128)(2,1)} %b2_hbm.1) | copy-start | bytes 9220

commit v7 on v6

--- a/solution.py
+++ b/solution.py
@@ -70,7 +70,7 @@
     return [pltpu.make_async_copy(s, d, sem.at[i]) for i, (s, d) in enumerate(pairs)]
 
 
-def self_kernel(layer, beams, h_hbm, pos_hbm, g_hbm, b_hbm, wq_hbm, wk_hbm, wv_hbm, bq_hbm, bv_hbm, k_hbm, v_hbm, o_hbm, ko_hbm, vo_hbm,
+def self_kernel(layer, beams, parts, h_hbm, pos_hbm, g_hbm, b_hbm, wq_hbm, wk_hbm, wv_hbm, bq_hbm, bv_hbm, k_hbm, v_hbm, o_hbm, ko_hbm, vo_hbm,
                 h, pos_ref, g, b, wq, wk, wv, bq, bv, kbuf, vbuf, qs, kt, vt, os, o, psem, ksem, vsem, kosem, vosem):
     rows = h.shape[0]
     audios = rows // beams
@@ -152,7 +152,8 @@
     def _(pair):
         release(pair)
 
-    o[...] = os[...].astype(BF)
+    for m in range(parts):
+        o[m] = os[m * rows // parts:(m + 1) * rows // parts, :].astype(BF)
     last = pltpu.make_async_copy(o, o_hbm, psem.at[0])
     last.start()
 
@@ -164,14 +165,14 @@
     last.wait()
 
 
-def self_call(layer, beams, h, pos, g, b, wq, wk, wv, bq, bv, k, v):
+def self_call(layer, beams, parts, h, pos, g, b, wq, wk, wv, bq, bv, k, v):
     rows = h.shape[0]
     audios = rows // beams
     _, _, width, slots = k.shape
     args = (h, pos, g, b, wq, wk, wv, bq, bv, k, v)
     return pl.pallas_call(
-        functools.partial(self_kernel, layer, beams),
-        out_shape=(jax.ShapeDtypeStruct((rows, width), BF), jax.ShapeDtypeStruct(k.shape, BF), jax.ShapeDtypeStruct(v.shape, BF)),
+        functools.partial(self_kernel, layer, beams, parts),
+        out_shape=(jax.ShapeDtypeStruct((parts, rows // parts, width), BF), jax.ShapeDtypeStruct(k.shape, BF), jax.ShapeDtypeStruct(v.shape, BF)),
         in_specs=[ANY] * 11,
         out_specs=(ANY, ANY, ANY),
         scratch_shapes=[
@@ -179,7 +180,7 @@
             pltpu.VMEM(wq.shape[1:], BF), pltpu.VMEM(wk.shape[1:], BF), pltpu.VMEM(wv.shape[1:], BF),
             pltpu.VMEM(bq.shape, BF), pltpu.VMEM(bv.shape, BF),
             pltpu.VMEM((rows, width, slots), BF), pltpu.VMEM((rows, width, slots), BF),
-            pltpu.VMEM((rows, width), F32), pltpu.VMEM((width, 128), F32), pltpu.VMEM((width, 128), F32), pltpu.VMEM((rows, width), F32), pltpu.VMEM((rows, width), BF),
+            pltpu.VMEM((rows, width), F32), pltpu.VMEM((width, 128), F32), pltpu.VMEM((width, 128), F32), pltpu.VMEM((rows, width), F32), pltpu.VMEM((parts, rows // parts, width), BF),
             DMA((9,)), DMA((audios,)), DMA((audios,)), DMA((audios,)), DMA((audios,)),
         ],
         cost_estimate=pl.CostEstimate(flops=0, bytes_accessed=4 * k.size, transcendentals=0),
@@ -196,7 +197,7 @@
     audios = rows // beams
     group = audios // parts
     prow = rows // parts
-    width = o.shape[1]
+    width = o.shape[-1]
     heads = width // 64
     scale = 64 ** -0.25
     dp = lax.axis_index('dp')
@@ -230,25 +231,9 @@
 
     start(early)
     start(small)
-    start(first[:1])
-
-    @pl.loop(0, audios)
-    def _(a):
-        start(cross_in(0, a))
-
-    start(first[1:])
     barrier = pltpu.get_barrier_semaphore()
     for peer in peers:
         pl.semaphore_signal(barrier, inc=1, device_id=(dp, peer), device_id_type=MESH)
-
-    start(extra)
-    start(second)
-
-    @pl.loop(0, audios)
-    def _(a):
-        start(self_in(a))
-
-    pl.semaphore_wait(barrier, 3)
 
     def sends(step, m):
         return [pltpu.make_async_remote_copy(snd.at[step, m], rcv.at[step, m, j], ssem.at[step, m, j], rsem.at[step, m, j], device_id=(dp, peer), device_id_type=MESH) for j, peer in enumerate(peers)]
@@ -297,11 +282,9 @@
                 acc = acc + out[j * 8:j * 8 + 8]
             os[m, n * beams:(n + 1) * beams, :] = acc[0:beams]
 
-        p = probs_of(0)
+        probs = [probs_of(n) for n in range(group)]
         for n in range(group):
-            p_next = probs_of(n + 1) if n + 1 < group else None
-            mix(n, p)
-            p = p_next
+            mix(n, probs[n])
 
         if layer == 0:
             @pl.loop(0, group)
@@ -359,18 +342,32 @@
                 out = jnp.where(own, out, 0.0) + p_new[j * 8:j * 8 + 8] * row(vr, r)
                 os[m, r:r + 1, :] = jnp.sum(out, axis=0, keepdims=True)
 
-        p = probs_of(0)
+        probs = [probs_of(n) for n in range(group)]
         for n in range(group):
-            p_next = probs_of(n + 1) if n + 1 < group else None
-            mix(n, *p)
-            p = p_next
+            mix(n, *probs[n])
 
         return dot(os[m].astype(BF), wo[1])
 
     wait(early)
     wait(small)
-    for m in range(parts):
-        push(0, m, dot(dot(pick(m), o[...]).astype(BF), wo[0]))
+    shares = [dot(o[m], wo[0]) for m in range(parts)]
+    pl.semaphore_wait(barrier, 3)
+    for m in range(parts):
+        push(0, m, shares[m])
+    start(first[:1])
+
+    @pl.loop(0, audios)
+    def _(a):
+        start(cross_in(0, a))
+
+    start(first[1:])
+    start(extra)
+    start(second)
+
+    @pl.loop(0, audios)
+    def _(a):
+        start(self_in(a))
+
     for m in range(parts):
         hid[m] = dot(pick(m), h[...]).astype(BF)
         qr[m, prow:, :] = jnp.zeros((qr.shape[1] - prow, width), F32)
@@ -503,8 +500,9 @@
         def hop(x, flip):
             return lax.ppermute(x, 'tp', [(i, i ^ flip) for i in range(4)])
 
-        o, ko, vo = self_call(0, beams, hidden, positions, g, b, wq, wk, wv, bq, bv, sk, sv)
-        part, hidden, sk1, sv1, kt, vt, spot = rest_call(beams, 3, o, hidden, positions, g, b, wq, bq, wk, wv, bv, wo, bo, wc, bc, wco, bco, w1, b1, w2, b2, sk, sv, ck, cv)
+        parts = 2
+        o, ko, vo = self_call(0, beams, parts, hidden, positions, g, b, wq, wk, wv, bq, bv, sk, sv)
+        part, hidden, sk1, sv1, kt, vt, spot = rest_call(beams, parts, o, hidden, positions, g, b, wq, bq, wk, wv, bv, wo, bo, wc, bc, wco, bco, w1, b1, w2, b2, sk, sv, ck, cv)
         ko, vo = write_call(1, beams, spot, kt, vt, sk1, sv1, ko, vo)
         here, mate, far, diag = (x.astype(F32) for x in (part, hop(part, 1), hop(part, 2), hop(part, 3)))
         hidden = (hidden.astype(F32) + ((here + mate) + (far + diag)) + b2[1].astype(F32)).astype(BF)

time: 70.8 us -> 68.2 us (0.963)
  Pallas kernels: 66.6 us -> 64.8 us
  starting transfers between devices: 2.73 us -> 1.88 us
    pallas_call x1, Pallas kernels: 42.1 us -> 40.3 us  [rest_call(): pl.pallas_call(functools.partial(rest_kernel, beams, parts), out_shape=(p...]
    ppermute x3, starting transfers between devices: 2.73 us -> 1.88 us  [hop(): return lax.ppermute(x, 'tp', [(i, i ^ flip) for i in range(4)])]
where the time goes in v7:
time: 68.2 us; the launch traced here: 68.1 us
  Pallas kernels  64.8 us (95%)
  starting transfers between devices  1.88 us (3%)
  other arithmetic  0.74 us (1%)
  between operations  0.69 us (1%)
    pallas_call x1, Pallas kernels, rest_call(): pl.pallas_call(functools.partial(rest_kernel, beams, parts), out_shape=(p...  40.3 us
    pallas_call x1, Pallas kernels, self_call(): pl.pallas_call(functools.partial(self_kernel, layer, beams, parts), out_s...  16.1 us
    pallas_call x1, Pallas kernels, write_call(): pl.pallas_call(functools.partial(write_kernel, layer, beams), out_shape=(...  8.4 us
    ppermute x3, starting transfers between devices, hop(): return lax.ppermute(x, 'tp', [(i, i ^ flip) for i in range(4)])  1.88 us
  transfers between devices with their start and end apart: 3, of which 0 were waited for; matrix products, arithmetic and copies ran while one was open for 0% of the time, Pallas kernels for 12%

profile of v7, /device:TPU:0, one launch (start us, length us, event | category | flops | bytes accessed | tf_op | source)
XLA Modules:
  0.0 68.1 jit_solution(13161361856653821089)
XLA Ops:
  0.6 16.1 %self_0.1 = (bf16[2,30,192]{2,1,0:T(8,128)(2,1)}, bf16[2,60,192,448]{3,2,1,0:T(8,128)(2,1)}, bf16[2,60,192,448]{3,2,1,0:T(8,128)(2,1)}) custom-call(bf16[60,768]{1,0:T(8,128)(2,1)} %h_hbm.3, s32[60]{0:T(128)} %pos_hbm.3, bf16[3,2,768]{2,1,0:T(2,128)(2,1)} %bitcast.39, bf16[3,2,768]{2,1,0:T(2,128)(2,1)} %bitcast.41, bf16[2,192,768]{2,1,0:T(8,128)(2,1)} %bitcast.32, ...), custom_call_target="tpu_custom_call" | custom-call | bytes 41287680 | tf_op jit(solution)/shard_map/self_0/pallas_call | solution.py:173
  16.7 40.3 %rest.1 = (bf16[60,768]{1,0:T(8,128)(2,1)S(1)}, bf16[60,768]{1,0:T(8,128)(2,1)S(1)}, bf16[60,192,448]{2,1,0:T(8,128)(2,1)S(1)}, bf16[60,192,448]{2,1,0:T(8,128)(...) custom-call(bf16[2,30,192]{2,1,0:T(8,128)(2,1)} %get-tuple-element.15.o_hbm, ...), custom_call_target="tpu_custom_call" | custom-call | tf_op jit(solution)/shard_map/rest/pallas_call | solution.py:415
  57.1 0.7 %collective-permute-start.2 = (bf16[60,768]{1,0:T(8,128)(2,1)S(1)}, bf16[60,768]{1,0:T(8,128)(2,1)S(1)}, u32[]{:S(2)}, u32[]{:S(2)}) collective-permute-start(bf16[60,768]{1,0:T(8,128)(2,1)S(1)} %get-tuple-element.17), channel_id=1, source_target_pairs={{0,3},{1,2},{2,1},{3,0},{4,7},{5,6},{6,5},{7,4}} | collective-permute-start | bytes 276488 | tf_op jit(solution)/shard_map/ppermute | solution.py:501
  57.8 1.1 %collective-permute-start.1 = (bf16[60,768]{1,0:T(8,128)(2,1)S(1)}, bf16[60,768]{1,0:T(8,128)(2,1)S(1)}, u32[]{:S(2)}, u32[]{:S(2)}) collective-permute-start(bf16[60,768]{1,0:T(8,128)(2,1)S(1)} %get-tuple-element.17), channel_id=1, source_target_pairs={{0,2},{1,3},{2,0},{3,1},{4,6},{5,7},{6,4},{7,5}} | collective-permute-start | bytes 276488 | tf_op jit(solution)/shard_map/ppermute | solution.py:501
  58.9 0.1 collective-permute-start
  58.9 0.0 copy-start
  58.9 8.4 %write.1 = (bf16[2,60,192,448]{3,2,1,0:T(8,128)(2,1)}, bf16[2,60,192,448]{3,2,1,0:T(8,128)(2,1)}, bf16[60,192,448]{2,1,0:T(8,128)(2,1)S(1)}, bf16[60,192,448]{2,1,0:T(8,128)(2,1)S(1)}) custom-call(s32[12,8,128]{2,1,0:T(8,128)S(1)} %get-tuple-element.18.spot, ...), custom_call_target="tpu_custom_call", output_to_operand_aliasing={{2}: (3, {}), {3}: (4, {}), {0}: (5, {}), {1}: (6, {})} | custom-call | bytes 20643840 | tf_op jit(solution)/shard_map/write/pallas_call | solution.py:466
  67.3 0.0 copy-done
  67.4 0.0 collective-permute-done.2
  67.4 0.0 collective-permute-done.1
  67.4 0.0 collective-permute-done
  67.4 0.7 %add_convert_fusion = bf16[60,768]{1,0:T(8,128)(2,1)} fusion(bf16[60,768]{1,0:T(8,128)(2,1)S(1)} %collective-permute-done.2, bf16[60,768]{1,0:T(8,128)(2,1)S(1)} %collective-permute-done.1, bf16[60,768]{1,0:T(8,128)(2,1)S(1)} %collective-permute-done, bf16[60,768]{1,0:T(8,128)(2,1)S(1)} %get-tuple-element.17, bf16[60,768]{1,0:T(8,128)(2,1)S(1)} %get-tuple-element.16, ...), kind=kLoop, calls=%fused_computation | loop fusion | flops 506880 | bytes 556032 | tf_op jit(solution)/shard_map/convert_element_type | solution.py:508
  (1 shorter events, 0.0 us)
Async XLA Ops:
  57.1 10.3 %collective-permute-start.2 = (bf16[60,768]{1,0:T(8,128)(2,1)S(1)}, bf16[60,768]{1,0:T(8,128)(2,1)S(1)}, u32[]{:S(2)}, u32[]{:S(2)}) collective-permute-start(bf16[60,768]{1,0:T(8,128)(2,1)S(1)} %get-tuple-element.17), channel_id=1, source_target_pairs={{0,3},{1,2},{2,1},{3,0},{4,7},{5,6},{6,5},{7,4}} | collective-permute-start | bytes 276488 | tf_op jit(solution)/shard_map/ppermute | solution.py:501
  57.8 9.6 %collective-permute-start.1 = (bf16[60,768]{1,0:T(8,128)(2,1)S(1)}, bf16[60,768]{1,0:T(8,128)(2,1)S(1)}, u32[]{:S(2)}, u32[]{:S(2)}) collective-permute-start(bf16[60,768]{1,0:T(8,128)(2,1)S(1)} %get-tuple-element.17), channel_id=1, source_target_pairs={{0,2},{1,3},{2,0},{3,1},{4,6},{5,7},{6,4},{7,5}} | collective-permute-start | bytes 276488 | tf_op jit(solution)/shard_map/ppermute | solution.py:501
  58.9 8.5 %collective-permute-start = (bf16[60,768]{1,0:T(8,128)(2,1)S(1)}, bf16[60,768]{1,0:T(8,128)(2,1)S(1)}, u32[]{:S(2)}, u32[]{:S(2)}) collective-permute-start(bf16[60,768]{1,0:T(8,128)(2,1)S(1)} %get-tuple-element.17), channel_id=1, source_target_pairs={{0,1},{1,0},{2,3},{3,2},{4,5},{5,4},{6,7},{7,6}} | collective-permute-start | bytes 276488 | tf_op jit(solution)/shard_map/ppermute | solution.py:501
  58.9 8.4 %copy-start = (bf16[2,768]{1,0:T(2,128)(2,1)S(1)}, bf16[2,768]{1,0:T(2,128)(2,1)}, u32[]{:S(2)}) copy-start(bf16[2,768]{1,0:T(2,128)(2,1)} %b2_hbm.1) | copy-start | bytes 9220

commit v8 on v7

--- a/solution.py
+++ b/solution.py
@@ -190,9 +190,9 @@
 
 
 def rest_kernel(beams, parts, o_hbm, h_hbm, pos_hbm, g_hbm, b_hbm, wq_hbm, bq_hbm, wk_hbm, wv_hbm, bv_hbm, wo_hbm, bo_hbm, wc_hbm, bc_hbm, wco_hbm, bco_hbm, w1_hbm, b1_hbm, w2_hbm, b2_hbm,
-                sk_hbm, sv_hbm, ck_hbm, cv_hbm, part_ref, out_ref, sk, sv, kt, vt, spot,
-                o, h, pos_ref, g, b, wq, bq, wk, wv, bv, wo, bo, wc, bc, wco, bco, w1, b1, w2, b2, ck, cv, hid, qr, kr, vr, kall, vall, os, snd, rcv,
-                psem, wsem, skem, svem, ckem, cvem, ssem, rsem):
+                wo_far, sk_hbm, sv_hbm, ck_hbm, cv_hbm, part_ref, out_ref, sk, sv, kt, vt, spot,
+                o, h, pos_ref, g, b, wq, bq, wk, wv, bv, wo, bo, wc, bc, wco, bco, w1, b1, w2, b2, ck, cv, hid, qr, kr, vr, kall, vall, os, got, snd, rcv,
+                psem, wsem, msem, mrsem, skem, svem, ckem, cvem, ssem, rsem):
     rows = h.shape[0]
     audios = rows // beams
     group = audios // parts
@@ -209,9 +209,13 @@
     def layer_copies(layer, arrays, sem):
         return copies([(x.at[layer], y.at[layer]) for x, y in arrays], sem)
 
-    early = layer_copies(0, ((wo_hbm, wo),), wsem.at[0])
     first = layer_copies(0, ((wc_hbm, wc), (wco_hbm, wco), (w1_hbm, w1), (w2_hbm, w2)), wsem.at[1])
-    second = layer_copies(1, ((wo_hbm, wo), (wc_hbm, wc), (wco_hbm, wco), (w1_hbm, w1), (w2_hbm, w2)), wsem.at[2])
+    second = layer_copies(1, ((wc_hbm, wc), (wco_hbm, wco), (w1_hbm, w1), (w2_hbm, w2)), wsem.at[2])
+    early = copies([(wo_hbm.at[i], wo.at[i, 0]) for i in range(2)], wsem.at[0])
+
+    def shared(layer):
+        return [pltpu.make_async_remote_copy(src.at[layer], wo.at[layer, 1 + j], msem.at[layer, j], mrsem.at[layer, j], device_id=(dp, mate), device_id_type=MESH) for j, src in enumerate((wo_hbm, wo_far))]
+
     extra = copies([(x.at[1], y) for x, y in ((wq_hbm, wq), (wk_hbm, wk), (wv_hbm, wv))], wsem.at[3])
 
     def cross_in(layer, a):
@@ -229,8 +233,8 @@
         for c in pair:
             c.wait()
 
+    start(small)
     start(early)
-    start(small)
     barrier = pltpu.get_barrier_semaphore()
     for peer in peers:
         pl.semaphore_signal(barrier, inc=1, device_id=(dp, peer), device_id_type=MESH)
@@ -246,6 +250,18 @@
         wait(sends(step, m))
         mine = snd[step, m].astype(F32) + rcv[step, m, 2].astype(F32)
         return mine + (rcv[step, m, 0].astype(F32) + rcv[step, m, 1].astype(F32))
+
+    def heads_sends(step, m):
+        return [pltpu.make_async_remote_copy(got.at[step, m, 3], got.at[step, m, j], ssem.at[step, m, j], rsem.at[step, m, j], device_id=(dp, peer), device_id_type=MESH) for j, peer in enumerate(peers)]
+
+    def push_heads(step, m, out):
+        got[step, m, 3] = out
+        start(heads_sends(step, m))
+
+    def project(step, m, layer):
+        wait(heads_sends(step, m))
+        here = dot(got[step, m, 3], wo[layer, 0]) + dot(got[step, m, 2], wo[layer, 1])
+        return here + (dot(got[step, m, 0], wo_far[layer]) + dot(got[step, m, 1], wo[layer, 2]))
 
     def settle(m, update, bias):
         new = (hid[m].astype(F32) + update + bias.astype(F32)).astype(BF)
@@ -346,14 +362,13 @@
         for n in range(group):
             mix(n, *probs[n])
 
-        return dot(os[m].astype(BF), wo[1])
-
-    wait(early)
+        return os[m].astype(BF)
+
     wait(small)
-    shares = [dot(o[m], wo[0]) for m in range(parts)]
     pl.semaphore_wait(barrier, 3)
     for m in range(parts):
-        push(0, m, shares[m])
+        push_heads(0, m, o[m])
+    start(shared(0))
     start(first[:1])
 
     @pl.loop(0, audios)
@@ -362,6 +377,7 @@
 
     start(first[1:])
     start(extra)
+    start(shared(1))
     start(second)
 
     @pl.loop(0, audios)
@@ -373,21 +389,24 @@
         qr[m, prow:, :] = jnp.zeros((qr.shape[1] - prow, width), F32)
     kall[rows:, :] = jnp.zeros((128 - rows, width), F32)
     vall[rows:, :] = jnp.zeros((128 - rows, width), F32)
+    wait(early)
+    wait(shared(0))
     wait(first)
     for m in range(parts):
-        push(1, m, cross_half(0, m, settle(m, total(0, m), bo[0:1, :])))
+        push(1, m, cross_half(0, m, settle(m, project(0, m, 0), bo[0:1, :])))
     for m in range(parts):
         push(2, m, mlp_half(0, m, settle(m, total(1, m), bco[0:1, :])))
     wait(second)
     wait(extra)
     for m in range(parts):
-        push(3, m, self_half(m, settle(m, total(2, m), b2[0:1, :])))
+        push_heads(3, m, self_half(m, settle(m, total(2, m), b2[0:1, :])))
     kt[...] = kall[...].T
     vt[...] = vall[...].T
     for a in range(audios):
         spot[a] = jnp.full(spot.shape[1:], pos_ref[a * beams], jnp.int32)
-    for m in range(parts):
-        push(4, m, cross_half(1, m, settle(m, total(3, m), bo[1:2, :])))
+    wait(shared(1))
+    for m in range(parts):
+        push(4, m, cross_half(1, m, settle(m, project(3, m, 1), bo[1:2, :])))
     final = jnp.zeros((rows, h.shape[1]), F32)
     resid = jnp.zeros((rows, h.shape[1]), F32)
     for m in range(parts):
@@ -399,12 +418,12 @@
     out_ref[...] = resid.astype(BF)
 
 
-def rest_call(beams, parts, o, h, pos, g, b, wq, bq, wk, wv, bv, wo, bo, wc, bc, wco, bco, w1, b1, w2, b2, sk, sv, ck, cv):
+def rest_call(beams, parts, o, h, pos, g, b, wq, bq, wk, wv, bv, wo, bo, wc, bc, wco, bco, w1, b1, w2, b2, wo_far, sk, sv, ck, cv):
     rows, dim = h.shape
     _, audios, width, frames = ck.shape
     slots = sk.shape[-1]
     prow = rows // parts
-    args = (o, h, pos, g, b, wq, bq, wk, wv, bv, wo, bo, wc, bc, wco, bco, w1, b1, w2, b2, sk, sv, ck, cv)
+    args = (o, h, pos, g, b, wq, bq, wk, wv, bv, wo, bo, wc, bc, wco, bco, w1, b1, w2, b2, wo_far, sk, sv, ck, cv)
 
     def whole(x):
         return pltpu.VMEM(x.shape, BF)
@@ -415,15 +434,15 @@
     return pl.pallas_call(
         functools.partial(rest_kernel, beams, parts),
         out_shape=(pltpu.VMEM(h.shape, BF), pltpu.VMEM(h.shape, BF), pltpu.VMEM((rows, width, slots), BF), pltpu.VMEM((rows, width, slots), BF), pltpu.VMEM((width, 128), F32), pltpu.VMEM((width, 128), F32), pltpu.VMEM((audios, 8, 128), jnp.int32)),
-        in_specs=[ANY] * len(args),
+        in_specs=[ANY] * (len(args) - 5) + [VM] + [ANY] * 4,
         out_specs=(VM,) * 7,
         scratch_shapes=[
-            whole(o), whole(h), pltpu.SMEM(pos.shape, jnp.int32), whole(g), whole(b), one(wq), whole(bq), one(wk), one(wv), whole(bv), whole(wo), whole(bo), whole(wc), whole(bc), whole(wco), whole(bco), whole(w1), whole(b1), whole(w2), whole(b2), one(ck), one(cv),
+            whole(o), whole(h), pltpu.SMEM(pos.shape, jnp.int32), whole(g), whole(b), one(wq), whole(bq), one(wk), one(wv), whole(bv), pltpu.VMEM((2, 3, width, dim), BF), whole(bo), whole(wc), whole(bc), whole(wco), whole(bco), whole(w1), whole(b1), whole(w2), whole(b2), one(ck), one(cv),
             pltpu.VMEM((parts, prow, dim), BF),
             pltpu.VMEM((parts, prow + 8, width), F32), pltpu.VMEM((parts, prow, width), F32), pltpu.VMEM((parts, prow, width), F32),
             pltpu.VMEM((128, width), F32), pltpu.VMEM((128, width), F32), pltpu.VMEM((parts, prow, width), F32),
-            pltpu.VMEM((5, parts, prow, dim), BF), pltpu.VMEM((5, parts, 3, prow, dim), BF),
-            DMA((12,)), DMA((4, 8)), DMA((audios,)), DMA((audios,)), DMA((audios,)), DMA((audios,)), DMA((5, parts, 3)), DMA((5, parts, 3)),
+            pltpu.VMEM((5, parts, 4, prow, width), BF), pltpu.VMEM((5, parts, prow, dim), BF), pltpu.VMEM((5, parts, 3, prow, dim), BF),
+            DMA((12,)), DMA((4, 8)), DMA((2, 2)), DMA((2, 2)), DMA((audios,)), DMA((audios,)), DMA((audios,)), DMA((audios,)), DMA((5, parts, 3)), DMA((5, parts, 3)),
         ],
         compiler_params=pltpu.CompilerParams(collective_id=0, has_side_effects=True, vmem_limit_bytes=REST_LIMIT),
         name="rest",
@@ -501,8 +520,9 @@
             return lax.ppermute(x, 'tp', [(i, i ^ flip) for i in range(4)])
 
         parts = 2
+        wo_far = pltpu.with_memory_space_constraint(hop(wo, 2), pltpu.VMEM)
         o, ko, vo = self_call(0, beams, parts, hidden, positions, g, b, wq, wk, wv, bq, bv, sk, sv)
-        part, hidden, sk1, sv1, kt, vt, spot = rest_call(beams, parts, o, hidden, positions, g, b, wq, bq, wk, wv, bv, wo, bo, wc, bc, wco, bco, w1, b1, w2, b2, sk, sv, ck, cv)
+        part, hidden, sk1, sv1, kt, vt, spot = rest_call(beams, parts, o, hidden, positions, g, b, wq, bq, wk, wv, bv, wo, bo, wc, bc, wco, bco, w1, b1, w2, b2, wo_far, sk, sv, ck, cv)
         ko, vo = write_call(1, beams, spot, kt, vt, sk1, sv1, ko, vo)
         here, mate, far, diag = (x.astype(F32) for x in (part, hop(part, 1), hop(part, 2), hop(part, 3)))
         hidden = (hidden.astype(F32) + ((here + mate) + (far + diag)) + b2[1].astype(F32)).astype(BF)

time: 68.2 us -> 69.1 us (1.013)
  starting transfers between devices: 1.88 us -> 5.36 us
  Pallas kernels: 64.8 us -> 62.2 us
    ppermute x3 -> x4, starting transfers between devices: 1.88 us -> 5.36 us  [hop(): return lax.ppermute(x, 'tp', [(i, i ^ flip) for i in range(4)])]
    pallas_call x1, Pallas kernels: 40.3 us -> 37.7 us  [rest_call(): pl.pallas_call(functools.partial(rest_kernel, beams, parts), out_shape=(p...]
  transfers between devices with their start and end apart: 3 -> 4, of which waited for: 0 -> 0; matrix products, arithmetic and copies ran while one was open for 0% -> 0% of each run, Pallas kernels for 12% -> 35%
where the time goes in v8:
time: 69.1 us; the launch traced here: 69 us
  Pallas kernels  62.2 us (90%)
  starting transfers between devices  5.36 us (8%)
  other arithmetic  0.73 us (1%)
  between operations  0.7 us (1%)
    pallas_call x1, Pallas kernels, rest_call(): pl.pallas_call(functools.partial(rest_kernel, beams, parts), out_shape=(p...  37.7 us
    pallas_call x1, Pallas kernels, self_call(): pl.pallas_call(functools.partial(self_kernel, layer, beams, parts), out_s...  16.1 us
    pallas_call x1, Pallas kernels, write_call(): pl.pallas_call(functools.partial(write_kernel, layer, beams), out_shape=(...  8.4 us
    ppermute x4, starting transfers between devices, hop(): return lax.ppermute(x, 'tp', [(i, i ^ flip) for i in range(4)])  5.36 us
  transfers between devices with their start and end apart: 4, of which 0 were waited for; matrix products, arithmetic and copies ran while one was open for 0% of the time, Pallas kernels for 35%

profile of v8, /device:TPU:0, one launch (start us, length us, event | category | flops | bytes accessed | tf_op | source)
XLA Modules:
  0.0 69.0 jit_solution(15201354951585301071)
XLA Ops:
  0.6 3.4 %collective-permute-start = (bf16[2,192,768]{2,1,0:T(8,128)(2,1)}, bf16[2,192,768]{2,1,0:T(8,128)(2,1)S(1)}, u32[]{:S(2)}, u32[]{:S(2)}) collective-permute-start(bf16[2,192,768]{2,1,0:T(8,128)(2,1)} %wo_hbm.1), channel_id=1, source_target_pairs={{0,2},{1,3},{2,0},{3,1},{4,6},{5,7},{6,4},{7,5}} | collective-permute-start | bytes 1769480 | tf_op jit(solution)/shard_map/ppermute | solution.py:520
  4.0 16.1 %self_0.1 = (bf16[2,30,192]{2,1,0:T(8,128)(2,1)}, bf16[2,60,192,448]{3,2,1,0:T(8,128)(2,1)}, bf16[2,60,192,448]{3,2,1,0:T(8,128)(2,1)}) custom-call(bf16[60,768]{1,0:T(8,128)(2,1)} %h_hbm.3, s32[60]{0:T(128)} %pos_hbm.3, bf16[3,2,768]{2,1,0:T(2,128)(2,1)} %bitcast.39, bf16[3,2,768]{2,1,0:T(2,128)(2,1)} %bitcast.41, bf16[2,192,768]{2,1,0:T(8,128)(2,1)} %bitcast.32, ...), custom_call_target="tpu_custom_call" | custom-call | bytes 41287680 | tf_op jit(solution)/shard_map/self_0/pallas_call | solution.py:173
  20.1 0.0 collective-permute-done.wo_far
  20.1 0.0 copy-start
  20.1 37.7 %rest.1 = (bf16[60,768]{1,0:T(8,128)(2,1)S(1)}, bf16[60,768]{1,0:T(8,128)(2,1)S(1)}, bf16[60,192,448]{2,1,0:T(8,128)(2,1)S(1)}, bf16[60,192,448]{2,1,0:T(8,128)(...) custom-call(bf16[2,30,192]{2,1,0:T(8,128)(2,1)} %get-tuple-element.15.o_hbm, ...), custom_call_target="tpu_custom_call" | custom-call | tf_op jit(solution)/shard_map/rest/pallas_call | solution.py:434
  57.8 1.5 %collective-permute-start.3 = (bf16[60,768]{1,0:T(8,128)(2,1)S(1)}, bf16[60,768]{1,0:T(8,128)(2,1)S(1)}, u32[]{:S(2)}, u32[]{:S(2)}) collective-permute-start(bf16[60,768]{1,0:T(8,128)(2,1)S(1)} %get-tuple-element.17), channel_id=1, source_target_pairs={{0,3},{1,2},{2,1},{3,0},{4,7},{5,6},{6,5},{7,4}} | collective-permute-start | bytes 276488 | tf_op jit(solution)/shard_map/ppermute | solution.py:520
  59.4 0.5 collective-permute-start.2
  59.8 0.0 collective-permute-start.1
  59.8 0.0 copy-done
  59.8 8.4 %write.1 = (bf16[2,60,192,448]{3,2,1,0:T(8,128)(2,1)}, bf16[2,60,192,448]{3,2,1,0:T(8,128)(2,1)}, bf16[60,192,448]{2,1,0:T(8,128)(2,1)S(1)}, bf16[60,192,448]{2,1,0:T(8,128)(2,1)S(1)}) custom-call(s32[12,8,128]{2,1,0:T(8,128)S(1)} %get-tuple-element.18.spot, ...), custom_call_target="tpu_custom_call", output_to_operand_aliasing={{2}: (3, {}), {3}: (4, {}), {0}: (5, {}), {1}: (6, {})} | custom-call | bytes 20643840 | tf_op jit(solution)/shard_map/write/pallas_call | solution.py:485
  68.3 0.0 collective-permute-done.3
  68.3 0.0 collective-permute-done.2
  68.3 0.0 collective-permute-done.1
  68.3 0.7 %add_convert_fusion = bf16[60,768]{1,0:T(8,128)(2,1)} fusion(bf16[60,768]{1,0:T(8,128)(2,1)S(1)} %collective-permute-done.3, bf16[60,768]{1,0:T(8,128)(2,1)S(1)} %collective-permute-done.2, bf16[60,768]{1,0:T(8,128)(2,1)S(1)} %collective-permute-done.1, bf16[60,768]{1,0:T(8,128)(2,1)S(1)} %get-tuple-element.17, bf16[60,768]{1,0:T(8,128)(2,1)S(1)} %get-tuple-element.16, ...), kind=kLoop, calls=%fused_computation | loop fusion | flops 506880 | bytes 556032 | tf_op jit(solution)/shard_map/convert_element_type | solution.py:528
  (1 shorter events, 0.0 us)
Async XLA Ops:
  0.6 19.4 %collective-permute-start = (bf16[2,192,768]{2,1,0:T(8,128)(2,1)}, bf16[2,192,768]{2,1,0:T(8,128)(2,1)S(1)}, u32[]{:S(2)}, u32[]{:S(2)}) collective-permute-start(bf16[2,192,768]{2,1,0:T(8,128)(2,1)} %wo_hbm.1), channel_id=1, source_target_pairs={{0,2},{1,3},{2,0},{3,1},{4,6},{5,7},{6,4},{7,5}} | collective-permute-start | bytes 1769480 | tf_op jit(solution)/shard_map/ppermute | solution.py:520
  20.1 39.8 %copy-start = (bf16[2,768]{1,0:T(2,128)(2,1)S(1)}, bf16[2,768]{1,0:T(2,128)(2,1)}, u32[]{:S(2)}) copy-start(bf16[2,768]{1,0:T(2,128)(2,1)} %b2_hbm.1) | copy-start | bytes 9220
  57.8 10.4 %collective-permute-start.3 = (bf16[60,768]{1,0:T(8,128)(2,1)S(1)}, bf16[60,768]{1,0:T(8,128)(2,1)S(1)}, u32[]{:S(2)}, u32[]{:S(2)}) collective-permute-start(bf16[60,768]{1,0:T(8,128)(2,1)S(1)} %get-tuple-element.17), channel_id=1, source_target_pairs={{0,3},{1,2},{2,1},{3,0},{4,7},{5,6},{6,5},{7,4}} | collective-permute-start | bytes 276488 | tf_op jit(solution)/shard_map/ppermute | solution.py:520
  59.4 8.9 %collective-permute-start.2 = (bf16[60,768]{1,0:T(8,128)(2,1)S(1)}, bf16[60,768]{1,0:T(8,128)(2,1)S(1)}, u32[]{:S(2)}, u32[]{:S(2)}) collective-permute-start(bf16[60,768]{1,0:T(8,128)(2,1)S(1)} %get-tuple-element.17), channel_id=1, source_target_pairs={{0,2},{1,3},{2,0},{3,1},{4,6},{5,7},{6,4},{7,5}} | collective-permute-start | bytes 276488 | tf_op jit(solution)/shard_map/ppermute | solution.py:520
  59.8 8.5 %collective-permute-start.1 = (bf16[60,768]{1,0:T(8,128)(2,1)S(1)}, bf16[60,768]{1,0:T(8,128)(2,1)S(1)}, u32[]{:S(2)}, u32[]{:S(2)}) collective-permute-start(bf16[60,768]{1,0:T(8,128)(2,1)S(1)} %get-tuple-element.17), channel_id=1, source_target_pairs={{0,1},{1,0},{2,3},{3,2},{4,5},{5,4},{6,7},{7,6}} | collective-permute-start | bytes 276488 | tf_op jit(solution)/shard_map/ppermute | solution.py:520

commit v9 on v8

--- a/solution.py
+++ b/solution.py
@@ -283,6 +283,13 @@
         def _(n):
             wait(cross_in(layer, m * group + n))
 
+        if layer == 0:
+            @pl.loop(0, group)
+            def _(n):
+                start(self_in(m * group + n))
+
+            start(first[2:] if m == 0 else extra if m == 1 else [])
+
         own = iota((heads * 8, width), 1) // 64 == iota((heads * 8, width), 0) // 8
 
         def probs_of(n):
@@ -302,10 +309,6 @@
         for n in range(group):
             mix(n, probs[n])
 
-        if layer == 0:
-            @pl.loop(0, group)
-            def _(n):
-                start(cross_in(1, m * group + n))
         return dot(os[m].astype(BF), wco[layer])
 
     def mlp_half(layer, m, wide):
@@ -329,6 +332,13 @@
         @pl.loop(0, group)
         def _(n):
             wait(self_in(m * group + n))
+
+        if m == 0:
+            start(second)
+
+        @pl.loop(0, group)
+        def _(n):
+            start(cross_in(1, m * group + n))
 
         def row(ref, r):
             return jnp.where(own, jnp.broadcast_to(ref[m, r:r + 1, :], own.shape), 0.0)
@@ -369,20 +379,13 @@
     for m in range(parts):
         push_heads(0, m, o[m])
     start(shared(0))
-    start(first[:1])
+    start(first[:2])
 
     @pl.loop(0, audios)
     def _(a):
         start(cross_in(0, a))
 
-    start(first[1:])
-    start(extra)
     start(shared(1))
-    start(second)
-
-    @pl.loop(0, audios)
-    def _(a):
-        start(self_in(a))
 
     for m in range(parts):
         hid[m] = dot(pick(m), h[...]).astype(BF)
@@ -391,12 +394,12 @@
     vall[rows:, :] = jnp.zeros((128 - rows, width), F32)
     wait(early)
     wait(shared(0))
-    wait(first)
+    wait(first[:2])
     for m in range(parts):
         push(1, m, cross_half(0, m, settle(m, project(0, m, 0), bo[0:1, :])))
+    wait(first[2:])
     for m in range(parts):
         push(2, m, mlp_half(0, m, settle(m, total(1, m), bco[0:1, :])))
-    wait(second)
     wait(extra)
     for m in range(parts):
         push_heads(3, m, self_half(m, settle(m, total(2, m), b2[0:1, :])))
@@ -404,6 +407,7 @@
     vt[...] = vall[...].T
     for a in range(audios):
         spot[a] = jnp.full(spot.shape[1:], pos_ref[a * beams], jnp.int32)
+    wait(second)
     wait(shared(1))
     for m in range(parts):
         push(4, m, cross_half(1, m, settle(m, project(3, m, 1), bo[1:2, :])))

time: 69.1 us -> 66.4 us (0.961)
  Pallas kernels: 62.2 us -> 59.6 us
    pallas_call x1, Pallas kernels: 37.7 us -> 35.1 us  [rest_call(): pl.pallas_call(functools.partial(rest_kernel, beams, parts), out_shape=(p...]
  transfers between devices with their start and end apart: 4 -> 4, of which waited for: 0 -> 0; matrix products, arithmetic and copies ran while one was open for 0% -> 0% of each run, Pallas kernels for 35% -> 37%
where the time goes in v9:
time: 66.4 us; the launch traced here: 66.3 us
  Pallas kernels  59.6 us (90%)
  starting transfers between devices  5.24 us (8%)
  other arithmetic  0.73 us (1%)
  between operations  0.7 us (1%)
    pallas_call x1, Pallas kernels, rest_call(): pl.pallas_call(functools.partial(rest_kernel, beams, parts), out_shape=(p...  35.1 us
    pallas_call x1, Pallas kernels, self_call(): pl.pallas_call(functools.partial(self_kernel, layer, beams, parts), out_s...  16.1 us
    pallas_call x1, Pallas kernels, write_call(): pl.pallas_call(functools.partial(write_kernel, layer, beams), out_shape=(...  8.4 us
    ppermute x4, starting transfers between devices, hop(): return lax.ppermute(x, 'tp', [(i, i ^ flip) for i in range(4)])  5.24 us
  transfers between devices with their start and end apart: 4, of which 0 were waited for; matrix products, arithmetic and copies ran while one was open for 0% of the time, Pallas kernels for 37%

profile of v9, /device:TPU:0, one launch (start us, length us, event | category | flops | bytes accessed | tf_op | source)
XLA Modules:
  0.0 66.3 jit_solution(14822837421028432992)
XLA Ops:
  0.6 3.4 %collective-permute-start = (bf16[2,192,768]{2,1,0:T(8,128)(2,1)}, bf16[2,192,768]{2,1,0:T(8,128)(2,1)S(1)}, u32[]{:S(2)}, u32[]{:S(2)}) collective-permute-start(bf16[2,192,768]{2,1,0:T(8,128)(2,1)} %wo_hbm.1), channel_id=1, source_target_pairs={{0,2},{1,3},{2,0},{3,1},{4,6},{5,7},{6,4},{7,5}} | collective-permute-start | bytes 1769480 | tf_op jit(solution)/shard_map/ppermute | solution.py:524
  4.0 16.1 %self_0.1 = (bf16[2,30,192]{2,1,0:T(8,128)(2,1)}, bf16[2,60,192,448]{3,2,1,0:T(8,128)(2,1)}, bf16[2,60,192,448]{3,2,1,0:T(8,128)(2,1)}) custom-call(bf16[60,768]{1,0:T(8,128)(2,1)} %h_hbm.3, s32[60]{0:T(128)} %pos_hbm.3, bf16[3,2,768]{2,1,0:T(2,128)(2,1)} %bitcast.39, bf16[3,2,768]{2,1,0:T(2,128)(2,1)} %bitcast.41, bf16[2,192,768]{2,1,0:T(8,128)(2,1)} %bitcast.32, ...), custom_call_target="tpu_custom_call" | custom-call | bytes 41287680 | tf_op jit(solution)/shard_map/self_0/pallas_call | solution.py:173
  20.1 0.0 collective-permute-done.wo_far
  20.1 0.0 copy-start
  20.1 35.1 %rest.1 = (bf16[60,768]{1,0:T(8,128)(2,1)S(1)}, bf16[60,768]{1,0:T(8,128)(2,1)S(1)}, bf16[60,192,448]{2,1,0:T(8,128)(2,1)S(1)}, bf16[60,192,448]{2,1,0:T(8,128)(...) custom-call(bf16[2,30,192]{2,1,0:T(8,128)(2,1)} %get-tuple-element.15.o_hbm, ...), custom_call_target="tpu_custom_call" | custom-call | tf_op jit(solution)/shard_map/rest/pallas_call | solution.py:438
  55.2 0.6 collective-permute-start.3
  55.8 1.3 %collective-permute-start.2 = (bf16[60,768]{1,0:T(8,128)(2,1)S(1)}, bf16[60,768]{1,0:T(8,128)(2,1)S(1)}, u32[]{:S(2)}, u32[]{:S(2)}) collective-permute-start(bf16[60,768]{1,0:T(8,128)(2,1)S(1)} %get-tuple-element.17), channel_id=1, source_target_pairs={{0,2},{1,3},{2,0},{3,1},{4,6},{5,7},{6,4},{7,5}} | collective-permute-start | bytes 276488 | tf_op jit(solution)/shard_map/ppermute | solution.py:524
  57.0 0.1 collective-permute-start.1
  57.1 0.0 copy-done
  57.1 8.4 %write.1 = (bf16[2,60,192,448]{3,2,1,0:T(8,128)(2,1)}, bf16[2,60,192,448]{3,2,1,0:T(8,128)(2,1)}, bf16[60,192,448]{2,1,0:T(8,128)(2,1)S(1)}, bf16[60,192,448]{2,1,0:T(8,128)(2,1)S(1)}) custom-call(s32[12,8,128]{2,1,0:T(8,128)S(1)} %get-tuple-element.18.spot, ...), custom_call_target="tpu_custom_call", output_to_operand_aliasing={{2}: (3, {}), {3}: (4, {}), {0}: (5, {}), {1}: (6, {})} | custom-call | bytes 20643840 | tf_op jit(solution)/shard_map/write/pallas_call | solution.py:489
  65.5 0.0 collective-permute-done.3
  65.5 0.0 collective-permute-done.2
  65.6 0.0 collective-permute-done.1
  65.6 0.7 %add_convert_fusion = bf16[60,768]{1,0:T(8,128)(2,1)} fusion(bf16[60,768]{1,0:T(8,128)(2,1)S(1)} %collective-permute-done.3, bf16[60,768]{1,0:T(8,128)(2,1)S(1)} %collective-permute-done.2, bf16[60,768]{1,0:T(8,128)(2,1)S(1)} %collective-permute-done.1, bf16[60,768]{1,0:T(8,128)(2,1)S(1)} %get-tuple-element.17, bf16[60,768]{1,0:T(8,128)(2,1)S(1)} %get-tuple-element.16, ...), kind=kLoop, calls=%fused_computation | loop fusion | flops 506880 | bytes 556032 | tf_op jit(solution)/shard_map/convert_element_type | solution.py:532
  (1 shorter events, 0.0 us)
Async XLA Ops:
  0.6 19.4 %collective-permute-start = (bf16[2,192,768]{2,1,0:T(8,128)(2,1)}, bf16[2,192,768]{2,1,0:T(8,128)(2,1)S(1)}, u32[]{:S(2)}, u32[]{:S(2)}) collective-permute-start(bf16[2,192,768]{2,1,0:T(8,128)(2,1)} %wo_hbm.1), channel_id=1, source_target_pairs={{0,2},{1,3},{2,0},{3,1},{4,6},{5,7},{6,4},{7,5}} | collective-permute-start | bytes 1769480 | tf_op jit(solution)/shard_map/ppermute | solution.py:524
  20.1 37.0 %copy-start = (bf16[2,768]{1,0:T(2,128)(2,1)S(1)}, bf16[2,768]{1,0:T(2,128)(2,1)}, u32[]{:S(2)}) copy-start(bf16[2,768]{1,0:T(2,128)(2,1)} %b2_hbm.1) | copy-start | bytes 9220
  55.2 10.3 %collective-permute-start.3 = (bf16[60,768]{1,0:T(8,128)(2,1)S(1)}, bf16[60,768]{1,0:T(8,128)(2,1)S(1)}, u32[]{:S(2)}, u32[]{:S(2)}) collective-permute-start(bf16[60,768]{1,0:T(8,128)(2,1)S(1)} %get-tuple-element.17), channel_id=1, source_target_pairs={{0,3},{1,2},{2,1},{3,0},{4,7},{5,6},{6,5},{7,4}} | collective-permute-start | bytes 276488 | tf_op jit(solution)/shard_map/ppermute | solution.py:524
  55.8 9.8 %collective-permute-start.2 = (bf16[60,768]{1,0:T(8,128)(2,1)S(1)}, bf16[60,768]{1,0:T(8,128)(2,1)S(1)}, u32[]{:S(2)}, u32[]{:S(2)}) collective-permute-start(bf16[60,768]{1,0:T(8,128)(2,1)S(1)} %get-tuple-element.17), channel_id=1, source_target_pairs={{0,2},{1,3},{2,0},{3,1},{4,6},{5,7},{6,4},{7,5}} | collective-permute-start | bytes 276488 | tf_op jit(solution)/shard_map/ppermute | solution.py:524
  57.0 8.5 %collective-permute-start.1 = (bf16[60,768]{1,0:T(8,128)(2,1)S(1)}, bf16[60,768]{1,0:T(8,128)(2,1)S(1)}, u32[]{:S(2)}, u32[]{:S(2)}) collective-permute-start(bf16[60,768]{1,0:T(8,128)(2,1)S(1)} %get-tuple-element.17), channel_id=1, source_target_pairs={{0,1},{1,0},{2,3},{3,2},{4,5},{5,4},{6,7},{7,6}} | collective-permute-start | bytes 276488 | tf_op jit(solution)/shard_map/ppermute | solution.py:524

commit v10 on v9

--- a/solution.py
+++ b/solution.py
@@ -191,8 +191,8 @@
 
 def rest_kernel(beams, parts, o_hbm, h_hbm, pos_hbm, g_hbm, b_hbm, wq_hbm, bq_hbm, wk_hbm, wv_hbm, bv_hbm, wo_hbm, bo_hbm, wc_hbm, bc_hbm, wco_hbm, bco_hbm, w1_hbm, b1_hbm, w2_hbm, b2_hbm,
                 wo_far, sk_hbm, sv_hbm, ck_hbm, cv_hbm, part_ref, out_ref, sk, sv, kt, vt, spot,
-                o, h, pos_ref, g, b, wq, bq, wk, wv, bv, wo, bo, wc, bc, wco, bco, w1, b1, w2, b2, ck, cv, hid, qr, kr, vr, kall, vall, os, got, snd, rcv,
-                psem, wsem, msem, mrsem, skem, svem, ckem, cvem, ssem, rsem):
+                o, h, pos_ref, g, b, wq, bq, wk, wv, bv, wo, bo, wc, bc, wco, bco, w1, b1, w2, b2, ck, cv, hid, qr, kr, vr, kall, vall, os, got, snd, rcv, wcx,
+                psem, wsem, msem, mrsem, xsem, xrsem, skem, svem, ckem, cvem, ssem, rsem):
     rows = h.shape[0]
     audios = rows // beams
     group = audios // parts
@@ -263,6 +263,23 @@
         here = dot(got[step, m, 3], wo[layer, 0]) + dot(got[step, m, 2], wo[layer, 1])
         return here + (dot(got[step, m, 0], wo_far[layer]) + dot(got[step, m, 1], wo[layer, 2]))
 
+    band = width // 2
+
+    def over_link(i):
+        r = pl.ds(i * band, band)
+        return pltpu.make_async_remote_copy(wco_hbm.at[1, r], wcx.at[0, r], xsem.at[i], xrsem.at[i], device_id=(dp, peers[0]), device_id_type=MESH)
+
+    def to_mate(i):
+        if i == 2:
+            return pltpu.make_async_remote_copy(wco_hbm.at[1], wcx.at[1], xsem.at[4], xrsem.at[4], device_id=(dp, mate), device_id_type=MESH)
+        r = pl.ds(i * band, band)
+        return pltpu.make_async_remote_copy(wcx.at[0, r], wcx.at[2, r], xsem.at[2 + i], xrsem.at[2 + i], device_id=(dp, mate), device_id_type=MESH)
+
+    def project_cross(m):
+        wait(heads_sends(4, m))
+        here = dot(got[4, m, 3], wco[1]) + dot(got[4, m, 2], wcx[1])
+        return here + (dot(got[4, m, 0], wcx[0]) + dot(got[4, m, 1], wcx[2]))
+
     def settle(m, update, bias):
         new = (hid[m].astype(F32) + update + bias.astype(F32)).astype(BF)
         hid[m] = new
@@ -309,7 +326,7 @@
         for n in range(group):
             mix(n, probs[n])
 
-        return dot(os[m].astype(BF), wco[layer])
+        return os[m].astype(BF)
 
     def mlp_half(layer, m, wide):
         normed = layer_norm(wide, g[2, layer:layer + 1, :], b[2, layer:layer + 1, :])
@@ -396,13 +413,19 @@
     wait(shared(0))
     wait(first[:2])
     for m in range(parts):
-        push(1, m, cross_half(0, m, settle(m, project(0, m, 0), bo[0:1, :])))
+        push(1, m, dot(cross_half(0, m, settle(m, project(0, m, 0), bo[0:1, :])), wco[0]))
     wait(first[2:])
     for m in range(parts):
         push(2, m, mlp_half(0, m, settle(m, total(1, m), bco[0:1, :])))
     wait(extra)
     for m in range(parts):
-        push_heads(3, m, self_half(m, settle(m, total(2, m), b2[0:1, :])))
+        wide = settle(m, total(2, m), b2[0:1, :])
+        if m == 0:
+            over_link(0).start()
+            to_mate(2).start()
+        push_heads(3, m, self_half(m, wide))
+        if m == 0:
+            over_link(1).start()
     kt[...] = kall[...].T
     vt[...] = vall[...].T
     for a in range(audios):
@@ -410,12 +433,17 @@
     wait(second)
     wait(shared(1))
     for m in range(parts):
-        push(4, m, cross_half(1, m, settle(m, project(3, m, 1), bo[1:2, :])))
+        wide = settle(m, project(3, m, 1), bo[1:2, :])
+        if m < 2:
+            over_link(m).wait()
+            to_mate(m).start()
+        push_heads(4, m, cross_half(1, m, wide))
+    wait([to_mate(i) for i in range(3)])
     final = jnp.zeros((rows, h.shape[1]), F32)
     resid = jnp.zeros((rows, h.shape[1]), F32)
     for m in range(parts):
         place = flags((rows, prow), lambda r, c: r == c + m * prow)
-        wide = settle(m, total(4, m), bco[1:2, :])
+        wide = settle(m, project_cross(m), bco[1:2, :])
         final = final + dot(place, mlp_half(1, m, wide).astype(BF))
         resid = resid + dot(place, hid[m])
     part_ref[...] = final.astype(BF)
@@ -445,8 +473,8 @@
             pltpu.VMEM((parts, prow, dim), BF),
             pltpu.VMEM((parts, prow + 8, width), F32), pltpu.VMEM((parts, prow, width), F32), pltpu.VMEM((parts, prow, width), F32),
             pltpu.VMEM((128, width), F32), pltpu.VMEM((128, width), F32), pltpu.VMEM((parts, prow, width), F32),
-            pltpu.VMEM((5, parts, 4, prow, width), BF), pltpu.VMEM((5, parts, prow, dim), BF), pltpu.VMEM((5, parts, 3, prow, dim), BF),
-            DMA((12,)), DMA((4, 8)), DMA((2, 2)), DMA((2, 2)), DMA((audios,)), DMA((audios,)), DMA((audios,)), DMA((audios,)), DMA((5, parts, 3)), DMA((5, parts, 3)),
+            pltpu.VMEM((5, parts, 4, prow, width), BF), pltpu.VMEM((5, parts, prow, dim), BF), pltpu.VMEM((5, parts, 3, prow, dim), BF), pltpu.VMEM((3, width, dim), BF),
+            DMA((12,)), DMA((4, 8)), DMA((2, 2)), DMA((2, 2)), DMA((5,)), DMA((5,)), DMA((audios,)), DMA((audios,)), DMA((audios,)), DMA((audios,)), DMA((5, parts, 3)), DMA((5, parts, 3)),
         ],
         compiler_params=pltpu.CompilerParams(collective_id=0, has_side_effects=True, vmem_limit_bytes=REST_LIMIT),
         name="rest",

time: 66.4 us -> 65.7 us (0.989)
  Pallas kernels: 59.6 us -> 58.9 us
    pallas_call x1, Pallas kernels: 35.1 us -> 34.5 us  [rest_call(): pl.pallas_call(functools.partial(rest_kernel, beams, parts), out_shape=(p...]
where the time goes in v10:
time: 65.7 us; the launch traced here: 65.6 us
  Pallas kernels  58.9 us (90%)
  starting transfers between devices  5.24 us (8%)
  other arithmetic  0.73 us (1%)
  between operations  0.7 us (1%)
    pallas_call x1, Pallas kernels, rest_call(): pl.pallas_call(functools.partial(rest_kernel, beams, parts), out_shape=(p...  34.5 us
    pallas_call x1, Pallas kernels, self_call(): pl.pallas_call(functools.partial(self_kernel, layer, beams, parts), out_s...  16.1 us
    pallas_call x1, Pallas kernels, write_call(): pl.pallas_call(functools.partial(write_kernel, layer, beams), out_shape=(...  8.4 us
    ppermute x4, starting transfers between devices, hop(): return lax.ppermute(x, 'tp', [(i, i ^ flip) for i in range(4)])  5.24 us
  transfers between devices with their start and end apart: 4, of which 0 were waited for; matrix products, arithmetic and copies ran while one was open for 0% of the time, Pallas kernels for 37%

profile of v10, /device:TPU:0, one launch (start us, length us, event | category | flops | bytes accessed | tf_op | source)
XLA Modules:
  0.0 65.6 jit_solution(7371412928674306240)
XLA Ops:
  0.6 3.4 %collective-permute-start = (bf16[2,192,768]{2,1,0:T(8,128)(2,1)}, bf16[2,192,768]{2,1,0:T(8,128)(2,1)S(1)}, u32[]{:S(2)}, u32[]{:S(2)}) collective-permute-start(bf16[2,192,768]{2,1,0:T(8,128)(2,1)} %wo_hbm.1), channel_id=1, source_target_pairs={{0,2},{1,3},{2,0},{3,1},{4,6},{5,7},{6,4},{7,5}} | collective-permute-start | bytes 1769480 | tf_op jit(solution)/shard_map/ppermute | solution.py:552
  4.0 16.1 %self_0.1 = (bf16[2,30,192]{2,1,0:T(8,128)(2,1)}, bf16[2,60,192,448]{3,2,1,0:T(8,128)(2,1)}, bf16[2,60,192,448]{3,2,1,0:T(8,128)(2,1)}) custom-call(bf16[60,768]{1,0:T(8,128)(2,1)} %h_hbm.3, s32[60]{0:T(128)} %pos_hbm.3, bf16[3,2,768]{2,1,0:T(2,128)(2,1)} %bitcast.39, bf16[3,2,768]{2,1,0:T(2,128)(2,1)} %bitcast.41, bf16[2,192,768]{2,1,0:T(8,128)(2,1)} %bitcast.32, ...), custom_call_target="tpu_custom_call" | custom-call | bytes 41287680 | tf_op jit(solution)/shard_map/self_0/pallas_call | solution.py:173
  20.1 0.0 collective-permute-done.wo_far
  20.1 0.0 copy-start
  20.1 34.5 %rest.1 = (bf16[60,768]{1,0:T(8,128)(2,1)S(1)}, bf16[60,768]{1,0:T(8,128)(2,1)S(1)}, bf16[60,192,448]{2,1,0:T(8,128)(2,1)S(1)}, bf16[60,192,448]{2,1,0:T(8,128)(...) custom-call(bf16[2,30,192]{2,1,0:T(8,128)(2,1)} %get-tuple-element.15.o_hbm, ...), custom_call_target="tpu_custom_call" | custom-call | tf_op jit(solution)/shard_map/rest/pallas_call | solution.py:466
  54.5 1.4 %collective-permute-start.3 = (bf16[60,768]{1,0:T(8,128)(2,1)S(1)}, bf16[60,768]{1,0:T(8,128)(2,1)S(1)}, u32[]{:S(2)}, u32[]{:S(2)}) collective-permute-start(bf16[60,768]{1,0:T(8,128)(2,1)S(1)} %get-tuple-element.17), channel_id=1, source_target_pairs={{0,3},{1,2},{2,1},{3,0},{4,7},{5,6},{6,5},{7,4}} | collective-permute-start | bytes 276488 | tf_op jit(solution)/shard_map/ppermute | solution.py:552
  55.9 0.4 collective-permute-start.2
  56.3 0.1 collective-permute-start.1
  56.4 0.0 copy-done
  56.5 8.4 %write.1 = (bf16[2,60,192,448]{3,2,1,0:T(8,128)(2,1)}, bf16[2,60,192,448]{3,2,1,0:T(8,128)(2,1)}, bf16[60,192,448]{2,1,0:T(8,128)(2,1)S(1)}, bf16[60,192,448]{2,1,0:T(8,128)(2,1)S(1)}) custom-call(s32[12,8,128]{2,1,0:T(8,128)S(1)} %get-tuple-element.18.spot, ...), custom_call_target="tpu_custom_call", output_to_operand_aliasing={{2}: (3, {}), {3}: (4, {}), {0}: (5, {}), {1}: (6, {})} | custom-call | bytes 20643840 | tf_op jit(solution)/shard_map/write/pallas_call | solution.py:517
  64.9 0.0 collective-permute-done.3
  64.9 0.0 collective-permute-done.2
  64.9 0.0 collective-permute-done.1
  64.9 0.7 %add_convert_fusion = bf16[60,768]{1,0:T(8,128)(2,1)} fusion(bf16[60,768]{1,0:T(8,128)(2,1)S(1)} %collective-permute-done.3, bf16[60,768]{1,0:T(8,128)(2,1)S(1)} %collective-permute-done.2, bf16[60,768]{1,0:T(8,128)(2,1)S(1)} %collective-permute-done.1, bf16[60,768]{1,0:T(8,128)(2,1)S(1)} %get-tuple-element.17, bf16[60,768]{1,0:T(8,128)(2,1)S(1)} %get-tuple-element.16, ...), kind=kLoop, calls=%fused_computation | loop fusion | flops 506880 | bytes 556032 | tf_op jit(solution)/shard_map/convert_element_type | solution.py:560
  (1 shorter events, 0.0 us)
Async XLA Ops:
  0.6 19.4 %collective-permute-start = (bf16[2,192,768]{2,1,0:T(8,128)(2,1)}, bf16[2,192,768]{2,1,0:T(8,128)(2,1)S(1)}, u32[]{:S(2)}, u32[]{:S(2)}) collective-permute-start(bf16[2,192,768]{2,1,0:T(8,128)(2,1)} %wo_hbm.1), channel_id=1, source_target_pairs={{0,2},{1,3},{2,0},{3,1},{4,6},{5,7},{6,4},{7,5}} | collective-permute-start | bytes 1769480 | tf_op jit(solution)/shard_map/ppermute | solution.py:552
  20.1 36.4 %copy-start = (bf16[2,768]{1,0:T(2,128)(2,1)S(1)}, bf16[2,768]{1,0:T(2,128)(2,1)}, u32[]{:S(2)}) copy-start(bf16[2,768]{1,0:T(2,128)(2,1)} %b2_hbm.1) | copy-start | bytes 9220
  54.5 10.3 %collective-permute-start.3 = (bf16[60,768]{1,0:T(8,128)(2,1)S(1)}, bf16[60,768]{1,0:T(8,128)(2,1)S(1)}, u32[]{:S(2)}, u32[]{:S(2)}) collective-permute-start(bf16[60,768]{1,0:T(8,128)(2,1)S(1)} %get-tuple-element.17), channel_id=1, source_target_pairs={{0,3},{1,2},{2,1},{3,0},{4,7},{5,6},{6,5},{7,4}} | collective-permute-start | bytes 276488 | tf_op jit(solution)/shard_map/ppermute | solution.py:552
  55.9 8.9 %collective-permute-start.2 = (bf16[60,768]{1,0:T(8,128)(2,1)S(1)}, bf16[60,768]{1,0:T(8,128)(2,1)S(1)}, u32[]{:S(2)}, u32[]{:S(2)}) collective-permute-start(bf16[60,768]{1,0:T(8,128)(2,1)S(1)} %get-tuple-element.17), channel_id=1, source_target_pairs={{0,2},{1,3},{2,0},{3,1},{4,6},{5,7},{6,4},{7,5}} | collective-permute-start | bytes 276488 | tf_op jit(solution)/shard_map/ppermute | solution.py:552
  56.3 8.6 %collective-permute-start.1 = (bf16[60,768]{1,0:T(8,128)(2,1)S(1)}, bf16[60,768]{1,0:T(8,128)(2,1)S(1)}, u32[]{:S(2)}, u32[]{:S(2)}) collective-permute-start(bf16[60,768]{1,0:T(8,128)(2,1)S(1)} %get-tuple-element.17), channel_id=1, source_target_pairs={{0,1},{1,0},{2,3},{3,2},{4,5},{5,4},{6,7},{7,6}} | collective-permute-start | bytes 276488 | tf_op jit(solution)/shard_map/ppermute | solution.py:552

commit v11 on v10

--- a/solution.py
+++ b/solution.py
@@ -122,15 +122,15 @@
     @pl.loop(0, pairs)
     def _(pair):
         group = (pair * 2, pair * 2 + 1)
+        @pl.when(pair >= hold)
+        def _():
+            release(pair - hold)
+
         for a in group:
             k_in(a).wait()
             v_in(a).wait()
         for a in group:
             insert_slot(((kbuf, kt), (vbuf, vt)), a * beams, beams, pos_ref[a * beams], slots)
-
-        @pl.when(pair >= hold)
-        def _():
-            release(pair - hold)
 
         probs = []
         for a in group:

time: 65.7 us -> 65.3 us (level)
  no operation moved by 1% of the time
where the time goes in v11:
time: 65.3 us; the launch traced here: 65.1 us
  Pallas kernels  58.4 us (89%)
  starting transfers between devices  5.24 us (8%)
  other arithmetic  0.73 us (1%)
  between operations  0.7 us (1%)
    pallas_call x1, Pallas kernels, rest_call(): pl.pallas_call(functools.partial(rest_kernel, beams, parts), out_shape=(p...  34.4 us
    pallas_call x1, Pallas kernels, self_call(): pl.pallas_call(functools.partial(self_kernel, layer, beams, parts), out_s...  15.6 us
    pallas_call x1, Pallas kernels, write_call(): pl.pallas_call(functools.partial(write_kernel, layer, beams), out_shape=(...  8.4 us
    ppermute x4, starting transfers between devices, hop(): return lax.ppermute(x, 'tp', [(i, i ^ flip) for i in range(4)])  5.24 us
  transfers between devices with their start and end apart: 4, of which 0 were waited for; matrix products, arithmetic and copies ran while one was open for 0% of the time, Pallas kernels for 37%

profile of v11, /device:TPU:0, one launch (start us, length us, event | category | flops | bytes accessed | tf_op | source)
XLA Modules:
  0.0 65.1 jit_solution(3368167536791527268)
XLA Ops:
  0.6 3.4 %collective-permute-start = (bf16[2,192,768]{2,1,0:T(8,128)(2,1)}, bf16[2,192,768]{2,1,0:T(8,128)(2,1)S(1)}, u32[]{:S(2)}, u32[]{:S(2)}) collective-permute-start(bf16[2,192,768]{2,1,0:T(8,128)(2,1)} %wo_hbm.1), channel_id=1, source_target_pairs={{0,2},{1,3},{2,0},{3,1},{4,6},{5,7},{6,4},{7,5}} | collective-permute-start | bytes 1769480 | tf_op jit(solution)/shard_map/ppermute | solution.py:552
  4.0 15.6 %self_0.1 = (bf16[2,30,192]{2,1,0:T(8,128)(2,1)}, bf16[2,60,192,448]{3,2,1,0:T(8,128)(2,1)}, bf16[2,60,192,448]{3,2,1,0:T(8,128)(2,1)}) custom-call(bf16[60,768]{1,0:T(8,128)(2,1)} %h_hbm.3, s32[60]{0:T(128)} %pos_hbm.3, bf16[3,2,768]{2,1,0:T(2,128)(2,1)} %bitcast.39, bf16[3,2,768]{2,1,0:T(2,128)(2,1)} %bitcast.41, bf16[2,192,768]{2,1,0:T(8,128)(2,1)} %bitcast.32, ...), custom_call_target="tpu_custom_call" | custom-call | bytes 41287680 | tf_op jit(solution)/shard_map/self_0/pallas_call | solution.py:173
  19.6 0.0 collective-permute-done.wo_far
  19.6 0.0 copy-start
  19.6 34.4 %rest.1 = (bf16[60,768]{1,0:T(8,128)(2,1)S(1)}, bf16[60,768]{1,0:T(8,128)(2,1)S(1)}, bf16[60,192,448]{2,1,0:T(8,128)(2,1)S(1)}, bf16[60,192,448]{2,1,0:T(8,128)(...) custom-call(bf16[2,30,192]{2,1,0:T(8,128)(2,1)} %get-tuple-element.15.o_hbm, ...), custom_call_target="tpu_custom_call" | custom-call | tf_op jit(solution)/shard_map/rest/pallas_call | solution.py:466
  54.1 1.4 %collective-permute-start.3 = (bf16[60,768]{1,0:T(8,128)(2,1)S(1)}, bf16[60,768]{1,0:T(8,128)(2,1)S(1)}, u32[]{:S(2)}, u32[]{:S(2)}) collective-permute-start(bf16[60,768]{1,0:T(8,128)(2,1)S(1)} %get-tuple-element.17), channel_id=1, source_target_pairs={{0,3},{1,2},{2,1},{3,0},{4,7},{5,6},{6,5},{7,4}} | collective-permute-start | bytes 276488 | tf_op jit(solution)/shard_map/ppermute | solution.py:552
  55.5 0.4 collective-permute-start.2
  55.8 0.1 collective-permute-start.1
  56.0 0.0 copy-done
  56.0 8.4 %write.1 = (bf16[2,60,192,448]{3,2,1,0:T(8,128)(2,1)}, bf16[2,60,192,448]{3,2,1,0:T(8,128)(2,1)}, bf16[60,192,448]{2,1,0:T(8,128)(2,1)S(1)}, bf16[60,192,448]{2,1,0:T(8,128)(2,1)S(1)}) custom-call(s32[12,8,128]{2,1,0:T(8,128)S(1)} %get-tuple-element.18.spot, ...), custom_call_target="tpu_custom_call", output_to_operand_aliasing={{2}: (3, {}), {3}: (4, {}), {0}: (5, {}), {1}: (6, {})} | custom-call | bytes 20643840 | tf_op jit(solution)/shard_map/write/pallas_call | solution.py:517
  64.4 0.0 collective-permute-done.3
  64.4 0.0 collective-permute-done.2
  64.4 0.0 collective-permute-done.1
  64.4 0.7 %add_convert_fusion = bf16[60,768]{1,0:T(8,128)(2,1)} fusion(bf16[60,768]{1,0:T(8,128)(2,1)S(1)} %collective-permute-done.3, bf16[60,768]{1,0:T(8,128)(2,1)S(1)} %collective-permute-done.2, bf16[60,768]{1,0:T(8,128)(2,1)S(1)} %collective-permute-done.1, bf16[60,768]{1,0:T(8,128)(2,1)S(1)} %get-tuple-element.17, bf16[60,768]{1,0:T(8,128)(2,1)S(1)} %get-tuple-element.16, ...), kind=kLoop, calls=%fused_computation | loop fusion | flops 506880 | bytes 556032 | tf_op jit(solution)/shard_map/convert_element_type | solution.py:560
  (1 shorter events, 0.0 us)
Async XLA Ops:
  0.6 19.0 %collective-permute-start = (bf16[2,192,768]{2,1,0:T(8,128)(2,1)}, bf16[2,192,768]{2,1,0:T(8,128)(2,1)S(1)}, u32[]{:S(2)}, u32[]{:S(2)}) collective-permute-start(bf16[2,192,768]{2,1,0:T(8,128)(2,1)} %wo_hbm.1), channel_id=1, source_target_pairs={{0,2},{1,3},{2,0},{3,1},{4,6},{5,7},{6,4},{7,5}} | collective-permute-start | bytes 1769480 | tf_op jit(solution)/shard_map/ppermute | solution.py:552
  19.6 36.4 %copy-start = (bf16[2,768]{1,0:T(2,128)(2,1)S(1)}, bf16[2,768]{1,0:T(2,128)(2,1)}, u32[]{:S(2)}) copy-start(bf16[2,768]{1,0:T(2,128)(2,1)} %b2_hbm.1) | copy-start | bytes 9220
  54.1 10.3 %collective-permute-start.3 = (bf16[60,768]{1,0:T(8,128)(2,1)S(1)}, bf16[60,768]{1,0:T(8,128)(2,1)S(1)}, u32[]{:S(2)}, u32[]{:S(2)}) collective-permute-start(bf16[60,768]{1,0:T(8,128)(2,1)S(1)} %get-tuple-element.17), channel_id=1, source_target_pairs={{0,3},{1,2},{2,1},{3,0},{4,7},{5,6},{6,5},{7,4}} | collective-permute-start | bytes 276488 | tf_op jit(solution)/shard_map/ppermute | solution.py:552
  55.5 8.9 %collective-permute-start.2 = (bf16[60,768]{1,0:T(8,128)(2,1)S(1)}, bf16[60,768]{1,0:T(8,128)(2,1)S(1)}, u32[]{:S(2)}, u32[]{:S(2)}) collective-permute-start(bf16[60,768]{1,0:T(8,128)(2,1)S(1)} %get-tuple-element.17), channel_id=1, source_target_pairs={{0,2},{1,3},{2,0},{3,1},{4,6},{5,7},{6,4},{7,5}} | collective-permute-start | bytes 276488 | tf_op jit(solution)/shard_map/ppermute | solution.py:552
  55.8 8.6 %collective-permute-start.1 = (bf16[60,768]{1,0:T(8,128)(2,1)S(1)}, bf16[60,768]{1,0:T(8,128)(2,1)S(1)}, u32[]{:S(2)}, u32[]{:S(2)}) collective-permute-start(bf16[60,768]{1,0:T(8,128)(2,1)S(1)} %get-tuple-element.17), channel_id=1, source_target_pairs={{0,1},{1,0},{2,3},{3,2},{4,5},{5,4},{6,7},{7,6}} | collective-permute-start | bytes 276488 | tf_op jit(solution)/shard_map/ppermute | solution.py:552

commit v12 on v11

--- a/solution.py
+++ b/solution.py
@@ -426,10 +426,6 @@
         push_heads(3, m, self_half(m, wide))
         if m == 0:
             over_link(1).start()
-    kt[...] = kall[...].T
-    vt[...] = vall[...].T
-    for a in range(audios):
-        spot[a] = jnp.full(spot.shape[1:], pos_ref[a * beams], jnp.int32)
     wait(second)
     wait(shared(1))
     for m in range(parts):
@@ -446,6 +442,11 @@
         wide = settle(m, project_cross(m), bco[1:2, :])
         final = final + dot(place, mlp_half(1, m, wide).astype(BF))
         resid = resid + dot(place, hid[m])
+        if m == 0:
+            kt[...] = kall[...].T
+            vt[...] = vall[...].T
+            for a in range(audios):
+                spot[a] = jnp.full(spot.shape[1:], pos_ref[a * beams], jnp.int32)
     part_ref[...] = final.astype(BF)
     out_ref[...] = resid.astype(BF)
 

time: 65.3 us -> 65.2 us (level)
  no operation moved by 1% of the time
where the time goes in v12:
time: 65.2 us; the launch traced here: 65.1 us
  Pallas kernels  58.5 us (90%)
  starting transfers between devices  5.24 us (8%)
  other arithmetic  0.73 us (1%)
  between operations  0.7 us (1%)
    pallas_call x1, Pallas kernels, rest_call(): pl.pallas_call(functools.partial(rest_kernel, beams, parts), out_shape=(p...  34.4 us
    pallas_call x1, Pallas kernels, self_call(): pl.pallas_call(functools.partial(self_kernel, layer, beams, parts), out_s...  15.6 us
    pallas_call x1, Pallas kernels, write_call(): pl.pallas_call(functools.partial(write_kernel, layer, beams), out_shape=(...  8.4 us
    ppermute x4, starting transfers between devices, hop(): return lax.ppermute(x, 'tp', [(i, i ^ flip) for i in range(4)])  5.24 us
  transfers between devices with their start and end apart: 4, of which 0 were waited for; matrix products, arithmetic and copies ran while one was open for 0% of the time, Pallas kernels for 37%

profile of v12, /device:TPU:0, one launch (start us, length us, event | category | flops | bytes accessed | tf_op | source)
XLA Modules:
  0.0 65.1 jit_solution(9186193711567133231)
XLA Ops:
  0.6 3.4 %collective-permute-start = (bf16[2,192,768]{2,1,0:T(8,128)(2,1)}, bf16[2,192,768]{2,1,0:T(8,128)(2,1)S(1)}, u32[]{:S(2)}, u32[]{:S(2)}) collective-permute-start(bf16[2,192,768]{2,1,0:T(8,128)(2,1)} %wo_hbm.1), channel_id=1, source_target_pairs={{0,2},{1,3},{2,0},{3,1},{4,6},{5,7},{6,4},{7,5}} | collective-permute-start | bytes 1769480 | tf_op jit(solution)/shard_map/ppermute | solution.py:553
  4.0 15.6 %self_0.1 = (bf16[2,30,192]{2,1,0:T(8,128)(2,1)}, bf16[2,60,192,448]{3,2,1,0:T(8,128)(2,1)}, bf16[2,60,192,448]{3,2,1,0:T(8,128)(2,1)}) custom-call(bf16[60,768]{1,0:T(8,128)(2,1)} %h_hbm.3, s32[60]{0:T(128)} %pos_hbm.3, bf16[3,2,768]{2,1,0:T(2,128)(2,1)} %bitcast.39, bf16[3,2,768]{2,1,0:T(2,128)(2,1)} %bitcast.41, bf16[2,192,768]{2,1,0:T(8,128)(2,1)} %bitcast.32, ...), custom_call_target="tpu_custom_call" | custom-call | bytes 41287680 | tf_op jit(solution)/shard_map/self_0/pallas_call | solution.py:173
  19.6 0.0 collective-permute-done.wo_far
  19.6 0.0 copy-start
  19.6 34.4 %rest.1 = (bf16[60,768]{1,0:T(8,128)(2,1)S(1)}, bf16[60,768]{1,0:T(8,128)(2,1)S(1)}, bf16[60,192,448]{2,1,0:T(8,128)(2,1)S(1)}, bf16[60,192,448]{2,1,0:T(8,128)(...) custom-call(bf16[2,30,192]{2,1,0:T(8,128)(2,1)} %get-tuple-element.15.o_hbm, ...), custom_call_target="tpu_custom_call" | custom-call | tf_op jit(solution)/shard_map/rest/pallas_call | solution.py:467
  54.1 1.4 %collective-permute-start.3 = (bf16[60,768]{1,0:T(8,128)(2,1)S(1)}, bf16[60,768]{1,0:T(8,128)(2,1)S(1)}, u32[]{:S(2)}, u32[]{:S(2)}) collective-permute-start(bf16[60,768]{1,0:T(8,128)(2,1)S(1)} %get-tuple-element.17), channel_id=1, source_target_pairs={{0,3},{1,2},{2,1},{3,0},{4,7},{5,6},{6,5},{7,4}} | collective-permute-start | bytes 276488 | tf_op jit(solution)/shard_map/ppermute | solution.py:553
  55.5 0.4 collective-permute-start.2
  55.8 0.1 collective-permute-start.1
  56.0 0.0 copy-done
  56.0 8.4 %write.1 = (bf16[2,60,192,448]{3,2,1,0:T(8,128)(2,1)}, bf16[2,60,192,448]{3,2,1,0:T(8,128)(2,1)}, bf16[60,192,448]{2,1,0:T(8,128)(2,1)S(1)}, bf16[60,192,448]{2,1,0:T(8,128)(2,1)S(1)}) custom-call(s32[12,8,128]{2,1,0:T(8,128)S(1)} %get-tuple-element.18.spot, ...), custom_call_target="tpu_custom_call", output_to_operand_aliasing={{2}: (3, {}), {3}: (4, {}), {0}: (5, {}), {1}: (6, {})} | custom-call | bytes 20643840 | tf_op jit(solution)/shard_map/write/pallas_call | solution.py:518
  64.4 0.0 collective-permute-done.3
  64.4 0.0 collective-permute-done.2
  64.4 0.0 collective-permute-done.1
  64.4 0.7 %add_convert_fusion = bf16[60,768]{1,0:T(8,128)(2,1)} fusion(bf16[60,768]{1,0:T(8,128)(2,1)S(1)} %collective-permute-done.3, bf16[60,768]{1,0:T(8,128)(2,1)S(1)} %collective-permute-done.2, bf16[60,768]{1,0:T(8,128)(2,1)S(1)} %collective-permute-done.1, bf16[60,768]{1,0:T(8,128)(2,1)S(1)} %get-tuple-element.17, bf16[60,768]{1,0:T(8,128)(2,1)S(1)} %get-tuple-element.16, ...), kind=kLoop, calls=%fused_computation | loop fusion | flops 506880 | bytes 556032 | tf_op jit(solution)/shard_map/convert_element_type | solution.py:561
  (1 shorter events, 0.0 us)
Async XLA Ops:
  0.6 19.0 %collective-permute-start = (bf16[2,192,768]{2,1,0:T(8,128)(2,1)}, bf16[2,192,768]{2,1,0:T(8,128)(2,1)S(1)}, u32[]{:S(2)}, u32[]{:S(2)}) collective-permute-start(bf16[2,192,768]{2,1,0:T(8,128)(2,1)} %wo_hbm.1), channel_id=1, source_target_pairs={{0,2},{1,3},{2,0},{3,1},{4,6},{5,7},{6,4},{7,5}} | collective-permute-start | bytes 1769480 | tf_op jit(solution)/shard_map/ppermute | solution.py:553
  19.6 36.4 %copy-start = (bf16[2,768]{1,0:T(2,128)(2,1)S(1)}, bf16[2,768]{1,0:T(2,128)(2,1)}, u32[]{:S(2)}) copy-start(bf16[2,768]{1,0:T(2,128)(2,1)} %b2_hbm.1) | copy-start | bytes 9220
  54.1 10.3 %collective-permute-start.3 = (bf16[60,768]{1,0:T(8,128)(2,1)S(1)}, bf16[60,768]{1,0:T(8,128)(2,1)S(1)}, u32[]{:S(2)}, u32[]{:S(2)}) collective-permute-start(bf16[60,768]{1,0:T(8,128)(2,1)S(1)} %get-tuple-element.17), channel_id=1, source_target_pairs={{0,3},{1,2},{2,1},{3,0},{4,7},{5,6},{6,5},{7,4}} | collective-permute-start | bytes 276488 | tf_op jit(solution)/shard_map/ppermute | solution.py:553
  55.5 8.9 %collective-permute-start.2 = (bf16[60,768]{1,0:T(8,128)(2,1)S(1)}, bf16[60,768]{1,0:T(8,128)(2,1)S(1)}, u32[]{:S(2)}, u32[]{:S(2)}) collective-permute-start(bf16[60,768]{1,0:T(8,128)(2,1)S(1)} %get-tuple-element.17), channel_id=1, source_target_pairs={{0,2},{1,3},{2,0},{3,1},{4,6},{5,7},{6,4},{7,5}} | collective-permute-start | bytes 276488 | tf_op jit(solution)/shard_map/ppermute | solution.py:553
  55.8 8.6 %collective-permute-start.1 = (bf16[60,768]{1,0:T(8,128)(2,1)S(1)}, bf16[60,768]{1,0:T(8,128)(2,1)S(1)}, u32[]{:S(2)}, u32[]{:S(2)}) collective-permute-start(bf16[60,768]{1,0:T(8,128)(2,1)S(1)} %get-tuple-element.17), channel_id=1, source_target_pairs={{0,1},{1,0},{2,3},{3,2},{4,5},{5,4},{6,7},{7,6}} | collective-permute-start | bytes 276488 | tf_op jit(solution)/shard_map/ppermute | solution.py:553
